TPU v7x, 32 devices: a whole 2x2x4 slice. The times are simulated.
32 devices in a mesh: dp: 4 (over y, x), ctx: 8 (over z, core).
Axes of the slice: x: 2, y: 2, z: 4, core: 2. Of those that a mesh axis runs over, the one named last changes fastest.
Arguments:
- inputs: bfloat16 [4, 16, 128, 2048], P('dp', 'ctx'), may hold values from -6 to 6
- block_of: int32 [4, 16], P('dp', 'ctx'), may hold values from 0 to 15, as said below
- first_gain: float32 [2048], P('dp'), may hold values from 0.5 to 1.5
- first_shift: float32 [2048], P('dp'), may hold values from -3 to 3
- w_qkv: bfloat16 [2048, 6144], P('dp'), may hold values from -8 to 8
- qkv_bias: float32 [6144], P('dp'), may hold values from -3 to 3
- w_out: bfloat16 [2048, 2048], P('dp'), may hold values from -0.75 to 0.75
- second_gain: float32 [2048], P('dp'), may hold values from 0.5 to 1.5
- second_shift: float32 [2048], P('dp'), may hold values from -3 to 3
- w_gateup: bfloat16 [2048, 11264], P('dp'), may hold values from -0.125 to 0.125
- w_down: bfloat16 [5632, 2048], P('dp'), may hold values from -0.078125 to 0.078125
- cotangent: bfloat16 [4, 16, 128, 2048], P('dp', 'ctx'), may hold values from -6 to 6
Outputs:
- outputs: bfloat16 [4, 16, 128, 2048], P('dp', 'ctx')
- grad_inputs: float32 [4, 16, 128, 2048], P('dp', 'ctx')
- grad_first_gain: float32 [2048], P('dp')
- grad_first_shift: float32 [2048], P('dp')
- grad_w_qkv: float32 [2048, 6144], P('dp')
- grad_qkv_bias: float32 [6144], P('dp')
- grad_w_out: float32 [2048, 2048], P('dp')
- grad_second_gain: float32 [2048], P('dp')
- grad_second_shift: float32 [2048], P('dp')
- grad_w_gateup: float32 [2048, 11264], P('dp')
- grad_w_down: float32 [5632, 2048], P('dp')
Inputs may be any that keep to these rules, and one draw needn't show every extreme that they name: `block_of`: for each sequence the 16 entries are a permutation of the blocks, and the two slots of one index of ctx hold blocks b and 15 - b, in either order.
All inputs are finite; a program needn't handle non-finite values.
Results may differ from a plain program's by a relative error of at most 0.035.
Values may be sent and summed in bfloat16 or wider, within the bound.
A program may use at most 640 MiB of HBM per device.

v0:
```python
import jax
import jax.numpy as jnp
from jax import lax
from jax.sharding import PartitionSpec as P

HEADS = 32
HEAD_DIM = 64
ROT = 16


epsilon = 1e-05


def layer_norm(token_rows, gain_vec, shift_vec):
    centre = jnp.mean(token_rows, axis=-1, keepdims=True)
    centred = token_rows - centre
    spread = jnp.mean(centred * centred, axis=-1, keepdims=True)
    inverse = lax.rsqrt(spread + epsilon)
    normed = centred * inverse
    return (normed * gain_vec + shift_vec, normed, inverse)


def norm_back(grad_rows, normed, inverse, gain_vec):
    scaled = grad_rows * gain_vec
    mean_plain = jnp.mean(scaled, axis=-1, keepdims=True)
    mean_cross = jnp.mean(scaled * normed, axis=-1, keepdims=True)
    return inverse * (scaled - mean_plain - normed * mean_cross)


def rotary_tables(positions):
    half_rot = ROT // 2
    frequency = 10000.0 ** (-2.0 * jnp.arange(half_rot, dtype=jnp.float32) / ROT)
    angles = positions.astype(jnp.float32)[:, None] * frequency[None, :]
    return (jnp.cos(angles), jnp.sin(angles))


def rotate_heads(head_rows, cosine, sine_part, direction_sign):
    half_rot = ROT // 2
    first_half = head_rows[..., :half_rot]
    second_half = head_rows[..., half_rot:ROT]
    cos_rows = cosine[:, None, :]
    sin_rows = sine_part[:, None, :] * direction_sign
    return jnp.concatenate(
        [
            first_half * cos_rows - second_half * sin_rows,
            second_half * cos_rows + first_half * sin_rows,
            head_rows[..., ROT:],
        ],
        axis=-1,
    )


def attend(query, keys_all, values_all, query_pos, key_pos):
    tok_count, head_count, head_width = query.shape
    per_group = min(4, head_count)
    score_scale = head_width ** (-0.5)
    allowed = key_pos[None, :] <= query_pos[:, None]

    def group_step(group_index, carry):
        output_all, lse_all = carry
        first_head = jnp.asarray(group_index).astype(jnp.int32) * per_group
        query_part = lax.dynamic_slice_in_dim(query, first_head, per_group, 1)
        keys_part = lax.dynamic_slice_in_dim(keys_all, first_head, per_group, 1)
        values_part = lax.dynamic_slice_in_dim(values_all, first_head, per_group, 1)
        scores = (
            jnp.einsum("thd,shd->hts", query_part, keys_part, preferred_element_type=jnp.float32)
            * score_scale
        )
        scores = jnp.where(allowed[None], scores, -jnp.inf)
        row_max = jnp.max(scores, axis=-1, keepdims=True)
        log_total = row_max + jnp.log(jnp.sum(jnp.exp(scores - row_max), axis=-1, keepdims=True))
        weights = jnp.exp(scores - log_total).astype(jnp.bfloat16)
        mixed = jnp.einsum(
            "hts,shd->thd", weights, values_part, preferred_element_type=jnp.float32
        ).astype(jnp.bfloat16)
        output_all = lax.dynamic_update_slice_in_dim(output_all, mixed, first_head, 1)
        lse_all = lax.dynamic_update_slice_in_dim(lse_all, log_total[..., 0], first_head, 0)
        return (output_all, lse_all)

    init = (jnp.zeros(query.shape, jnp.bfloat16), jnp.zeros((head_count, tok_count), jnp.float32))
    return lax.fori_loop(0, head_count // per_group, group_step, init)


def attend_back(query, keys_all, values_all, output, grad_output, lse_all, query_pos, key_pos):
    tok_count, head_count, head_width = query.shape
    per_group = min(4, head_count)
    score_scale = head_width ** (-0.5)
    allowed = key_pos[None, :] <= query_pos[:, None]
    delta_all = jnp.einsum(
        "thd,thd->ht", output.astype(jnp.float32), grad_output.astype(jnp.float32)
    )

    def group_step(group_index, carry):
        grad_q_all, grad_k_all, grad_v_all = carry
        first_head = jnp.asarray(group_index).astype(jnp.int32) * per_group
        query_part = lax.dynamic_slice_in_dim(query, first_head, per_group, 1)
        keys_part = lax.dynamic_slice_in_dim(keys_all, first_head, per_group, 1)
        values_part = lax.dynamic_slice_in_dim(values_all, first_head, per_group, 1)
        dout_part = lax.dynamic_slice_in_dim(grad_output, first_head, per_group, 1)
        lse_part = lax.dynamic_slice_in_dim(lse_all, first_head, per_group, 0)
        delta_part = lax.dynamic_slice_in_dim(delta_all, first_head, per_group, 0)
        scores = (
            jnp.einsum("thd,shd->hts", query_part, keys_part, preferred_element_type=jnp.float32)
            * score_scale
        )
        scores = jnp.where(allowed[None], scores, -jnp.inf)
        probs = jnp.exp(scores - lse_part[..., None])
        probs_low = probs.astype(jnp.bfloat16)
        grad_v_part = jnp.einsum(
            "hts,thd->shd", probs_low, dout_part, preferred_element_type=jnp.float32
        )
        grad_p = jnp.einsum(
            "thd,shd->hts", dout_part, values_part, preferred_element_type=jnp.float32
        )
        grad_s = (probs * (grad_p - delta_part[..., None])).astype(jnp.bfloat16)
        grad_q_part = (
            jnp.einsum("hts,shd->thd", grad_s, keys_part, preferred_element_type=jnp.float32)
            * score_scale
        )
        grad_k_part = (
            jnp.einsum("hts,thd->shd", grad_s, query_part, preferred_element_type=jnp.float32)
            * score_scale
        )
        grad_q_all = lax.dynamic_update_slice_in_dim(grad_q_all, grad_q_part, first_head, 1)
        grad_k_all = lax.dynamic_update_slice_in_dim(grad_k_all, grad_k_part, first_head, 1)
        grad_v_all = lax.dynamic_update_slice_in_dim(grad_v_all, grad_v_part, first_head, 1)
        return (grad_q_all, grad_k_all, grad_v_all)

    init = (
        jnp.zeros(query.shape, jnp.float32),
        jnp.zeros(keys_all.shape, jnp.float32),
        jnp.zeros(values_all.shape, jnp.float32),
    )
    return lax.fori_loop(0, head_count // per_group, group_step, init)


def local(
    inputs,
    block_of,
    first_gain,
    first_shift,
    w_qkv,
    qkv_bias,
    w_out,
    second_gain,
    second_shift,
    w_gateup,
    w_down,
    cotangent,
):
    block_rows = inputs.shape[2]
    tok_count = inputs.shape[1] * block_rows
    model_width = inputs.shape[3]
    token_rows = inputs.reshape(tok_count, model_width).astype(jnp.float32)
    offsets = jnp.arange(block_rows, dtype=jnp.int32)
    local_pos = (block_of.reshape(-1)[:, None] * block_rows + offsets[None, :]).reshape(tok_count)
    cosine, sine_part = rotary_tables(local_pos)
    head_shape = (tok_count, HEADS, HEAD_DIM)
    full_qkv, full_out, gain_one, shift_one, bias_full = (
        lax.all_gather(w_qkv, "dp", axis=0, tiled=True),
        lax.all_gather(w_out, "dp", axis=0, tiled=True),
        lax.all_gather(first_gain.astype(jnp.bfloat16), "dp", axis=0, tiled=True).astype(
            first_gain.dtype
        ),
        lax.all_gather(first_shift.astype(jnp.bfloat16), "dp", axis=0, tiled=True).astype(
            first_shift.dtype
        ),
        lax.all_gather(qkv_bias.astype(jnp.bfloat16), "dp", axis=0, tiled=True).astype(
            qkv_bias.dtype
        ),
    )
    normed_out, normed_one, inverse_one = layer_norm(token_rows, gain_one, shift_one)
    hidden_one = normed_out.astype(jnp.bfloat16)
    projected = jnp.dot(hidden_one, full_qkv, preferred_element_type=jnp.float32) + bias_full
    query = rotate_heads(
        projected[:, :model_width].reshape(head_shape), cosine, sine_part, 1.0
    ).astype(jnp.bfloat16)
    keys_flat = (
        rotate_heads(
            projected[:, model_width : 2 * model_width].reshape(head_shape), cosine, sine_part, 1.0
        )
        .reshape(tok_count, model_width)
        .astype(jnp.bfloat16)
    )
    values_flat = projected[:, 2 * model_width :].astype(jnp.bfloat16)
    keys_gathered, values_gathered, blocks_gathered = (
        lax.all_gather(keys_flat, "ctx", axis=0, tiled=True),
        lax.all_gather(values_flat, "ctx", axis=0, tiled=True),
        lax.all_gather(block_of, "ctx", axis=1, tiled=True),
    )
    seq_rows = keys_gathered.shape[0]
    key_pos = (blocks_gathered.reshape(-1)[:, None] * block_rows + offsets[None, :]).reshape(
        seq_rows
    )
    key_shape = (seq_rows, HEADS, HEAD_DIM)
    attended, log_totals = attend(
        query,
        keys_gathered.reshape(key_shape),
        values_gathered.reshape(key_shape),
        local_pos,
        key_pos,
    )
    attended_flat = attended.reshape(tok_count, model_width)
    middle = token_rows + jnp.dot(attended_flat, full_out, preferred_element_type=jnp.float32)
    full_gateup, full_down, gain_two, shift_two = (
        lax.all_gather(w_gateup, "dp", axis=0, tiled=True),
        lax.all_gather(w_down, "dp", axis=0, tiled=True),
        lax.all_gather(second_gain.astype(jnp.bfloat16), "dp", axis=0, tiled=True).astype(
            second_gain.dtype
        ),
        lax.all_gather(second_shift.astype(jnp.bfloat16), "dp", axis=0, tiled=True).astype(
            second_shift.dtype
        ),
    )
    normed_out_two, normed_two, inverse_two = layer_norm(middle, gain_two, shift_two)
    hidden_two = normed_out_two.astype(jnp.bfloat16)
    gate_up = jnp.dot(hidden_two, full_gateup, preferred_element_type=jnp.float32)
    hidden_units = full_down.shape[0]
    gate_part = gate_up[:, :hidden_units]
    up_part = gate_up[:, hidden_units:]
    sigmoid_gate = jax.nn.sigmoid(gate_part)
    activation = (gate_part * sigmoid_gate * up_part).astype(jnp.bfloat16)
    result = middle + jnp.dot(activation, full_down, preferred_element_type=jnp.float32)
    outputs = result.astype(jnp.bfloat16).reshape(inputs.shape)
    grad_rows = cotangent.reshape(tok_count, model_width)
    grad_act = jnp.einsum("td,fd->tf", grad_rows, full_down, preferred_element_type=jnp.float32)
    grad_gate = grad_act * up_part * sigmoid_gate * (1.0 + gate_part * (1.0 - sigmoid_gate))
    grad_up = grad_act * gate_part * sigmoid_gate
    grad_gu = jnp.concatenate([grad_gate, grad_up], axis=1).astype(jnp.bfloat16)
    grad_hidden_two = jnp.einsum(
        "tf,df->td", grad_gu, full_gateup, preferred_element_type=jnp.float32
    )
    gain_two_term = jnp.sum(grad_hidden_two * normed_two, axis=0)
    shift_two_term = jnp.sum(grad_hidden_two, axis=0)
    grad_middle = grad_rows.astype(jnp.float32) + norm_back(
        grad_hidden_two, normed_two, inverse_two, gain_two
    )
    grad_gateup = jnp.einsum("td,tf->df", hidden_two, grad_gu, preferred_element_type=jnp.float32)
    grad_down = jnp.einsum("tf,td->fd", activation, grad_rows, preferred_element_type=jnp.float32)
    mlp_shards = (
        lax.psum_scatter(
            grad_gateup.astype(jnp.bfloat16), "dp", scatter_dimension=0, tiled=True
        ).astype(jnp.float32),
        lax.psum_scatter(
            grad_down.astype(jnp.bfloat16), "dp", scatter_dimension=0, tiled=True
        ).astype(jnp.float32),
        lax.psum_scatter(
            gain_two_term.astype(jnp.bfloat16), "dp", scatter_dimension=0, tiled=True
        ).astype(jnp.float32),
        lax.psum_scatter(
            shift_two_term.astype(jnp.bfloat16), "dp", scatter_dimension=0, tiled=True
        ).astype(jnp.float32),
    )
    mlp_grads = (
        lax.psum(mlp_shards[0].astype(jnp.bfloat16), "ctx").astype(jnp.float32),
        lax.psum(mlp_shards[1].astype(jnp.bfloat16), "ctx").astype(jnp.float32),
        lax.psum(mlp_shards[2].astype(jnp.bfloat16), "ctx").astype(jnp.float32),
        lax.psum(mlp_shards[3].astype(jnp.bfloat16), "ctx").astype(jnp.float32),
    )
    full_qkv_again, full_out_again, gain_again = (
        lax.all_gather(w_qkv, "dp", axis=0, tiled=True),
        lax.all_gather(w_out, "dp", axis=0, tiled=True),
        lax.all_gather(first_gain.astype(jnp.bfloat16), "dp", axis=0, tiled=True).astype(
            first_gain.dtype
        ),
    )
    grad_middle_low = grad_middle.astype(jnp.bfloat16)
    grad_attended = jnp.einsum(
        "te,de->td", grad_middle_low, full_out_again, preferred_element_type=jnp.float32
    ).astype(jnp.bfloat16)
    grad_query, grad_keys_all, grad_values_all = attend_back(
        query,
        keys_gathered.reshape(key_shape),
        values_gathered.reshape(key_shape),
        attended,
        grad_attended.reshape(head_shape),
        log_totals,
        local_pos,
        key_pos,
    )
    grad_keys, grad_values = (
        lax.psum_scatter(
            grad_keys_all.reshape(seq_rows, model_width).astype(jnp.bfloat16),
            "ctx",
            scatter_dimension=0,
            tiled=True,
        ).astype(jnp.float32),
        lax.psum_scatter(
            grad_values_all.reshape(seq_rows, model_width).astype(jnp.bfloat16),
            "ctx",
            scatter_dimension=0,
            tiled=True,
        ).astype(jnp.float32),
    )
    grad_query_plain = rotate_heads(grad_query, cosine, sine_part, -1.0).reshape(
        tok_count, model_width
    )
    grad_keys_plain = rotate_heads(grad_keys.reshape(head_shape), cosine, sine_part, -1.0).reshape(
        tok_count, model_width
    )
    grad_proj = jnp.concatenate([grad_query_plain, grad_keys_plain, grad_values], axis=1)
    grad_proj_low = grad_proj.astype(jnp.bfloat16)
    grad_hidden_one = jnp.einsum(
        "tf,df->td", grad_proj_low, full_qkv_again, preferred_element_type=jnp.float32
    )
    bias_term = jnp.sum(grad_proj, axis=0)
    gain_one_term = jnp.sum(grad_hidden_one * normed_one, axis=0)
    shift_one_term = jnp.sum(grad_hidden_one, axis=0)
    grad_inputs = grad_middle + norm_back(grad_hidden_one, normed_one, inverse_one, gain_again)
    grad_wout = jnp.einsum(
        "td,te->de", attended_flat, grad_middle_low, preferred_element_type=jnp.float32
    )
    grad_wqkv = jnp.einsum(
        "td,tf->df", hidden_one, grad_proj_low, preferred_element_type=jnp.float32
    )
    attn_shards = (
        lax.psum_scatter(
            grad_wqkv.astype(jnp.bfloat16), "dp", scatter_dimension=0, tiled=True
        ).astype(jnp.float32),
        lax.psum_scatter(
            bias_term.astype(jnp.bfloat16), "dp", scatter_dimension=0, tiled=True
        ).astype(jnp.float32),
        lax.psum_scatter(
            grad_wout.astype(jnp.bfloat16), "dp", scatter_dimension=0, tiled=True
        ).astype(jnp.float32),
        lax.psum_scatter(
            gain_one_term.astype(jnp.bfloat16), "dp", scatter_dimension=0, tiled=True
        ).astype(jnp.float32),
        lax.psum_scatter(
            shift_one_term.astype(jnp.bfloat16), "dp", scatter_dimension=0, tiled=True
        ).astype(jnp.float32),
    )
    attn_grads = (
        lax.psum(attn_shards[0].astype(jnp.bfloat16), "ctx").astype(jnp.float32),
        lax.psum(attn_shards[1].astype(jnp.bfloat16), "ctx").astype(jnp.float32),
        lax.psum(attn_shards[2].astype(jnp.bfloat16), "ctx").astype(jnp.float32),
        lax.psum(attn_shards[3].astype(jnp.bfloat16), "ctx").astype(jnp.float32),
        lax.psum(attn_shards[4].astype(jnp.bfloat16), "ctx").astype(jnp.float32),
    )
    results = (
        attn_grads[3],
        attn_grads[4],
        attn_grads[0],
        attn_grads[1],
        attn_grads[2],
        mlp_grads[2],
        mlp_grads[3],
        mlp_grads[0],
        mlp_grads[1],
    )
    return (outputs, grad_inputs.reshape(inputs.shape)) + results


def solution(mesh):
    placed = (
        P("dp", "ctx", None, None),
        P("dp", "ctx"),
        P("dp"),
        P("dp"),
        P("dp", None),
        P("dp"),
        P("dp", None),
        P("dp"),
        P("dp"),
        P("dp", None),
        P("dp", None),
        P("dp", "ctx", None, None),
    )
    return jax.shard_map(
        local,
        mesh=mesh,
        in_specs=placed,
        out_specs=(
            P("dp", "ctx", None, None),
            P("dp", "ctx", None, None),
            P("dp"),
            P("dp"),
            P("dp", None),
            P("dp"),
            P("dp", None),
            P("dp"),
            P("dp"),
            P("dp", None),
            P("dp", None),
        ),
        check_vma=False,
    )
```

profile of v0, /device:TPU:0, one launch (start us, length us, event | category | flops | bytes accessed | tf_op | source)
XLA Modules:
  0.0 2973.1 jit_solution(4743477724046858579)
XLA Ops:
  8.0 9.6 all-gather.1
  17.7 8.1 all-gather
  25.8 7.6 all-gather.2
  34.6 205.7 %all-gather.12.cloned.1.call-done = bf16[2048,6144]{1,0:T(8,128)(2,1)} async-done(((bf16[512,6144]{1,0:T(8,128)(2,1)}), bf16[2048,6144]{1,0:T(8,128)(2,1)}) %all-gather.12.cloned.1.call-update) | async-done | bytes 25165840 | tf_op jit(solution)/shard_map/all_gather | solution.py:160
  240.3 11.6 convolution_add_fusion
  271.3 8.2 all-gather.4
  279.5 7.0 all-gather.3
  287.9 9.8 all-reduce
  299.5 38.6 %all-gather.14.cloned.1.call-done = bf16[2048,2048]{1,0:T(8,128)(2,1)} async-done(((bf16[256,2048]{1,0:T(8,128)(2,1)}), bf16[2048,2048]{1,0:T(8,128)(2,1)}) %all-gather.14.cloned.1.call-update) | async-done | bytes 8388624 | tf_op jit(solution)/shard_map/all_gather | solution.py:188
  338.1 12.3 copy.38
  350.4 70.9 %all-gather.16.cloned.1.call-done = bf16[2048,2048]{0,1:T(8,128)(2,1)} async-done(((bf16[256,2048]{0,1:T(8,128)(2,1)}), bf16[2048,2048]{0,1:T(8,128)(2,1)}) %all-gather.16.cloned.1.call-update) | async-done | bytes 8388624 | tf_op jit(solution)/shard_map/all_gather | solution.py:187
  421.5 72.2 %while.34 = (s32[]{:T(128)}, bf16[256,32,64]{0,2,1:T(8,128)(2,1)S(1)}, f32[32,256]{1,0:T(8,128)S(1)}, bf16[2048,32,64]{0,2,1:T(8,128)(2,1)}, bf16[256,32,64]{0,2...) while((s32[]{:T(128)}, ...), condition=%wide.region_5.6_spmd.clone, body=%wide.region_2.5_spmd.clone.sunk | while | flops 560528384 | bytes 29666480 | solution.py:81
  493.7 15.1 all-gather.18.cloned.1.call-done
  508.7 6.2 fusion.64
  515.3 397.2 %all-gather.20.cloned.1.call-done = bf16[2048,11264]{1,0:T(8,128)(2,1)} async-done(((bf16[512,11264]{1,0:T(8,128)(2,1)}), bf16[2048,11264]{1,0:T(8,128)(2,1)}) %all-gather.20.cloned.1.call-update) | async-done | bytes 46137360 | tf_op jit(solution)/shard_map/all_gather | solution.py:206
  912.5 28.4 fusion.62
  940.9 183.7 %all-gather.22.cloned.1.call-done = bf16[5632,2048]{1,0:T(8,128)(2,1)} async-done(((bf16[1408,2048]{1,0:T(8,128)(2,1)}), bf16[5632,2048]{1,0:T(8,128)(2,1)}) %all-gather.22.cloned.1.call-update) | async-done | bytes 23068688 | tf_op jit(solution)/shard_map/all_gather | solution.py:207
  1124.5 26.0 multiply_convert_fusion.2
  1150.6 22.1 multiply_reduce_fusion
  1176.4 6.8 convolution_convert_fusion.4
  1188.7 4.5 broadcast.231
  1197.5 142.9 %while.35 = (s32[]{:T(128)}, f32[256,32,64]{0,2,1:T(8,128)}, bf16[2048,32,64]{0,2,1:T(8,128)(2,1)}, bf16[2048,32,64]{0,2,1:T(8,128)(2,1)}, bf16[2048,32,64]{0,2,...) while((s32[]{:T(128)}, f32[256,32,64]{0,2,1:T(8,128)}, ...), condition=%wide.region_11.12_spmd.clone, body=%wide.region_10.11_spmd.clone.sunk | while | flops 1364262912 | bytes 47491280 | solution.py:134
  1200.7 4.5 multiply_convert_fusion.5
  1218.6 4.5 multiply_convert_fusion.5
  1236.4 4.5 multiply_convert_fusion.5
  1254.2 4.5 multiply_convert_fusion.5
  1272.1 4.5 multiply_convert_fusion.5
  1289.9 4.5 multiply_convert_fusion.5
  1307.7 4.5 multiply_convert_fusion.5
  1325.5 4.5 multiply_convert_fusion.5
  1341.2 7.5 convolution_convert_fusion.3
  1349.9 13.4 convolution_convert_fusion.1
  1366.2 63.9 %reduce-scatter.7.cloned.1.call-done = bf16[256,2048]{0,1:T(8,128)(2,1)} async-done(((bf16[2048,2048]{0,1:T(8,128)(2,1)}), bf16[256,2048]{0,1:T(8,128)(2,1)}) %reduce-scatter.7.cloned.1.call-update) | async-done | bytes 1048592 | tf_op jit(solution)/shard_map/reduce_scatter | solution.py:282
  1434.3 86.1 %reduce-scatter.9.cloned.1.call-done = bf16[256,2048]{0,1:T(8,128)(2,1)} async-done(((bf16[2048,2048]{0,1:T(8,128)(2,1)}), bf16[256,2048]{0,1:T(8,128)(2,1)}) %reduce-scatter.9.cloned.1.call-update) | async-done | bytes 1048592 | tf_op jit(solution)/shard_map/reduce_scatter | solution.py:288
  1527.2 13.6 convolution_convert_fusion.2
  1541.5 21.6 convolution_convert_fusion
  1563.2 45.7 %reduce-scatter.13.cloned.1.call-done = bf16[512,2048]{1,0:T(8,128)(2,1)} async-done(((bf16[2048,2048]{1,0:T(8,128)(2,1)}), bf16[512,2048]{1,0:T(8,128)(2,1)}) %reduce-scatter.13.cloned.1.call-update) | async-done | bytes 2097168 | tf_op jit(solution)/shard_map/reduce_scatter | solution.py:323
  1608.9 208.3 %reduce-scatter.17.cloned.1.call-done = bf16[1408,2048]{1,0:T(8,128)(2,1)} async-done(((bf16[5632,2048]{1,0:T(8,128)(2,1)}), bf16[1408,2048]{1,0:T(8,128)(2,1)}) %reduce-scatter.17.cloned.1.call-update) | async-done | bytes 5767184 | tf_op jit(solution)/shard_map/reduce_scatter | solution.py:244
  1817.2 224.9 %reduce-scatter.11.cloned.1.call-done = bf16[512,6144]{1,0:T(8,128)(2,1)} async-done(((bf16[2048,6144]{1,0:T(8,128)(2,1)}), bf16[512,6144]{1,0:T(8,128)(2,1)}) %reduce-scatter.11.cloned.1.call-update) | async-done | bytes 6291472 | tf_op jit(solution)/shard_map/reduce_scatter | solution.py:317
  2042.0 393.1 %reduce-scatter.15.cloned.1.call-done = bf16[512,11264]{1,0:T(8,128)(2,1)} async-done(((bf16[2048,11264]{1,0:T(8,128)(2,1)}), bf16[512,11264]{1,0:T(8,128)(2,1)}) %reduce-scatter.15.cloned.1.call-update) | async-done | bytes 11534352 | tf_op jit(solution)/shard_map/reduce_scatter | solution.py:241
  2437.7 14.1 fusion.50
  2453.8 14.3 multiply_reduce_fusion.1
  2468.1 15.4 all-reduce.8
  2484.0 15.0 all-reduce.6
  2506.3 432.8 %all-reduce.11.cloned.1.call-done = (bf16[512,6144]{1,0:T(8,128)(2,1)}, bf16[512,2048]{1,0:T(8,128)(2,1)}, bf16[512,11264]{1,0:T(8,128)(2,1)}, bf16[1408,2048]{1,0:T(8,128)(2,1)}) async-done(((bf16[512,6144]{1,0:T(8,128)(2,1)}, bf16[512,2048]{1,0:T(8,128)(2,1)}, bf16[512,11264]{1,0:T(8,128)(2,1)}, bf16[1408,2048]{1,0:T(8,128)(2,1)}), (bf16[512,6144]{1,0:T(8,128)(2,1)}, bf16[512,2048]{1,0:T(8,128)(2,1)}, ...) | async-done | bytes 25690128 | tf_op jit(solution)/shard_map/psum | solution.py:334
  2939.1 10.1 convert_element_type.234
  2951.9 8.3 convert_element_type.244
  2960.1 6.0 convert_element_type.246
  (275 shorter events, 246.0 us)
Async XLA Ops:
  7.2 10.4 copy-start.36
  7.2 18.5 copy-start.32
  7.2 26.2 copy-start
  7.2 233.1 %all-gather.12.cloned.1.call-start = ((), (), s32[]{:S(2)}) async-start(), calls=%async_computation.6 | async-start | bytes 31457280 | tf_op jit(solution)/shard_map/all_gather | solution.py:160
  8.0 330.2 %all-gather.14.cloned.1.call-start = ((), (), s32[]{:S(2)}) async-start(), calls=%async_computation.7 | async-start | bytes 9437184 | tf_op jit(solution)/shard_map/all_gather | solution.py:188
  25.7 226.2 %copy-start.25 = (f32[4,1,512]{2,1,0:T(1,128)}, f32[4,1,512]{2,1,0:T(1,128)S(1)}, u32[]{:S(2)}) copy-start(f32[4,1,512]{2,1,0:T(1,128)S(1)} %convert_element_type.248) | copy-start | bytes 24580
  33.7 218.3 %copy-start.28 = (f32[256]{0:T(256)}, f32[256]{0:T(256)S(1)}, u32[]{:S(2)}) copy-start(f32[256]{0:T(256)S(1)} %get-tuple-element.483) | copy-start | bytes 3076
  34.1 217.8 %copy-start.30 = (f32[256]{0:T(256)}, f32[256]{0:T(256)S(1)}, u32[]{:S(2)}) copy-start(f32[256]{0:T(256)S(1)} %rsqrt_bitcast_fusion) | copy-start | bytes 3076
  34.6 217.3 %copy-start.15 = (bf16[256,2048]{1,0:T(8,128)(2,1)}, bf16[256,2048]{1,0:T(8,128)(2,1)S(1)}, u32[]{:S(2)}) copy-start(bf16[256,2048]{1,0:T(8,128)(2,1)S(1)} %add_convert_fusion.1) | copy-start | bytes 3145732
  251.9 2.7 copy-start.17
  255.8 165.5 %all-gather.16.cloned.1.call-start = ((), (), s32[]{:S(2)}) async-start(), calls=%async_computation.8 | async-start | bytes 9437184 | tf_op jit(solution)/shard_map/all_gather | solution.py:187
  256.7 10.3 copy-start.23
  269.4 239.3 %all-gather.18.cloned.1.call-start = ((), (), s32[]{:S(2)}) async-start(), calls=%async_computation.9 | async-start | bytes 10485760 | tf_op jit(solution)/shard_map/all_gather | solution.py:161
  270.0 642.5 %all-gather.20.cloned.1.call-start = ((), (), s32[]{:S(2)}) async-start(), calls=%async_computation.10 | async-start | bytes 57671680 | tf_op jit(solution)/shard_map/all_gather | solution.py:206
  270.6 8.9 copy-start.38
  270.6 16.0 copy-start.41
  270.6 853.9 %all-gather.22.cloned.1.call-start = ((), (), s32[]{:S(2)}) async-start(), calls=%async_computation.11 | async-start | bytes 28835840 | tf_op jit(solution)/shard_map/all_gather | solution.py:207
  271.2 1158.9 %reduce-scatter.7.cloned.1.call-start = ((), (), s32[]{:S(2)}) async-start(), calls=%async_computation.12 | async-start | bytes 9437184 | tf_op jit(solution)/shard_map/reduce_scatter | solution.py:282
  279.5 633.0 %copy-start.21 = (f32[4,1,512]{2,1,0:T(1,128)}, f32[4,1,512]{2,1,0:T(1,128)S(1)}, u32[]{:S(2)}) copy-start(f32[4,1,512]{2,1,0:T(1,128)S(1)} %convert_element_type.252) | copy-start | bytes 24580
  493.6 15.1 copy-start.2
  493.6 15.1 copy-start.11
  912.5 212.1 %copy-start.18 = (bf16[1,2,128,2048]{3,2,1,0:T(8,128)(2,1)S(1)}, bf16[1,2,128,2048]{3,2,1,0:T(8,128)(2,1)}, u32[]{:S(2)}) copy-start(bf16[1,2,128,2048]{3,2,1,0:T(8,128)(2,1)} %param.27) | copy-start | bytes 3145732
  1176.4 9.1 copy-start.3
  1340.4 180.0 %reduce-scatter.9.cloned.1.call-start = ((), (), s32[]{:S(2)}) async-start(), calls=%async_computation.13 | async-start | bytes 9437184 | tf_op jit(solution)/shard_map/reduce_scatter | solution.py:288
  1341.2 267.7 %reduce-scatter.13.cloned.1.call-start = ((), (), s32[]{:S(2)}) async-start(), calls=%async_computation.15 | async-start | bytes 10485760 | tf_op jit(solution)/shard_map/reduce_scatter | solution.py:323
  1348.7 468.4 %reduce-scatter.17.cloned.1.call-start = ((), (), s32[]{:S(2)}) async-start(), calls=%async_computation.17 | async-start | bytes 28835840 | tf_op jit(solution)/shard_map/reduce_scatter | solution.py:244
  1363.4 678.6 %reduce-scatter.11.cloned.1.call-start = ((), (), s32[]{:S(2)}) async-start(), calls=%async_computation.14 | async-start | bytes 31457280 | tf_op jit(solution)/shard_map/reduce_scatter | solution.py:317
  1430.1 2.6 copy-start.12
  1432.7 89.3 %copy-start.24 = (f32[256,8]{0,1:T(8,128)S(1)}, f32[256,8]{0,1:T(8,128)}, u32[]{:S(2)}) copy-start(f32[256,8]{0,1:T(8,128)} %copy-done.23) | copy-start | bytes 24580
  1432.7 89.3 %copy-start.27 = (f32[256,8]{0,1:T(8,128)S(1)}, f32[256,8]{0,1:T(8,128)}, u32[]{:S(2)}) copy-start(f32[256,8]{0,1:T(8,128)} %get-tuple-element.480) | copy-start | bytes 24580
  1520.4 3.6 copy-start.14
  1521.9 5.1 copy-start.4
  1522.0 3.6 copy-start.13
  1540.8 894.4 %reduce-scatter.15.cloned.1.call-start = ((), (), s32[]{:S(2)}) async-start(), calls=%async_computation.16 | async-start | bytes 57671680 | tf_op jit(solution)/shard_map/reduce_scatter | solution.py:241
  1563.1 1375.9 %all-reduce.11.cloned.1.call-start = ((), (), s32[]{:S(2)}) async-start(), calls=%async_computation.18 | async-start | bytes 51380224 | tf_op jit(solution)/shard_map/psum | solution.py:334
  2437.7 14.1 copy-start.5
  2437.7 14.1 copy-start.7
  2437.7 14.1 copy-start.8
  2451.8 1.9 copy-start.6
  2451.9 1.9 copy-start.26
  2451.9 1.9 copy-start.29
  2451.9 1.9 copy-start.31
  2453.8 14.4 copy-start.33
  2453.8 14.4 copy-start.34
  2939.1 10.1 copy-start.20
  2939.1 12.8 copy-start.10
  2949.2 10.9 slice-start
  2951.9 8.3 slice-start.1
  (9 other events, 10.1 us)
Sparse Core Ops, SparseCore 0:
  9.9 230.3 all-gather.11
  255.9 82.1 all-gather.13
  340.3 80.9 all-gather.15
  423.0 85.6 all-gather.17
  510.4 401.9 all-gather.19
  914.2 210.3 all-gather.21
  1340.5 89.5 reduce-scatter.6
  1432.4 88.0 reduce-scatter.8
  1524.1 84.7 reduce-scatter.12
  1612.4 204.7 reduce-scatter.16
  1820.3 221.6 reduce-scatter.10
  2045.0 390.0 reduce-scatter.14
  2438.0 500.9 all-reduce.10
where the time goes:
time: 2980 us; the launch traced here: 2970 us
  waiting for transfers between devices  2370 us (80%)
  matrix products  376 us (13%)
  blocking collectives  80.8 us (3%)
  other arithmetic  76.8 us (3%)
  local copies, waits for them, and re-layouts  51.8 us (2%)
    psum x1, waiting for transfers between devices, local(): lax.psum(attn_shards[0].astype(jnp.bfloat16), 'ctx').astype(jnp.float32)  433 us
    all_gather x1, waiting for transfers between devices, local(): lax.all_gather(w_gateup, 'dp', axis=0, tiled=True)  397 us
    reduce_scatter x1, waiting for transfers between devices, local(): lax.psum_scatter(grad_gateup.astype(jnp.bfloat16), 'dp', scatter_dimensio...  393 us
    reduce_scatter x1, waiting for transfers between devices, local(): lax.psum_scatter(grad_wqkv.astype(jnp.bfloat16), 'dp', scatter_dimension=...  225 us
    reduce_scatter x1, waiting for transfers between devices, local(): lax.psum_scatter(grad_down.astype(jnp.bfloat16), 'dp', scatter_dimension=...  208 us
    all_gather x1, waiting for transfers between devices, local(): lax.all_gather(w_qkv, 'dp', axis=0, tiled=True)  206 us
    all_gather x1, waiting for transfers between devices, local(): lax.all_gather(w_down, 'dp', axis=0, tiled=True)  184 us
    reduce_scatter x1, waiting for transfers between devices, local(): lax.psum_scatter(grad_values_all.reshape(seq_rows, model_width).astype(jn...  86.1 us
  transfers between devices with their start and end apart: 13, of which 13 were waited for; matrix products, arithmetic and copies ran while one was open for 8% of the time, Pallas kernels for 0%

commit v1 on v0

v1 whole, which is shorter than its diff:
```python
import functools

import jax
import jax.numpy as jnp
from jax import lax
from jax.experimental import pallas as pl
from jax.experimental.pallas import tpu as pltpu
from jax.sharding import Mesh
from jax.sharding import PartitionSpec as P

HEADS = 32
HEAD_DIM = 64
ROT = 16
PAIR = 2 * HEAD_DIM
SCALE = HEAD_DIM ** (-0.5)
epsilon = 1e-05
F32 = jnp.float32
BF16 = jnp.bfloat16
PLANE = ("dp", "core")
EVERY = ("dp", "pl", "core")


def layer_norm(token_rows, gain_vec, shift_vec):
    centre = jnp.mean(token_rows, axis=-1, keepdims=True)
    centred = token_rows - centre
    spread = jnp.mean(centred * centred, axis=-1, keepdims=True)
    inverse = lax.rsqrt(spread + epsilon)
    normed = centred * inverse
    return (normed * gain_vec + shift_vec, normed, inverse)


def norm_back(grad_rows, normed, inverse, gain_vec):
    scaled = grad_rows * gain_vec
    mean_plain = jnp.mean(scaled, axis=-1, keepdims=True)
    mean_cross = jnp.mean(scaled * normed, axis=-1, keepdims=True)
    return inverse * (scaled - mean_plain - normed * mean_cross)


def rotary_tables(length):
    half = ROT // 2
    lane = jnp.arange(PAIR, dtype=jnp.int32) % HEAD_DIM
    frequency = 10000.0 ** (-2.0 * (lane % half).astype(F32) / ROT)
    angles = jnp.arange(length, dtype=F32)[:, None] * frequency[None, :]
    cosine, sine = jnp.cos(angles), jnp.sin(angles)
    cos_t = jnp.where(lane < ROT, cosine, 1.0)
    low_t = jnp.where(lane < half, -sine, 0.0)
    high_t = jnp.where((lane >= half) & (lane < ROT), sine, 0.0)
    return cos_t, low_t, high_t


def head_mask(shape, head):
    lane = lax.broadcasted_iota(jnp.int32, shape, 1)
    return (lane < HEAD_DIM) if head == 0 else (lane >= HEAD_DIM)


def roll_pair(x, shift):
    return pltpu.roll(x, shift % PAIR, 1)


def nt(a, b):
    return lax.dot_general(a, b, (((1,), (1,)), ((), ())), preferred_element_type=F32)


def nn(a, b):
    return lax.dot_general(a, b, (((1,), (0,)), ((), ())), preferred_element_type=F32)


def tn(a, b):
    return lax.dot_general(a, b, (((0,), (0,)), ((), ())), preferred_element_type=F32)


def attend_kernel(
    blk, tile, slot_ref, pq, pk, pv, bq, bk, bv, cos_t, low_t, high_t, qs, ks, vs, att, lse, acc, top, osc
):
    length = pq.shape[0]

    def sort_block(b, carry):
        src = pl.ds(pl.multiple_of(slot_ref[b] * blk, blk), blk)
        dst = pl.ds(pl.multiple_of(b * blk, blk), blk)
        c, lo, hi = cos_t[dst, :], low_t[dst, :], high_t[dst, :]
        q = pq[src, :] + bq[...]
        k = pk[src, :] + bk[...]
        q = q * c + roll_pair(q, -(ROT // 2)) * lo + roll_pair(q, ROT // 2) * hi
        k = k * c + roll_pair(k, -(ROT // 2)) * lo + roll_pair(k, ROT // 2) * hi
        qs[dst, :] = q.astype(BF16)
        ks[dst, :] = k.astype(BF16)
        vs[dst, :] = (pv[src, :] + bv[...]).astype(BF16)
        return carry

    lax.fori_loop(0, length // blk, sort_block, 0)
    rows = lax.broadcasted_iota(jnp.int32, (tile, tile), 0)
    cols = lax.broadcasted_iota(jnp.int32, (tile, tile), 1)
    masks = [head_mask((tile, PAIR), h) for h in range(2)]

    def q_step(qi, carry):
        q_at = pl.ds(pl.multiple_of(qi * tile, tile), tile)
        q = qs[q_at, :]
        acc[...] = jnp.zeros_like(acc)
        top[...] = jnp.full(top.shape, -1e30, F32)

        def one(kj, diagonal):
            k_at = pl.ds(pl.multiple_of(kj * tile, tile), tile)
            k, v = ks[k_at, :], vs[k_at, :]
            for h in range(2):
                qm = jnp.where(masks[h], q, 0).astype(BF16)
                s = nt(qm, k) * SCALE
                if diagonal:
                    s = jnp.where(cols <= rows, s, -jnp.inf)
                old = top[h]
                new = jnp.maximum(old, jnp.max(s, axis=1, keepdims=True))
                p = jnp.exp(s - new[:, :1]).astype(BF16)
                ve = jnp.where(masks[h], v, 1).astype(BF16)
                acc[h] = acc[h] * jnp.exp(old - new) + nn(p, ve)
                top[h] = new

        def k_step(kj, c):
            one(kj, False)
            return c

        lax.fori_loop(0, qi, k_step, 0)
        one(qi, True)
        a0, a1 = acc[0], acc[1]
        sum0 = roll_pair(a0, HEAD_DIM)
        sum1 = roll_pair(a1, HEAD_DIM)
        total = jnp.where(masks[0], sum0, sum1)
        mixed = jnp.where(masks[0], a0, a1) / total
        osc[q_at, :] = mixed.astype(BF16)
        lse[q_at, :] = jnp.where(masks[0], top[0], top[1]) + jnp.log(total)
        return carry

    lax.fori_loop(0, length // tile, q_step, 0)

    def place_block(b, carry):
        dst = pl.ds(pl.multiple_of(slot_ref[b] * blk, blk), blk)
        att[dst, :] = osc[pl.ds(pl.multiple_of(b * blk, blk), blk), :]
        return carry

    lax.fori_loop(0, length // blk, place_block, 0)


def attend(slot_of, proj, bias, tables, blk):
    length, width = proj.shape
    pairs = width // (3 * PAIR)
    tile = min(512, length)
    whole = lambda f: pl.BlockSpec((length, PAIR), f)
    table = pl.BlockSpec((length, PAIR), lambda p, s: (0, 0), pipeline_mode=pl.Buffered(1))
    in_specs = (
        [whole(lambda p, s, o=o: (0, o * pairs + p)) for o in range(3)]
        + [pl.BlockSpec((1, PAIR), lambda p, s, o=o: (0, o * pairs + p)) for o in range(3)]
        + [table] * 3
    )
    out = jax.ShapeDtypeStruct((length, pairs * PAIR), BF16)
    own = whole(lambda p, s: (0, p))
    return pl.pallas_call(
        functools.partial(attend_kernel, blk, tile),
        out_shape=(out, out, out, out, jax.ShapeDtypeStruct((length, pairs * PAIR), F32)),
        grid_spec=pltpu.PrefetchScalarGridSpec(
            num_scalar_prefetch=1,
            grid=(pairs,),
            in_specs=in_specs,
            out_specs=[own] * 5,
            scratch_shapes=[
                pltpu.VMEM((2, tile, PAIR), F32),
                pltpu.VMEM((2, tile, PAIR), F32),
                pltpu.VMEM((length, PAIR), BF16),
            ],
        ),
        compiler_params=pltpu.CompilerParams(vmem_limit_bytes=56 * 2**20),
        name="attend",
    )(slot_of, proj, proj, proj, bias, bias, bias, *tables)


def attend_back_kernel(
    blk, tile, slot_ref, qs, ks, vs, att, gat, lse, cos_t, low_t, high_t, gq, gk, gv, bias, dos, dlt, dq, dk, dv
):
    length = qs.shape[0]
    bmask = head_mask((blk, PAIR), 0)

    def sort_block(b, carry):
        src = pl.ds(pl.multiple_of(slot_ref[b] * blk, blk), blk)
        dst = pl.ds(pl.multiple_of(b * blk, blk), blk)
        g = gat[src, :]
        dos[dst, :] = g
        prod = g.astype(F32) * att[src, :].astype(F32)
        d0 = jnp.sum(jnp.where(bmask, prod, 0.0), axis=1, keepdims=True)
        d1 = jnp.sum(jnp.where(bmask, 0.0, prod), axis=1, keepdims=True)
        dlt[dst, :] = jnp.where(bmask, d0, d1)
        return carry

    lax.fori_loop(0, length // blk, sort_block, 0)
    dq[...] = jnp.zeros_like(dq)
    rows = lax.broadcasted_iota(jnp.int32, (tile, tile), 0)
    cols = lax.broadcasted_iota(jnp.int32, (tile, tile), 1)
    masks = [head_mask((tile, PAIR), h) for h in range(2)]
    steps = length // tile

    def k_step(kj, carry):
        k_at = pl.ds(pl.multiple_of(kj * tile, tile), tile)
        k, v = ks[k_at, :], vs[k_at, :]
        dk[...] = jnp.zeros_like(dk)
        dv[...] = jnp.zeros_like(dv)

        def one(qi, diagonal):
            q_at = pl.ds(pl.multiple_of(qi * tile, tile), tile)
            q, do = qs[q_at, :], dos[q_at, :]
            ls, dl = lse[q_at, :], dlt[q_at, :]
            for h in range(2):
                at = h * HEAD_DIM
                qm = jnp.where(masks[h], q, 0).astype(BF16)
                dm = jnp.where(masks[h], do, 0).astype(BF16)
                km = jnp.where(masks[h], k, 0).astype(BF16)
                p = jnp.exp(nt(qm, k) * SCALE - ls[:, at : at + 1])
                if diagonal:
                    p = jnp.where(cols <= rows, p, 0.0)
                ds = (p * (nt(dm, v) - dl[:, at : at + 1])).astype(BF16)
                dv[...] += tn(p.astype(BF16), dm)
                dk[...] += tn(ds, qm)
                dq[q_at, :] += nn(ds, km)

        one(kj, True)

        def q_step(qi, c):
            one(qi, False)
            return c

        lax.fori_loop(kj + 1, steps, q_step, 0)
        for part in range(tile // blk):
            b = kj * (tile // blk) + part
            sub = pl.ds(part * blk, blk)
            pos = pl.ds(pl.multiple_of(b * blk, blk), blk)
            dst = pl.ds(pl.multiple_of(slot_ref[b] * blk, blk), blk)
            g = dk[sub, :] * SCALE
            g = g * cos_t[pos, :] - roll_pair(g, -(ROT // 2)) * low_t[pos, :] - roll_pair(g, ROT // 2) * high_t[pos, :]
            gk[dst, :] = g.astype(BF16)
            bias[1:2, :] += jnp.sum(g, axis=0, keepdims=True)
            w = dv[sub, :]
            gv[dst, :] = w.astype(BF16)
            bias[2:3, :] += jnp.sum(w, axis=0, keepdims=True)
        return carry

    bias[...] = jnp.zeros_like(bias)
    lax.fori_loop(0, steps, k_step, 0)

    def place_block(b, carry):
        pos = pl.ds(pl.multiple_of(b * blk, blk), blk)
        dst = pl.ds(pl.multiple_of(slot_ref[b] * blk, blk), blk)
        g = dq[pos, :] * SCALE
        g = g * cos_t[pos, :] - roll_pair(g, -(ROT // 2)) * low_t[pos, :] - roll_pair(g, ROT // 2) * high_t[pos, :]
        gq[dst, :] = g.astype(BF16)
        bias[0:1, :] += jnp.sum(g, axis=0, keepdims=True)
        return carry

    lax.fori_loop(0, length // blk, place_block, 0)


def attend_back(slot_of, qs, ks, vs, att, gat, lse, tables, blk):
    length, width = qs.shape
    pairs = width // PAIR
    tile = min(512, length)
    own = pl.BlockSpec((length, PAIR), lambda p, s: (0, p))
    table = pl.BlockSpec((length, PAIR), lambda p, s: (0, 0), pipeline_mode=pl.Buffered(1))
    out = jax.ShapeDtypeStruct((length, width), BF16)
    return pl.pallas_call(
        functools.partial(attend_back_kernel, blk, tile),
        out_shape=(out, out, out, jax.ShapeDtypeStruct((8, width), F32)),
        grid_spec=pltpu.PrefetchScalarGridSpec(
            num_scalar_prefetch=1,
            grid=(pairs,),
            in_specs=[own] * 6 + [table] * 3,
            out_specs=[own] * 3 + [pl.BlockSpec((8, PAIR), lambda p, s: (0, p))],
            scratch_shapes=[
                pltpu.VMEM((length, PAIR), BF16),
                pltpu.VMEM((length, PAIR), F32),
                pltpu.VMEM((length, PAIR), F32),
                pltpu.VMEM((tile, PAIR), F32),
                pltpu.VMEM((tile, PAIR), F32),
            ],
        ),
        compiler_params=pltpu.CompilerParams(vmem_limit_bytes=56 * 2**20),
        name="attend_back",
    )(slot_of, qs, ks, vs, att, gat, lse, *tables)


def local(
    groups,
    inputs,
    block_of,
    first_gain,
    first_shift,
    w_qkv,
    qkv_bias,
    w_out,
    second_gain,
    second_shift,
    w_gateup,
    w_down,
    cotangent,
):
    n = groups
    blk = inputs.shape[2]
    toks = inputs.shape[1] * blk
    width = inputs.shape[3]
    rows = w_qkv.shape[0]
    me, plane, core = (lax.axis_index(a) for a in EVERY)
    hw = width // (2 * n)
    units = w_down.shape[0] // 2
    swap_pairs = [(s * n + z, z * n + s) for s in range(n) for z in range(n)]
    swap = lambda a: lax.ppermute(a, ("dp", "pl"), swap_pairs)
    gather = lambda a: lax.all_gather(a, PLANE, axis=0, tiled=True)
    scatter = lambda a: lax.psum_scatter(a.astype(BF16), PLANE, scatter_dimension=0, tiled=True).astype(F32)
    pick = lambda a, axis, at: lax.dynamic_index_in_dim(a, at, axis, keepdims=False)

    def columns(w, parts, wide):
        mine = pick(w.reshape(rows, parts, n, 2, wide), 3, core)
        mine = mine.transpose(2, 0, 1, 3).reshape(n * rows, parts * wide)
        return lax.all_to_all(mine, "dp", 0, 0, tiled=True)

    token_rows = swap(inputs.reshape(toks, width)).astype(F32)
    cot = swap(cotangent.reshape(toks, width))
    wq = columns(w_qkv, 3, hw)
    small = jnp.concatenate([first_gain, first_shift, second_gain, second_shift, qkv_bias])
    small = lax.all_gather(small, "dp", axis=0, tiled=False)
    gain_one, shift_one, gain_two, shift_two = (
        small[:, k * rows : (k + 1) * rows].reshape(width) for k in range(4)
    )
    bias = small[:, 4 * rows :].reshape(3, n, 2, hw)
    bias = pick(pick(bias, 1, me), 1, core).reshape(1, 3 * hw)
    blocks = lax.all_gather(block_of.reshape(-1), EVERY, axis=0, tiled=True)
    blocks = pick(blocks.reshape(n, -1), 0, plane)
    order = jnp.arange(blocks.shape[0], dtype=jnp.int32)
    slot_of = jnp.sum(jnp.where(blocks[None, :] == order[:, None], order[None, :], 0), axis=1)
    wgu = columns(w_gateup, 2, units)
    wo = pick(w_out.reshape(2, hw, width), 0, core)
    wd = pick(w_down.reshape(2, units, width), 0, core)
    tables = rotary_tables(blocks.shape[0] * blk)

    normed_out, normed_one, inverse_one = layer_norm(token_rows, gain_one, shift_one)
    hidden_one = gather(normed_out.astype(BF16))
    proj = nn(hidden_one, wq)
    qs, ks, vs, att, lse = attend(slot_of, proj, bias, tables, blk)
    middle = token_rows + scatter(nn(att, wo))
    normed_out_two, normed_two, inverse_two = layer_norm(middle, gain_two, shift_two)
    hidden_two = gather(normed_out_two.astype(BF16))
    cot_all = gather(cot)
    gate_up = nn(hidden_two, wgu)
    gate, upper = gate_up[:, :units], gate_up[:, units:]
    sig = jax.nn.sigmoid(gate)
    act = (gate * sig * upper).astype(BF16)
    grad_act = nt(cot_all, wd)
    grad_gate = grad_act * upper * sig * (1.0 + gate * (1.0 - sig))
    grad_up = grad_act * gate * sig
    grad_gu = jnp.concatenate([grad_gate, grad_up], axis=1).astype(BF16)
    grad_hidden_two = scatter(nt(grad_gu, wgu))
    outputs = (middle + scatter(nn(act, wd))).astype(BF16)
    outputs = swap(outputs)
    gain_two_term = jnp.sum(grad_hidden_two * normed_two, axis=0)
    shift_two_term = jnp.sum(grad_hidden_two, axis=0)
    grad_middle = cot.astype(F32) + norm_back(grad_hidden_two, normed_two, inverse_two, gain_two)
    grad_middle_all = gather(grad_middle.astype(BF16))
    grad_att = nt(grad_middle_all, wo).astype(BF16)
    gq, gk, gv, bias_terms = attend_back(slot_of, qs, ks, vs, att, grad_att, lse, tables, blk)
    grad_proj = jnp.concatenate([gq, gk, gv], axis=1)
    grad_hidden_one = scatter(nt(grad_proj, wq))
    gain_one_term = jnp.sum(grad_hidden_one * normed_one, axis=0)
    shift_one_term = jnp.sum(grad_hidden_one, axis=0)
    grad_inputs = grad_middle + norm_back(grad_hidden_one, normed_one, inverse_one, gain_one)
    grad_inputs = swap(grad_inputs.astype(BF16)).astype(F32)

    def by_rows(g):
        part = lax.psum_scatter(g.astype(BF16), "pl", scatter_dimension=0, tiled=True)
        return lax.all_gather(part, ("core", "pl"), axis=0, tiled=True).astype(F32)

    def by_columns(g, parts, wide):
        sub = rows // n
        g = g.astype(BF16).reshape(n, n, sub, parts * wide).transpose(1, 0, 2, 3).reshape(n * rows, parts * wide)
        part = lax.psum_scatter(g, "pl", scatter_dimension=0, tiled=True)
        part = lax.all_to_all(part, "dp", 0, 0, tiled=True)
        whole = lax.all_gather(part, ("core", "pl"), axis=0, tiled=True)
        whole = whole.reshape(2, n, n, sub, parts, wide).transpose(1, 3, 4, 2, 0, 5)
        return whole.reshape(rows, parts * n * 2 * wide).astype(F32)

    grad_down = by_rows(tn(act, cot_all))
    grad_gateup = by_columns(tn(hidden_two, grad_gu), 2, units)
    grad_out = by_rows(tn(att, grad_middle_all))
    grad_qkv = by_columns(tn(hidden_one, grad_proj), 3, hw)
    bias_term = bias_terms[:3].reshape(3, 1, hw)
    at = me * 2 + core
    spots = (jnp.arange(2 * n, dtype=jnp.int32) == at)[None, :, None]
    bias_term = jnp.where(spots, bias_term, 0.0).reshape(n, -1)
    tiny = jnp.concatenate(
        [a.reshape(n, rows) for a in (gain_one_term, shift_one_term, gain_two_term, shift_two_term)] + [bias_term],
        axis=1,
    )
    tiny = pick(lax.psum(tiny, EVERY), 0, me)
    terms = [tiny[k * rows : (k + 1) * rows] for k in range(4)]
    return (
        outputs.reshape(inputs.shape),
        grad_inputs.reshape(inputs.shape),
        terms[0],
        terms[1],
        grad_qkv,
        tiny[4 * rows :],
        grad_out,
        terms[2],
        terms[3],
        grad_gateup,
        grad_down,
    )


def solution(mesh):
    n = mesh.shape["dp"]
    if mesh.shape["ctx"] != 2 * n:
        raise ValueError("unsupported mesh")
    grid = Mesh(mesh.devices.reshape(n, n, 2), EVERY)
    act = P("dp", ("pl", "core"), None, None)
    mat = P("dp", None)
    vec = P("dp")
    return jax.shard_map(
        functools.partial(local, n),
        mesh=grid,
        in_specs=(act, P("dp", ("pl", "core")), vec, vec, mat, vec, mat, vec, vec, mat, mat, act),
        out_specs=(act, act, vec, vec, mat, vec, mat, vec, vec, mat, mat),
        check_vma=False,
    )
```

time: 2980 us -> 1610 us (0.54)
  waiting for transfers between devices: 2370 us -> 692 us
  blocking collectives: 80.8 us -> 350 us
  matrix products: 376 us -> 146 us
  local copies, waits for them, and re-layouts: 51.8 us -> 212 us
  Pallas kernels: 0 us -> 91.9 us
  starting transfers between devices: 0.52 us -> 58.1 us
  other arithmetic: 76.8 us -> 40.4 us
    reduce_scatter x6 -> x8, waiting for transfers between devices: 1020 us -> 399 us  [the longest x4 273 us: local(): lax.psum_scatter(a.astype(BF16), PLANE, scatter_dimension=0, tiled=True)]
    all_gather x6 -> x8, waiting for transfers between devices: 911 us -> 292 us  [the longest x2 163 us: by_rows(): return lax.all_gather(part, ('core', 'pl'), axis=0, tiled=True).astype(F32)]
    psum x1 -> x0, waiting for transfers between devices: 433 us -> none  [local(): lax.psum(attn_shards[0].astype(jnp.bfloat16), 'ctx').astype(jnp.float32)]
    dot_general x68 -> x12, matrix products: 376 us -> 146 us  [the longest x4 52 us: nt(): lax.dot_general(a, b, (((1,), (1,)), ((), ())), preferred_element_type=F32)]
    all_to_all x0 -> x3, blocking collectives: none -> 201 us  [the longest x1 163 us: columns(): return lax.all_to_all(mine, 'dp', 0, 0, tiled=True)]
    unnamed x102 -> x60, local copies, waits for them, and re-layouts: 8.5 us -> 102 us
    pallas_call x0 -> x2, Pallas kernels: none -> 91.9 us  [the longest x1 50.4 us: attend_back(): pl.pallas_call(functools.partial(attend_back_kernel, blk, tile), out_shap...]
    convert_element_type x1 -> x4, local copies, waits for them, and re-layouts: 2.26 us -> 77.7 us  [by_columns(): return whole.reshape(rows, parts * n * 2 * wide).astype(F32)]
  transfers between devices with their start and end apart: 13 -> 21, of which waited for: 13 -> 10; matrix products, arithmetic and copies ran while one was open for 8% -> 18% of each run, Pallas kernels for 0% -> 3%
where the time goes in v1:
time: 1610 us; the launch traced here: 1600 us
  waiting for transfers between devices  692 us (43%)
  blocking collectives  350 us (22%)
  local copies, waits for them, and re-layouts  212 us (13%)
  matrix products  146 us (9%)
  Pallas kernels  91.9 us (6%)
  starting transfers between devices  58.1 us (4%)
  other arithmetic  40.4 us (3%)
    reduce_scatter x4, waiting for transfers between devices, local(): lax.psum_scatter(a.astype(BF16), PLANE, scatter_dimension=0, tiled=True)  273 us
    all_gather x2, waiting for transfers between devices, by_rows(): return lax.all_gather(part, ('core', 'pl'), axis=0, tiled=True).astype(F32)  163 us
    all_to_all x1, blocking collectives, columns(): return lax.all_to_all(mine, 'dp', 0, 0, tiled=True)  163 us
    reduce_scatter x2, waiting for transfers between devices, by_columns(): part = lax.psum_scatter(g, 'pl', scatter_dimension=0, tiled=True)  119 us
    all_gather x2, waiting for transfers between devices, by_columns(): whole = lax.all_gather(part, ('core', 'pl'), axis=0, tiled=True)  105 us
    unnamed x60, local copies, waits for them, and re-layouts  102 us
    unnamed x1, blocking collectives  79.8 us
    convert_element_type x4, local copies, waits for them, and re-layouts, by_columns(): return whole.reshape(rows, parts * n * 2 * wide).astype(F32)  77.7 us
  transfers between devices with their start and end apart: 21, of which 10 were waited for; matrix products, arithmetic and copies ran while one was open for 18% of the time, Pallas kernels for 3%

profile of v1, /device:TPU:0, one launch (start us, length us, event | category | flops | bytes accessed | tf_op | source)
XLA Modules:
  0.0 1604.9 jit_solution(13424203912310791909)
XLA Ops:
  12.7 30.4 %all-gather.2 = f32[4,1,3584]{2,1,0:T(1,128)S(1)} all-gather(f32[1,1,3584]{2,1,0:T(1,128)S(1)} %reshape.227), channel_id=3, replica_groups=mesh['dp'=4,'pl'=4,'core'=2] {'dp'}, dimensions={0}, use_global_device_ids=true | all-gather | bytes 71680 | tf_op jit(solution)/shard_map/all_gather | solution.py:322
  45.3 8.6 copy.60
  57.9 41.9 %all-to-all-start = ((bf16[4,512,768]{1,2,0:T(8,128)(2,1)}), bf16[4,512,768]{1,2,0:T(8,128)(2,1)}, u32[]{:S(2)}, u32[]{:S(2)}) async-start(bf16[4,512,768]{1,2,0:T(8,128)(2,1)} %bitcast.115), calls=%async_computation | async-start | bytes 6291456 | tf_op jit(solution)/shard_map/all_to_all | solution.py:316
  100.1 79.8 %all-reduce.1 = s32[4,16]{1,0:T(4,128)S(1)} all-reduce(s32[4,16]{1,0:T(4,128)S(1)} %reshape.197), channel_id=2, replica_groups=mesh['dp'=4,'pl'=4,'core'=2] {'dp','pl','core'}, use_global_device_ids=true, to_apply=%add | all-reduce | flops 64 | bytes 512
  181.1 5.0 fusion.38
  186.1 4.6 copy.63
  190.8 11.7 fusion.54.pq.pk.pv
  202.4 41.4 %attend.1 = (bf16[2048,256]{1,0:T(8,128)(2,1)}, bf16[2048,256]{1,0:T(8,128)(2,1)}, bf16[2048,256]{1,0:T(8,128)(2,1)}, bf16[2048,256]{1,0:T(8,128)(2,1)}, f32[2048,256]{1,0:T(8,128)}) custom-call(s32[16]{0:T(128)} %select_reduce_fusion.slot_ref, f32[2048,768]{1,0:T(8,128)} %fusion.54.pq.pk.pv, f32[2048,768]{1,0:T(8,128)} %fusion.54.pq.pk.pv, ...), custom_call_target="tpu_custom_call" | custom-call | tf_op jit(solution)/shard_map/attend/pallas_call | solution.py:154
  243.8 7.0 convolution_convert_fusion.3
  250.9 71.3 %reduce-scatter.9.cloned.1.call-done = bf16[256,2048]{1,0:T(8,128)(2,1)} async-done(((bf16[2048,2048]{1,0:T(8,128)(2,1)}), bf16[256,2048]{1,0:T(8,128)(2,1)}) %reduce-scatter.9.cloned.1.call-update) | async-done | bytes 1048592 | tf_op jit(solution)/shard_map/reduce_scatter | solution.py:310
  327.2 9.5 collective-permute-start.2
  337.0 15.9 copy.64
  353.0 3.0 dynamic-slice_bitcast_fusion
  356.4 162.7 %all_to_all.48 = bf16[4,512,1408]{1,2,0:T(8,128)(2,1)} all-to-all(bf16[4,512,1408]{1,2,0:T(8,128)(2,1)S(1)} %bitcast.112), channel_id=1, replica_groups=mesh['dp'=4,'pl'=4,'core'=2] {'dp'}, dimensions={0} | all-to-all | bytes 11534336 | tf_op jit(solution)/shard_map/all_to_all | solution.py:316
  519.1 8.3 copy.66
  527.4 18.8 %fusion.55 = f32[2048,1408]{0,1:T(8,128)} fusion(bf16[2048,2048]{1,0:T(8,128)(2,1)} %all-gather.14.cloned.1.call-done, bf16[2048,1408]{1,0:T(8,128)(2,1)} %bitcast.116), kind=kOutput, calls=%fused_computation.129 | convolution fusion | flops 11811160064 | bytes 25690112 | tf_op jit(solution)/shard_map/dot_general | solution.py:65
  546.2 16.2 %fusion.2 = (bf16[2048,704]{0,1:T(8,128)(2,1)}, bf16[2048,704]{0,1:T(8,128)(2,1)}, bf16[2048,704]{0,1:T(8,128)(2,1)}) fusion(f32[2048,1408]{0,1:T(8,128)} %fusion.55, bf16[2048,2048]{1,0:T(8,128)(2,1)} %all-gather.16.cloned.1.call-done, bf16[2,704,2048]{2,1,0:T(8,128)(2,1)} %bitcast.146, s32[]{:T(128)S(6)} %select_n.95), kind=kOutput, calls=%fused_computation.10 | convolution fusion | flops 5928648704 | bytes 31457284 | tf_op jit(solution)/shard_map/dot_general | solution.py:61
  562.4 17.7 %convolution_convert_fusion.1 = bf16[2048,2048]{1,0:T(8,128)(2,1)} fusion(bf16[2048,1408]{1,0:T(8,128)(2,1)S(1)} %bitcast.117, bf16[2048,704]{0,1:T(8,128)(2,1)} %get-tuple-element.82, bf16[2048,704]{0,1:T(8,128)(2,1)} %get-tuple-element.81), kind=kOutput, calls=%fused_computation.1 | convolution fusion | flops 11826888704 | bytes 19922944 | tf_op jit(solution)/shard_map/dot_general | solution.py:61
  580.2 71.5 %reduce-scatter.13.cloned.1.call-done = bf16[256,2048]{1,0:T(8,128)(2,1)} async-done(((bf16[2048,2048]{1,0:T(8,128)(2,1)}), bf16[256,2048]{1,0:T(8,128)(2,1)}) %reduce-scatter.13.cloned.1.call-update) | async-done | bytes 1048592 | tf_op jit(solution)/shard_map/reduce_scatter | solution.py:310
  654.6 3.4 fusion.52
  658.1 10.5 convolution_convert_fusion.6
  668.7 17.4 %convolution_convert_fusion.4 = bf16[2048,1408]{1,0:T(8,128)(2,1)S(1)} fusion(bf16[2048,2048]{1,0:T(8,128)(2,1)} %all-gather.14.cloned.1.call-done, bf16[2048,704]{0,1:T(8,128)(2,1)} %get-tuple-element.82, bf16[2048,704]{0,1:T(8,128)(2,1)} %get-tuple-element.81), kind=kOutput, calls=%fused_computation.4 | convolution fusion | flops 11825577984 | bytes 19922944 | tf_op jit(solution)/shard_map/dot_general | solution.py:69
  689.2 23.3 %all-gather.18.cloned.1.call-done = bf16[2048,2048]{1,0:T(8,128)(2,1)} async-done(((bf16[256,2048]{1,0:T(8,128)(2,1)}), bf16[2048,2048]{1,0:T(8,128)(2,1)}) %all-gather.18.cloned.1.call-update) | async-done | bytes 8388624 | tf_op jit(solution)/shard_map/all_gather | solution.py:309
  712.5 6.7 convolution_convert_fusion.8.gat
  719.2 50.4 %attend_back.1 = (bf16[2048,256]{1,0:T(8,128)(2,1)}, bf16[2048,256]{1,0:T(8,128)(2,1)}, bf16[2048,256]{1,0:T(8,128)(2,1)}, f32[8,256]{1,0:T(8,128)}) custom-call(s32[16]{0:T(128)} %select_reduce_fusion.slot_ref, bf16[2048,256]{1,0:T(8,128)(2,1)} %get-tuple-element.21.qs, bf16[2048,256]{1,0:T(8,128)(2,1)} %get-tuple-element.22.ks, ...), custom_call_target="tpu_custom_call" | custom-call | tf_op jit(solution)/shard_map/attend_back/pallas_call | solution.py:263
  774.3 6.8 convolution_convert_fusion.7
  782.2 10.4 convolution_convert_fusion.5
  794.6 11.4 convolution_convert_fusion
  806.0 11.4 convolution_convert_fusion.2
  818.2 57.8 %reduce-scatter.21.cloned.1.call-done = bf16[512,1408]{1,0:T(8,128)(2,1)} async-done(((bf16[2048,1408]{1,0:T(8,128)(2,1)}), bf16[512,1408]{1,0:T(8,128)(2,1)}) %reduce-scatter.21.cloned.1.call-update) | async-done | bytes 1441808 | tf_op jit(solution)/shard_map/reduce_scatter | solution.py:376
  876.1 22.1 %all_to_all.49 = bf16[4,128,1408]{2,1,0:T(8,128)(2,1)S(1)} all-to-all(bf16[4,128,1408]{2,1,0:T(8,128)(2,1)} %bitcast.124), channel_id=1, replica_groups=mesh['dp'=4,'pl'=4,'core'=2] {'dp'}, dimensions={0} | all-to-all | bytes 2883584 | tf_op jit(solution)/shard_map/all_to_all | solution.py:377
  899.8 7.0 reduce-scatter.19.cloned.1.call-done
  906.9 61.0 %reduce-scatter.17.cloned.1.call-done = bf16[512,768]{1,0:T(8,128)(2,1)} async-done(((bf16[2048,768]{1,0:T(8,128)(2,1)}), bf16[512,768]{1,0:T(8,128)(2,1)}) %reduce-scatter.17.cloned.1.call-update) | async-done | bytes 786448 | tf_op jit(solution)/shard_map/reduce_scatter | solution.py:376
  967.9 15.8 all_to_all.50
  986.2 57.2 %reduce-scatter.15.cloned.1.call-done = bf16[256,2048]{1,0:T(8,128)(2,1)} async-done(((bf16[2048,2048]{1,0:T(8,128)(2,1)}), bf16[256,2048]{1,0:T(8,128)(2,1)}) %reduce-scatter.15.cloned.1.call-update) | async-done | bytes 1048592 | tf_op jit(solution)/shard_map/reduce_scatter | solution.py:310
  1045.6 73.1 %reduce-scatter.11.cloned.1.call-done = bf16[256,2048]{1,0:T(8,128)(2,1)} async-done(((bf16[2048,2048]{1,0:T(8,128)(2,1)}), bf16[256,2048]{1,0:T(8,128)(2,1)}) %reduce-scatter.11.cloned.1.call-update) | async-done | bytes 1048592 | tf_op jit(solution)/shard_map/reduce_scatter | solution.py:310
  1118.7 4.7 fusion.25
  1127.3 163.5 %all-gather.26.cloned.1.call-done = bf16[1408,2048]{1,0:T(8,128)(2,1)} async-done(((bf16[176,2048]{1,0:T(8,128)(2,1)}), bf16[1408,2048]{1,0:T(8,128)(2,1)}) %all-gather.26.cloned.1.call-update) | async-done | bytes 5767184 | tf_op jit(solution)/shard_map/all_gather | solution.py:371
  1290.8 8.7 convert_element_type.143
  1299.6 104.9 %all-gather.24.cloned.1.call-done = bf16[4096,1408]{0,1:T(8,128)(2,1)} async-done(((bf16[512,1408]{0,1:T(8,128)(2,1)}), bf16[4096,1408]{0,1:T(8,128)(2,1)}) %all-gather.24.cloned.1.call-update) | async-done | bytes 11534352 | tf_op jit(solution)/shard_map/all_gather | solution.py:378
  1404.5 26.9 %reshape.221 = f32[2,4,4,128,2,704]{3,2,1,0,5,4:T(4,128)} reshape(bf16[4096,1408]{0,1:T(8,128)(2,1)} %all-gather.24.cloned.1.call-done) | data formatting | bytes 34603008 | tf_op jit(solution)/shard_map/convert_element_type | solution.py:380
  1431.5 37.0 %copy.77 = f32[4,128,2,4,2,704]{5,4,3,2,1,0:T(2,128)} copy(f32[4,128,2,4,2,704]{1,3,0,4,5,2:T(4,128)} %bitcast.108) | data formatting | bytes 46137344
  1468.5 31.4 %reshape.231 = f32[512,11264]{1,0:T(8,128)} reshape(f32[4,128,2,4,2,704]{5,4,3,2,1,0:T(2,128)} %copy.77) | data formatting | bytes 46137344
  1499.9 4.1 convert_element_type.136
  1504.1 39.1 %psum.7 = f32[4,3584]{1,0:T(4,128)S(1)} all-reduce(f32[4,3584]{1,0:T(4,128)S(1)} %constant_dynamic-update-slice_fusion.4), channel_id=1, replica_groups=mesh['dp'=4,'pl'=4,'core'=2] {'dp','pl','core'}, use_global_device_ids=true, to_apply=%region_17.18 | all-reduce | flops 14336 | bytes 114688 | tf_op jit(solution)/shard_map/psum | solution.py:394
  1546.1 15.3 reshape.220
  1561.5 19.2 %copy.69 = f32[4,128,3,4,2,256]{5,4,3,2,1,0:T(2,128)} copy(f32[4,128,3,4,2,256]{1,3,0,4,5,2:T(4,128)} %bitcast.109) | data formatting | bytes 25165824 | tf_op jit(solution)/shard_map/convert_element_type | solution.py:380
  1580.6 16.3 %reshape.218 = f32[512,6144]{1,0:T(8,128)} reshape(f32[4,128,3,4,2,256]{5,4,3,2,1,0:T(2,128)} %copy.69) | data formatting | bytes 25165824 | tf_op jit(solution)/shard_map/convert_element_type | solution.py:380
  (149 shorter events, 47.7 us)
Async XLA Ops:
  7.2 236.7 %copy-start = (bf16[512,2048]{1,0:T(8,128)(2,1)S(1)}, bf16[512,2048]{1,0:T(8,128)(2,1)}, u32[]{:S(2)}) copy-start(bf16[512,2048]{1,0:T(8,128)(2,1)} %param.18) | copy-start | bytes 6291460
  7.2 183.6 %all-gather.12.cloned.1.call-start = ((), (), s32[]{:S(2)}) async-start(), calls=%async_computation.12 | async-start | bytes 9437184 | tf_op jit(solution)/shard_map/all_gather | solution.py:309
  7.2 35.9 %collective-permute-start = (bf16[256,2048]{1,0:T(8,128)(2,1)}, bf16[256,2048]{1,0:T(8,128)(2,1)S(1)}, u32[]{:S(2)}, u32[]{:S(2)}) collective-permute-start(bf16[256,2048]{1,0:T(8,128)(2,1)} %bitcast.148), channel_id=1, source_target_pairs={{0,0},{2,8},{4,16},{6,24},{8,2},{10,10},{12,18},{14,26},{16,4},{18... | collective-permute-start | bytes 3145736 | tf_op jit(solution)/shard_map/ppermute | solution.py:308
  43.2 0.7 copy-start.10
  43.4 10.6 copy-start.12
  43.9 10.1 copy-start.14
  57.9 41.9 %copy-start.17 = (s32[1,2]{1,0:T(1,128)S(1)}, s32[1,2]{1,0:T(1,128)}, u32[]{:S(2)}) copy-start(s32[1,2]{1,0:T(1,128)} %param.13) | copy-start | bytes 28
  57.9 128.2 %all-to-all-start = ((bf16[4,512,768]{1,2,0:T(8,128)(2,1)}), bf16[4,512,768]{1,2,0:T(8,128)(2,1)}, u32[]{:S(2)}, u32[]{:S(2)}) async-start(bf16[4,512,768]{1,2,0:T(8,128)(2,1)} %bitcast.115), calls=%async_computation | async-start | bytes 6291456 | tf_op jit(solution)/shard_map/all_to_all | solution.py:316
  99.8 222.4 %reduce-scatter.9.cloned.1.call-start = ((), (), s32[]{:S(2)}) async-start(), calls=%async_computation.13 | async-start | bytes 9437184 | tf_op jit(solution)/shard_map/reduce_scatter | solution.py:310
  250.8 276.6 %all-gather.14.cloned.1.call-start = ((), (), s32[]{:S(2)}) async-start(), calls=%async_computation.14 | async-start | bytes 9437184 | tf_op jit(solution)/shard_map/all_gather | solution.py:309
  322.2 3.4 copy-start.2
  327.2 219.0 %all-gather.16.cloned.1.call-start = ((), (), s32[]{:S(2)}) async-start(), calls=%async_computation.16 | async-start | bytes 9437184 | tf_op jit(solution)/shard_map/all_gather | solution.py:309
  327.2 9.5 collective-permute-start.2
  336.8 315.0 %reduce-scatter.13.cloned.1.call-start = ((), (), s32[]{:S(2)}) async-start(), calls=%async_computation.17 | async-start | bytes 9437184 | tf_op jit(solution)/shard_map/reduce_scatter | solution.py:310
  546.2 16.2 %copy-start.8 = (bf16[4,512,1408]{2,1,0:T(8,128)(2,1)S(1)}, bf16[4,512,1408]{2,1,0:T(8,128)(2,1)}, u32[]{:S(2)}) copy-start(bf16[4,512,1408]{2,1,0:T(8,128)(2,1)} %copy.66) | copy-start | bytes 17301508
  580.2 132.3 %all-gather.18.cloned.1.call-start = ((), (), s32[]{:S(2)}) async-start(), calls=%async_computation.18 | async-start | bytes 9437184 | tf_op jit(solution)/shard_map/all_gather | solution.py:309
  651.8 2.8 copy-start.3
  651.8 2.8 copy-start.6
  658.0 159.5 %reduce-scatter.23.cloned.1.call-start = ((), (), s32[]{:S(2)}) async-start(), calls=%async_computation.26 | async-start | bytes 3604480 | tf_op jit(solution)/shard_map/reduce_scatter | solution.py:370
  668.7 207.4 %reduce-scatter.21.cloned.1.call-start = ((), (), s32[]{:S(2)}) async-start(), calls=%async_computation.24 | async-start | bytes 7208960 | tf_op jit(solution)/shard_map/reduce_scatter | solution.py:376
  689.1 217.6 %reduce-scatter.19.cloned.1.call-start = ((), (), s32[]{:S(2)}) async-start(), calls=%async_computation.22 | async-start | bytes 1310720 | tf_op jit(solution)/shard_map/reduce_scatter | solution.py:370
  769.7 4.6 copy-start.5
  774.3 6.9 copy-start.9
  781.1 186.7 %reduce-scatter.17.cloned.1.call-start = ((), (), s32[]{:S(2)}) async-start(), calls=%async_computation.20 | async-start | bytes 3932160 | tf_op jit(solution)/shard_map/reduce_scatter | solution.py:376
  794.6 248.8 %reduce-scatter.15.cloned.1.call-start = ((), (), s32[]{:S(2)}) async-start(), calls=%async_computation.19 | async-start | bytes 9437184 | tf_op jit(solution)/shard_map/reduce_scatter | solution.py:310
  806.0 312.8 %reduce-scatter.11.cloned.1.call-start = ((), (), s32[]{:S(2)}) async-start(), calls=%async_computation.15 | async-start | bytes 9437184 | tf_op jit(solution)/shard_map/reduce_scatter | solution.py:310
  817.4 473.4 %all-gather.26.cloned.1.call-start = ((), (), s32[]{:S(2)}) async-start(), calls=%async_computation.27 | async-start | bytes 6488064 | tf_op jit(solution)/shard_map/all_gather | solution.py:371
  818.2 586.4 %all-gather.24.cloned.1.call-start = ((), (), s32[]{:S(2)}) async-start(), calls=%async_computation.25 | async-start | bytes 12976128 | tf_op jit(solution)/shard_map/all_gather | solution.py:378
  899.7 143.6 %copy-start.11 = (f32[1,4,4,128]{3,1,2,0:T(4,128)S(1)}, f32[1,4,4,128]{3,1,2,0:T(4,128)}, u32[]{:S(2)}) copy-start(f32[1,4,4,128]{3,1,2,0:T(4,128)} %copy-done.10) | copy-start | bytes 24580
  899.7 143.6 %copy-start.13 = (f32[256]{0:T(256)S(1)}, f32[256]{0:T(256)}, u32[]{:S(2)}) copy-start(f32[256]{0:T(256)} %copy-done.12) | copy-start | bytes 3076
  899.7 143.6 %copy-start.15 = (f32[256]{0:T(256)S(1)}, f32[256]{0:T(256)}, u32[]{:S(2)}) copy-start(f32[256]{0:T(256)} %copy-done.14) | copy-start | bytes 3076
  899.7 600.2 %all-gather.22.cloned.1.call-start = ((), (), s32[]{:S(2)}) async-start(), calls=%async_computation.23 | async-start | bytes 2359296 | tf_op jit(solution)/shard_map/all_gather | solution.py:371
  906.8 639.3 %all-gather.20.cloned.1.call-start = ((), (), s32[]{:S(2)}) async-start(), calls=%async_computation.21 | async-start | bytes 7077888 | tf_op jit(solution)/shard_map/all_gather | solution.py:378
  967.8 150.9 %copy-start.4 = (bf16[256,2048]{1,0:T(8,128)(2,1)S(1)}, bf16[256,2048]{1,0:T(8,128)(2,1)}, u32[]{:S(2)}) copy-start(bf16[256,2048]{1,0:T(8,128)(2,1)} %reduce-scatter.9.cloned.1.call-done) | copy-start | bytes 3145732
  967.8 150.9 %copy-start.7 = (bf16[256,2048]{1,0:T(8,128)(2,1)S(1)}, bf16[256,2048]{1,0:T(8,128)(2,1)}, u32[]{:S(2)}) copy-start(bf16[256,2048]{1,0:T(8,128)(2,1)} %reduce-scatter.13.cloned.1.call-done) | copy-start | bytes 3145732
  1123.5 421.1 %collective-permute-start.1 = (bf16[256,2048]{1,0:T(8,128)(2,1)}, bf16[256,2048]{1,0:T(8,128)(2,1)S(1)}, u32[]{:S(2)}, u32[]{:S(2)}) collective-permute-start(bf16[256,2048]{1,0:T(8,128)(2,1)} %get-tuple-element.85), channel_id=1, source_target_pairs={{0,0},{2,8},{4,16},{6,24},{8,2},{10,10},{12,18},{14,26},{16,4},{18... | collective-permute-start | bytes 3145736 | tf_op jit(solution)/shard_map/ppermute | solution.py:308
  1125.4 419.2 %collective-permute-start.3 = (bf16[256,2048]{1,0:T(8,128)(2,1)}, bf16[256,2048]{1,0:T(8,128)(2,1)S(1)}, u32[]{:S(2)}, u32[]{:S(2)}) collective-permute-start(bf16[256,2048]{1,0:T(8,128)(2,1)} %get-tuple-element.84), channel_id=1, source_target_pairs={{0,0},{2,8},{4,16},{6,24},{8,2},{10,10},{12,18},{14,26},{16,4},{18... | collective-permute-start | bytes 3145736 | tf_op jit(solution)/shard_map/ppermute | solution.py:308
  1127.3 172.2 %copy-start.16 = (f32[8,256]{1,0:T(8,128)S(1)}, f32[8,256]{1,0:T(8,128)}, u32[]{:S(2)}) copy-start(f32[8,256]{1,0:T(8,128)} %get-tuple-element.28) | copy-start | bytes 24580
  1580.6 17.3 %copy-start.1 = (bf16[512,2048]{1,0:T(8,128)(2,1)S(1)}, bf16[512,2048]{1,0:T(8,128)(2,1)}, u32[]{:S(2)}) copy-start(bf16[512,2048]{1,0:T(8,128)(2,1)} %param.18) | copy-start | bytes 6291460
Sparse Core Ops, SparseCore 0:
  45.5 119.9 all-gather.11
  251.0 71.1 reduce-scatter.8
  327.3 94.1 all-gather.13
  423.3 98.6 all-gather.15
  580.3 71.4 reduce-scatter.12
  658.2 54.2 all-gather.17
  714.8 56.3 reduce-scatter.22
  774.0 102.0 reduce-scatter.20
  878.9 27.8 reduce-scatter.18
  908.9 58.8 reduce-scatter.16
  971.9 71.3 reduce-scatter.14
  1047.2 71.4 reduce-scatter.10
  1120.3 170.4 all-gather.25
  1292.9 111.6 all-gather.23
  1406.0 29.1 all-gather.21
  1436.6 64.0 all-gather.19

commit v2 on v1

--- a/solution.py
+++ b/solution.py
@@ -166,6 +166,7 @@
             ],
         ),
         compiler_params=pltpu.CompilerParams(vmem_limit_bytes=56 * 2**20),
+        cost_estimate=cost(41, 0),
         name="attend",
     )(slot_of, proj, proj, proj, bias, bias, bias, *tables)
 
@@ -277,8 +278,702 @@
             ],
         ),
         compiler_params=pltpu.CompilerParams(vmem_limit_bytes=56 * 2**20),
+        cost_estimate=cost(50, 0),
         name="attend_back",
     )(slot_of, qs, ks, vs, att, gat, lse, *tables)
+
+
+HBM = pltpu.MemorySpace.HBM
+MESH_ID = pl.DeviceIdType.MESH
+
+
+def ring_pos(dp, n):
+    odd, half = dp % 2, dp // 2
+    return odd * (half + 1) + (1 - odd) * ((n - half) % n)
+
+
+def ring_dp(pos, n):
+    far = ((pos + n - 1) % n) // (n // 2)
+    return (1 - far) * (2 * pos - 1) + far * (2 * ((n - pos) % n))
+
+
+def plane_ids(n):
+    dp, core = lax.axis_index("dp"), lax.axis_index("core")
+    pos = ring_pos(dp, n)
+    at = lambda off: ring_dp((pos + off + n) % n, n)
+    return dp, core, at
+
+
+def greet(ids):
+    barrier = pltpu.get_barrier_semaphore()
+    for where in ids:
+        pl.semaphore_signal(barrier, inc=1, device_id=where, device_id_type=MESH_ID)
+    pl.semaphore_wait(barrier, len(ids))
+
+
+def remote(src, dst, send, recv, where):
+    return pltpu.make_async_remote_copy(
+        src_ref=src, dst_ref=dst, send_sem=send, recv_sem=recv, device_id=where, device_id_type=MESH_ID
+    )
+
+
+def col_tile(width):
+    for t in (512, 384, 256, 128):
+        if width % t == 0:
+            return t
+    return width
+
+
+def gather_blocks(n, x_ref, buf, s_in, s_ring, r_ring, s_part, r_part, ready, use):
+    dp, core, at = plane_ids(n)
+    rows = x_ref.shape[0]
+    half = rows // 2
+    mid = n // 2
+    slot = lambda off, flip: 2 * at(off) + (core if flip == 0 else 1 - core)
+    right, left, mate = {"dp": at(1)}, {"dp": at(-1)}, {"core": 1 - core}
+    load_x = pltpu.make_async_copy(x_ref, buf.at[slot(0, 0)], s_in)
+    load_x.start()
+    greet((right, left, mate))
+    load_x.wait()
+    top, low = pl.ds(0, half), pl.ds(half, half)
+
+    def push(src_slot, part, where, send, recv):
+        view = buf.at[src_slot] if part is None else buf.at[src_slot, part]
+        remote(view, view, send, recv, where).start()
+
+    def sent(part, send):
+        view = buf.at[0] if part is None else buf.at[0, part]
+        remote(view, view, send, r_ring.at[0, 0], right).wait_send()
+
+    def arrive(src_slot, part, sem):
+        view = buf.at[src_slot] if part is None else buf.at[src_slot, part]
+        remote(view, view, s_ring.at[0, 0], sem, right).wait_recv()
+
+    own = slot(0, 0)
+    push(own, None, right, s_ring.at[0, 0], r_ring.at[1, 0])
+    push(own, None, left, s_ring.at[0, 1], r_ring.at[1, 1])
+    push(own, None, mate, s_part.at[0, 0], r_part.at[0, 0])
+
+    def ring_step(d):
+        for side, sign in ((0, -1), (1, 1)):
+            src = slot(sign * d, 0)
+            onward = right if side == 0 else left
+            if d < mid:
+                arrive(src, None, r_ring.at[d, side])
+                if d + 1 < mid:
+                    push(src, None, onward, s_ring.at[d, side], r_ring.at[d + 1, side])
+                else:
+                    push(src, top if side == 0 else low, onward, s_ring.at[d, side], r_ring.at[mid, side])
+                push(src, None, mate, s_part.at[d, side], r_part.at[d, side])
+            else:
+                part = top if side == 0 else low
+                arrive(src, part, r_ring.at[mid, side])
+                push(src, part, mate, s_part.at[mid, side], r_part.at[mid, side])
+
+    def mate_step(d):
+        if d == 0:
+            arrive(slot(0, 1), None, r_part.at[0, 0])
+        elif d < mid:
+            arrive(slot(-d, 1), None, r_part.at[d, 0])
+            arrive(slot(d, 1), None, r_part.at[d, 1])
+        else:
+            arrive(slot(d, 1), top, r_part.at[d, 0])
+            arrive(slot(d, 1), low, r_part.at[d, 1])
+
+    ready()
+
+    def body(step, carry):
+        for d in range(1, mid + 1):
+            first = 2 + 4 * (d - 1)
+
+            @pl.when(step == first)
+            def _():
+                ring_step(d)
+
+            @pl.when(step == first + (2 if d < mid else 1))
+            def _():
+                mate_step(d)
+
+        @pl.when(step == 1)
+        def _():
+            mate_step(0)
+
+        later = jnp.maximum(step - 2, 0)
+        d = jnp.where(step < 2, 0, 1 + later // 4)
+        kind = jnp.where(step < 2, step, later % 4)
+        last = jnp.where(step < 2, 1, d // mid)
+        flip = jnp.where(last == 1, kind, kind // 2)
+        off = jnp.where(kind % 2 == 0, -d, d)
+        use(step, 2 * at(off) + core + flip - 2 * core * flip)
+        return carry
+
+    lax.fori_loop(0, 2 * n, body, 0)
+    for d in range(mid + 1):
+        for side in range(2):
+            part = top if side == 0 else low
+            if d < mid:
+                sent(part if d + 1 == mid and d > 0 else None, s_ring.at[d, side])
+            if d > 0 or side == 0:
+                sent(part if d == mid else None, s_part.at[d, side])
+
+
+def gather_dot_kernel(
+    n, trans, x_ref, w_ref, all_ref, res_ref, buf, wv, stage, s_ring, r_ring, s_part, r_part, s_in, s_out, s_res
+):
+    load_w = pltpu.make_async_copy(w_ref, wv, s_in.at[0])
+    load_w.start()
+    width = res_ref.shape[-1]
+    tile = col_tile(width)
+
+    def put(keep, where):
+        return pltpu.make_async_copy(stage.at[keep], res_ref.at[where], s_res.at[keep])
+
+    def use(step, where):
+        keep = step % 2
+
+        @pl.when(step >= 2)
+        def _():
+            put(keep, where).wait()
+
+        pltpu.make_async_copy(buf.at[where], all_ref.at[where], s_out.at[step]).start()
+        block = buf[where]
+        for c in range(width // tile):
+            cols = pl.ds(c * tile, tile)
+            part = nt(block, wv[cols, :]) if trans else nn(block, wv[:, cols])
+            stage[keep, :, cols] = part.astype(stage.dtype)
+        put(keep, where).start()
+
+    gather_blocks(n, x_ref, buf, s_in.at[1], s_ring, r_ring, s_part, r_part, load_w.wait, use)
+    for keep in range(2):
+        put(keep, 0).wait()
+    for step in range(2 * n):
+        pltpu.make_async_copy(buf.at[0], all_ref.at[0], s_out.at[step]).wait()
+
+
+def cost(us, flops):
+    return pl.CostEstimate(flops=flops, bytes_accessed=int(us * 3.4e6), transcendentals=0)
+
+
+def ring_sems(n):
+    dma = pltpu.SemaphoreType.DMA
+    mid = n // 2
+    return [dma((mid, 2)), dma((mid + 1, 2)), dma((mid + 1, 2)), dma((mid + 1, 2))]
+
+
+def gather_dot(n, cid, x, w, trans, dtype):
+    rows, depth = x.shape
+    width = w.shape[0] if trans else w.shape[1]
+    dma = pltpu.SemaphoreType.DMA
+    everything, result = pl.pallas_call(
+        functools.partial(gather_dot_kernel, n, trans),
+        out_shape=(
+            jax.ShapeDtypeStruct((2 * n, rows, depth), x.dtype),
+            jax.ShapeDtypeStruct((2 * n, rows, width), dtype),
+        ),
+        in_specs=[pl.BlockSpec(memory_space=HBM)] * 2,
+        out_specs=[pl.BlockSpec(memory_space=HBM)] * 2,
+        scratch_shapes=[
+            pltpu.VMEM((2 * n, rows, depth), x.dtype),
+            pltpu.VMEM(w.shape, w.dtype),
+            pltpu.VMEM((2, rows, width), dtype),
+        ]
+        + ring_sems(n)
+        + [dma((2,)), dma((2 * n,)), dma((2,))],
+        compiler_params=pltpu.CompilerParams(
+            collective_id=cid, has_side_effects=True, vmem_limit_bytes=60 * 2**20
+        ),
+        cost_estimate=cost(42, 4 * n * rows * depth * width),
+        name="gather_dot",
+    )(x, w)
+    return everything.reshape(2 * n * rows, depth), result.reshape(2 * n * rows, width)
+
+
+def gather_mlp_kernel(
+    n, x_ref, w_ref, c_ref, d_ref, all_ref, act_ref, gg_ref, gu_ref, buf, wv, dv, cv, stage, s_ring, r_ring, s_part, r_part, s_in, s_c, s_out, s_res
+):
+    load_w = pltpu.make_async_copy(w_ref, wv, s_in.at[0])
+    load_d = pltpu.make_async_copy(d_ref, dv, s_in.at[2])
+    load_w.start()
+    load_d.start()
+    outs = (act_ref, gg_ref, gu_ref)
+
+    def put(keep, k, where):
+        return pltpu.make_async_copy(stage.at[keep, k], outs[k].at[where], s_res.at[keep, k])
+
+    def ready():
+        load_w.wait()
+        load_d.wait()
+
+    def use(step, where):
+        keep = step % 2
+        load_c = pltpu.make_async_copy(c_ref.at[where], cv, s_c)
+        load_c.start()
+
+        @pl.when(step >= 2)
+        def _():
+            for k in range(3):
+                put(keep, k, where).wait()
+
+        pltpu.make_async_copy(buf.at[where], all_ref.at[where], s_out.at[step]).start()
+        block = buf[where]
+        gate = nn(block, wv[0])
+        upper = nn(block, wv[1])
+        load_c.wait()
+        back = nt(cv[...], dv[...])
+        sig = 1.0 / (1.0 + jnp.exp(-gate))
+        swish = gate * sig
+        stage[keep, 0] = (swish * upper).astype(BF16)
+        stage[keep, 1] = (back * upper * sig * (1.0 + gate * (1.0 - sig))).astype(BF16)
+        stage[keep, 2] = (back * swish).astype(BF16)
+        for k in range(3):
+            put(keep, k, where).start()
+
+    gather_blocks(n, x_ref, buf, s_in.at[1], s_ring, r_ring, s_part, r_part, ready, use)
+    for keep in range(2):
+        for k in range(3):
+            put(keep, k, 0).wait()
+    for step in range(2 * n):
+        pltpu.make_async_copy(buf.at[0], all_ref.at[0], s_out.at[step]).wait()
+
+
+def gather_mlp(n, cid, x, w, cot, wd):
+    rows, depth = x.shape
+    units = wd.shape[0]
+    dma = pltpu.SemaphoreType.DMA
+    out = jax.ShapeDtypeStruct((2 * n, rows, units), BF16)
+    res = pl.pallas_call(
+        functools.partial(gather_mlp_kernel, n),
+        out_shape=(jax.ShapeDtypeStruct((2 * n, rows, depth), x.dtype), out, out, out),
+        in_specs=[pl.BlockSpec(memory_space=HBM)] * 4,
+        out_specs=[pl.BlockSpec(memory_space=HBM)] * 4,
+        scratch_shapes=[
+            pltpu.VMEM((2 * n, rows, depth), x.dtype),
+            pltpu.VMEM(w.shape, w.dtype),
+            pltpu.VMEM(wd.shape, wd.dtype),
+            pltpu.VMEM((rows, depth), BF16),
+            pltpu.VMEM((2, 3, rows, units), BF16),
+        ]
+        + ring_sems(n)
+        + [dma((3,)), dma, dma((2 * n,)), dma((2, 3))],
+        compiler_params=pltpu.CompilerParams(
+            collective_id=cid, has_side_effects=True, vmem_limit_bytes=60 * 2**20
+        ),
+        cost_estimate=cost(48, 12 * n * rows * depth * units),
+        name="gather_mlp",
+    )(x, w, cot.reshape(2 * n, rows, depth), wd)
+    return [a.reshape(2 * n * rows, -1) for a in res]
+
+
+def dot_scatter_kernel(
+    n, count, trans, *refs
+):
+    a_refs, w_refs, out_ref = refs[:count], refs[count : 2 * count], refs[2 * count]
+    avs, wvs = refs[2 * count + 1 : 3 * count + 1], refs[3 * count + 1 : 4 * count + 1]
+    to_mate, from_mate, hop, from_ring, acc, s_a, s_w, s_part, r_part, s_ring, r_ring, s_o = refs[4 * count + 1 :]
+    dp, core, at = plane_ids(n)
+    rows = acc.shape[0]
+    half = rows // 2
+    mid = n // 2
+    right, left, mate = {"dp": at(1)}, {"dp": at(-1)}, {"core": 1 - core}
+    offsets = [mid]
+    for d in range(mid - 1, 0, -1):
+        offsets += [d, -d]
+    offsets += [0]
+
+    def offset_of(j):
+        d = mid - (j + 1) // 2
+        return jnp.where(j % 2 == 1, d, -d)
+
+    loads = [pltpu.make_async_copy(w_refs[k], wvs[k], s_w.at[k]) for k in range(count)]
+    for load in loads:
+        load.start()
+
+    def slot_of(step):
+        j, own = step // 2, step % 2
+        who = core + (1 - own) - 2 * core * (1 - own)
+        return 2 * at(offset_of(j)) + who
+
+    def load_a(step, k):
+        return pltpu.make_async_copy(a_refs[k].at[slot_of(step)], avs[k].at[step], s_a.at[step, k])
+
+    for step in range(2 * n):
+        for k in range(count):
+            load_a(step, k).start()
+    greet((right, left, mate))
+    for load in loads:
+        load.wait()
+    depth = out_ref.shape[-1]
+    tile = col_tile(depth)
+    top, low = pl.ds(0, half), pl.ds(half, half)
+    waits = []
+
+    def hand(j):
+        return remote(to_mate.at[j], from_mate.at[j], s_part.at[j], r_part.at[j], mate)
+
+    def ring(j, part, side, send, recv):
+        src = hop.at[j] if part is None else hop.at[j, part]
+        dst = from_ring.at[recv, side] if part is None else from_ring.at[recv, side, part]
+        return remote(src, dst, s_ring.at[send, side], r_ring.at[recv, side], right if side == 0 else left)
+
+    def body(step, carry):
+        j, own = step // 2, step % 2
+        for k in range(count):
+            load_a(step, k).wait()
+
+        def product(cols):
+            total = None
+            for k in range(count):
+                block = avs[k][step]
+                part = nt(block, wvs[k][cols, :]) if trans else nn(block, wvs[k][:, cols])
+                total = part if total is None else total + part
+            return total
+
+        @pl.when(own == 0)
+        def _():
+            for c in range(depth // tile):
+                cols = pl.ds(c * tile, tile)
+                to_mate[j, :, cols] = product(cols).astype(BF16)
+            hand(j).start()
+
+        @pl.when(own == 1)
+        def _():
+            hand(j).wait_recv()
+            for c in range(depth // tile):
+                cols = pl.ds(c * tile, tile)
+                part = product(cols) + from_mate[j, :, cols].astype(F32)
+                acc[:, cols] = part
+                hop[j, :, cols] = part.astype(BF16)
+
+            @pl.when(j == 0)
+            def _():
+                ring(0, top, 0, 0, mid - 1).start()
+                ring(0, low, 1, 0, mid - 1).start()
+
+            for d in range(mid - 1, 0, -1):
+                first = 1 + 2 * (mid - 1 - d)
+
+                @pl.when(j == first + 1)
+                def _():
+                    for side in range(2):
+                        k = first + side
+                        if d == mid - 1:
+                            part = top if side == 0 else low
+                            ring(0, part, side, 0, d).wait_recv()
+                            hop[k, part, :] = (
+                                hop[k, part, :].astype(F32) + from_ring[d, side, part, :].astype(F32)
+                            ).astype(BF16)
+                        else:
+                            ring(k - 2, None, side, 0, d).wait_recv()
+                            hop[k] = (hop[k].astype(F32) + from_ring[d, side].astype(F32)).astype(BF16)
+                        ring(k, None, side, mid - d, d - 1).start()
+
+        return carry
+
+    lax.fori_loop(0, 2 * n, body, 0)
+    for side in range(2):
+        ring(n - 2 + side - 1, None, side, mid - 1, 0).wait_recv()
+    acc[...] += from_ring[0, 0].astype(F32) + from_ring[0, 1].astype(F32)
+    put = pltpu.make_async_copy(acc, out_ref, s_o)
+    put.start()
+    for j in range(n):
+        hand(j).wait_send()
+    ring(0, top, 0, 0, mid - 1).wait_send()
+    ring(0, low, 1, 0, mid - 1).wait_send()
+    for d in range(mid - 1, 0, -1):
+        for side in range(2):
+            ring(1 + 2 * (mid - 1 - d) + side, None, side, mid - d, d - 1).wait_send()
+    put.wait()
+
+
+def dot_scatter(n, cid, terms, trans):
+    depth = terms[0][1].shape[0] if trans else terms[0][1].shape[1]
+    rows = terms[0][0].shape[0] // (2 * n)
+    mid = n // 2
+    count = len(terms)
+    dma = pltpu.SemaphoreType.DMA
+    lhs = [a.reshape(2 * n, rows, a.shape[1]) for a, _ in terms]
+    rhs = [w for _, w in terms]
+    return pl.pallas_call(
+        functools.partial(dot_scatter_kernel, n, count, trans),
+        out_shape=jax.ShapeDtypeStruct((rows, depth), F32),
+        in_specs=[pl.BlockSpec(memory_space=HBM)] * (2 * count),
+        out_specs=pl.BlockSpec(memory_space=HBM),
+        scratch_shapes=[pltpu.VMEM(a.shape, BF16) for a in lhs]
+        + [pltpu.VMEM(w.shape, BF16) for w in rhs]
+        + [
+            pltpu.VMEM((n, rows, depth), BF16),
+            pltpu.VMEM((n, rows, depth), BF16),
+            pltpu.VMEM((n, rows, depth), BF16),
+            pltpu.VMEM((mid, 2, rows, depth), BF16),
+            pltpu.VMEM((rows, depth), F32),
+            dma((2 * n, count)),
+            dma((count,)),
+            dma((n,)),
+            dma((n,)),
+            dma((mid, 2)),
+            dma((mid, 2)),
+            dma,
+        ],
+        compiler_params=pltpu.CompilerParams(
+            collective_id=cid, has_side_effects=True, vmem_limit_bytes=62 * 2**20
+        ),
+        cost_estimate=cost(45, 4 * n * rows * depth * sum(a.shape[2] for a in lhs)),
+        name="dot_scatter",
+    )(*lhs, *rhs)
+
+
+def start_kernel(
+    n, x_ref, w_ref, small_ref, block_ref, x_out, w_out, small_out, block_out, xv, wv, s_own, s_x, r_x, s_w, r_w, s_s, r_s, s_b, r_b
+):
+    dp, plane, core = (lax.axis_index(a) for a in EVERY)
+    rows = w_ref.shape[0]
+    width = w_ref.shape[1] // 3
+    wide = width // (2 * n)
+    away = dp != plane
+    across = {"dp": plane, "pl": dp, "core": core}
+    barrier = pltpu.get_barrier_semaphore()
+
+    def knock(where):
+        pl.semaphore_signal(barrier, inc=1, device_id=where, device_id_type=MESH_ID)
+
+    def send_x():
+        return remote(x_ref, x_out, s_x, r_x, across)
+
+    def send_w(j, part):
+        to = (dp + j) % n
+        at = pl.multiple_of(part * width + to * (2 * wide) + core * wide, 128)
+        dst = w_out.at[pl.ds(pl.multiple_of(dp * rows, 128), rows), pl.ds(part * wide, wide)]
+        return remote(w_ref.at[:, pl.ds(at, wide)], dst, s_w.at[j, part], r_w.at[j, part], {"dp": to})
+
+    def send_s(j):
+        to = (dp + j) % n
+        return remote(small_ref, small_out.at[dp], s_s.at[j], r_s.at[j], {"dp": to})
+
+    def send_b(i, k):
+        to = {"dp": (plane + i) % n, "pl": dp, "core": (core + k) % 2}
+        return remote(block_ref, block_out.at[2 * plane + core], s_b.at[i, k], r_b.at[i, k], to)
+
+    def own_w(part, back):
+        at = pl.multiple_of(part * width + dp * (2 * wide) + core * wide, 128)
+        src = w_ref.at[:, pl.ds(at, wide)]
+        dst = w_out.at[pl.ds(pl.multiple_of(dp * rows, 128), rows), pl.ds(part * wide, wide)]
+        if back:
+            return pltpu.make_async_copy(wv.at[part], dst, s_own.at[part])
+        return pltpu.make_async_copy(src, wv.at[part], s_own.at[part])
+
+    own_s = pltpu.make_async_copy(small_ref, small_out.at[dp], s_own.at[3])
+    own_b = pltpu.make_async_copy(block_ref, block_out.at[2 * plane + core], s_own.at[4])
+    for part in range(3):
+        own_w(part, False).start()
+    own_s.start()
+    for j in range(1, n):
+        knock({"dp": (dp + n - j) % n})
+    for i in range(n):
+        for k in range(2):
+
+            @pl.when(away | (i + k > 0))
+            def _():
+                knock({"dp": plane, "pl": (dp + n - i) % n, "core": (core + k) % 2})
+
+    @pl.when(away)
+    def _():
+        knock(across)
+        pl.semaphore_wait(barrier, 3 * n)
+        send_x().start()
+        send_b(0, 0).start()
+
+    @pl.when(jnp.logical_not(away))
+    def _():
+        pl.semaphore_wait(barrier, 3 * n - 2)
+        pltpu.make_async_copy(x_ref, xv, s_own.at[5]).start()
+        own_b.start()
+
+    for i in range(n):
+        for k in range(2):
+            if i + k > 0:
+                send_b(i, k).start()
+    for j in range(1, n):
+        send_s(j).start()
+    for j in range(1, n):
+        for part in range(3):
+            send_w(j, part).start()
+    for part in range(3):
+        own_w(part, False).wait()
+        own_w(part, True).start()
+
+    @pl.when(jnp.logical_not(away))
+    def _():
+        pltpu.make_async_copy(x_ref, xv, s_own.at[5]).wait()
+        pltpu.make_async_copy(xv, x_out, s_own.at[5]).start()
+        own_b.wait()
+        pltpu.make_async_copy(xv, x_out, s_own.at[5]).wait()
+
+    own_s.wait()
+    for part in range(3):
+        own_w(part, True).wait()
+    for i in range(n):
+        for k in range(2):
+            if i + k > 0:
+                send_b(i, k).wait()
+    for j in range(1, n):
+        send_s(j).wait()
+        for part in range(3):
+            send_w(j, part).wait()
+
+    @pl.when(away)
+    def _():
+        send_b(0, 0).wait()
+        send_x().wait()
+
+
+def start(n, cid, x, w, small, block):
+    rows, wide = w.shape[0], w.shape[1] // (6 * n)
+    dma = pltpu.SemaphoreType.DMA
+    return pl.pallas_call(
+        functools.partial(start_kernel, n),
+        out_shape=(
+            jax.ShapeDtypeStruct(x.shape, x.dtype),
+            jax.ShapeDtypeStruct((n * rows, 3 * wide), w.dtype),
+            jax.ShapeDtypeStruct((n,) + small.shape, small.dtype),
+            jax.ShapeDtypeStruct((2 * n,) + block.shape, block.dtype),
+        ),
+        in_specs=[pl.BlockSpec(memory_space=HBM)] * 4,
+        out_specs=[pl.BlockSpec(memory_space=HBM)] * 4,
+        scratch_shapes=[
+            pltpu.VMEM(x.shape, x.dtype),
+            pltpu.VMEM((3, rows, wide), w.dtype),
+            dma((6,)),
+            dma,
+            dma,
+            dma((n, 3)),
+            dma((n, 3)),
+            dma((n,)),
+            dma((n,)),
+            dma((n, 2)),
+            dma((n, 2)),
+        ],
+        compiler_params=pltpu.CompilerParams(collective_id=cid, has_side_effects=True),
+        cost_estimate=cost(75, 0),
+        name="start",
+    )(x, w, small, block)
+
+
+def total_kernel(n, a_ref, o_ref, mine, others, part, sums, s_in, s_a, r_a, s_b, r_b, s_out):
+    dp, plane, core = (lax.axis_index(a) for a in EVERY)
+    barrier = pltpu.get_barrier_semaphore()
+    load = pltpu.make_async_copy(a_ref, mine, s_in)
+    load.start()
+    peers = [{"dp": (dp + j) % n} for j in range(1, n)]
+    stack = [(z, k) for z in range(n) for k in range(2) if z + k > 0]
+    for j in range(1, n):
+        pl.semaphore_signal(barrier, inc=1, device_id={"dp": (dp + n - j) % n}, device_id_type=MESH_ID)
+    for z, k in stack:
+        where = {"pl": (plane + n - z) % n, "core": (core + k) % 2}
+        pl.semaphore_signal(barrier, inc=1, device_id=where, device_id_type=MESH_ID)
+    pl.semaphore_wait(barrier, 3 * n - 2)
+    load.wait()
+
+    def send_a(j):
+        to = (dp + j) % n
+        return remote(mine.at[to], others.at[j], s_a.at[j], r_a.at[j], {"dp": to})
+
+    def send_b(i):
+        z, k = stack[i]
+        where = {"pl": (plane + z) % n, "core": (core + k) % 2}
+        return remote(part, sums.at[i], s_b.at[i], r_b.at[i], where)
+
+    for j in range(1, n):
+        send_a(j).start()
+    value = mine[dp]
+    for j in range(1, n):
+        send_a(j).wait_recv()
+        value = value + others[j]
+    part[...] = value
+    for i in range(len(stack)):
+        send_b(i).start()
+    for i in range(len(stack)):
+        send_b(i).wait_recv()
+        value = value + sums[i]
+    for j in range(1, n):
+        send_a(j).wait_send()
+    for i in range(len(stack)):
+        send_b(i).wait_send()
+    mine[0] = value
+    put = pltpu.make_async_copy(mine.at[0], o_ref, s_out)
+    put.start()
+    put.wait()
+
+
+def total(n, cid, a):
+    dma = pltpu.SemaphoreType.DMA
+    shape = a.shape[1:]
+    return pl.pallas_call(
+        functools.partial(total_kernel, n),
+        out_shape=jax.ShapeDtypeStruct(shape, F32),
+        in_specs=[pl.BlockSpec(memory_space=HBM)],
+        out_specs=pl.BlockSpec(memory_space=HBM),
+        scratch_shapes=[
+            pltpu.VMEM(a.shape, F32),
+            pltpu.VMEM(a.shape, F32),
+            pltpu.VMEM(shape, F32),
+            pltpu.VMEM((2 * n - 1,) + shape, F32),
+            dma,
+            dma((n,)),
+            dma((n,)),
+            dma((2 * n - 1,)),
+            dma((2 * n - 1,)),
+            dma,
+        ],
+        compiler_params=pltpu.CompilerParams(collective_id=cid, has_side_effects=True),
+        cost_estimate=cost(12, 0),
+        name="total",
+    )(a)
+
+
+def assemble_kernel(wide, in_ref, out_ref):
+    for k in range(2):
+        out_ref[:, k * wide : (k + 1) * wide] = in_ref[k, 0, 0, 0].astype(F32)
+
+
+def assemble(n, whole, parts, wide):
+    sub = whole.shape[4]
+    apart = whole.shape[3] == parts
+    at = (lambda z, j, p: (0, z, j, p, 0, 0)) if apart else (lambda z, j, p: (0, z, j, 0, 0, p))
+    return pl.pallas_call(
+        functools.partial(assemble_kernel, wide),
+        grid=(n, n, parts),
+        out_shape=jax.ShapeDtypeStruct((n * sub, parts * n * 2 * wide), F32),
+        in_specs=[pl.BlockSpec((2, 1, 1, 1, sub, wide), at)],
+        out_specs=pl.BlockSpec((sub, 2 * wide), lambda z, j, p: (z, p * n + j)),
+        cost_estimate=cost(12, 0),
+        name="assemble",
+    )(whole)
+
+
+def split_columns_kernel(units, w_ref, o_ref):
+    core = lax.axis_index("core")
+    for k in range(2):
+
+        @pl.when(core == k)
+        def _():
+            o_ref[0, 0] = w_ref[:, k * units : (k + 1) * units]
+
+
+def split_columns(n, w):
+    rows = w.shape[0]
+    units = w.shape[1] // (4 * n)
+    if (2 * units) % 128:
+        mine = w.reshape(rows, 2, n, 2, units)
+        return lax.dynamic_index_in_dim(mine, lax.axis_index("core"), 3, keepdims=False).transpose(2, 1, 0, 3)
+    return pl.pallas_call(
+        functools.partial(split_columns_kernel, units),
+        grid=(n, 2),
+        out_shape=jax.ShapeDtypeStruct((n, 2, rows, units), w.dtype),
+        in_specs=[pl.BlockSpec((rows, 2 * units), lambda j, p: (0, p * n + j))],
+        out_specs=pl.BlockSpec((1, 1, rows, units), lambda j, p: (j, p, 0, 0)),
+        cost_estimate=cost(8, 0),
+        name="split_columns",
+    )(w)
 
 
 def local(
@@ -298,7 +993,8 @@
 ):
     n = groups
     blk = inputs.shape[2]
-    toks = inputs.shape[1] * blk
+    slots = inputs.shape[1]
+    toks = slots * blk
     width = inputs.shape[3]
     rows = w_qkv.shape[0]
     me, plane, core = (lax.axis_index(a) for a in EVERY)
@@ -306,83 +1002,90 @@
     units = w_down.shape[0] // 2
     swap_pairs = [(s * n + z, z * n + s) for s in range(n) for z in range(n)]
     swap = lambda a: lax.ppermute(a, ("dp", "pl"), swap_pairs)
-    gather = lambda a: lax.all_gather(a, PLANE, axis=0, tiled=True)
-    scatter = lambda a: lax.psum_scatter(a.astype(BF16), PLANE, scatter_dimension=0, tiled=True).astype(F32)
     pick = lambda a, axis, at: lax.dynamic_index_in_dim(a, at, axis, keepdims=False)
 
-    def columns(w, parts, wide):
-        mine = pick(w.reshape(rows, parts, n, 2, wide), 3, core)
-        mine = mine.transpose(2, 0, 1, 3).reshape(n * rows, parts * wide)
-        return lax.all_to_all(mine, "dp", 0, 0, tiled=True)
-
-    token_rows = swap(inputs.reshape(toks, width)).astype(F32)
-    cot = swap(cotangent.reshape(toks, width))
-    wq = columns(w_qkv, 3, hw)
-    small = jnp.concatenate([first_gain, first_shift, second_gain, second_shift, qkv_bias])
-    small = lax.all_gather(small, "dp", axis=0, tiled=False)
+    def rows_first(g):
+        return lax.psum_scatter(g.astype(BF16), "pl", scatter_dimension=0, tiled=True)
+
+    def last(part):
+        return lax.all_gather(part, ("core", "pl"), axis=0, tiled=True).astype(F32)
+
+    def columns_first(g):
+        parts, _, wide = g.shape
+        g = g.reshape(parts, n, n, rows // n, wide).transpose(2, 1, 0, 3, 4)
+        part = lax.psum_scatter(g, "pl", scatter_dimension=0, tiled=True)
+        part = part.reshape(n, parts * rows // n, wide)
+        return lax.all_to_all(part, "dp", 0, 0, tiled=True)
+
+    def columns_last(part, parts, wide):
+        whole = lax.all_gather(part, ("core", "pl"), axis=0, tiled=True)
+        whole = whole.reshape(2, n, n, -1, rows // n, part.shape[2])
+        if (2 * wide) % 128 == 0:
+            return assemble(n, whole, parts, wide)
+        whole = whole.reshape(2, n, n, whole.shape[3], rows // n, -1, wide).transpose(1, 4, 3, 5, 2, 0, 6)
+        return whole.reshape(rows, parts * n * 2 * wide).astype(F32)
+
+    small = jnp.concatenate([first_gain, first_shift, second_gain, second_shift, qkv_bias]).reshape(-1, 128)
+    ids = jnp.zeros((8, 128), jnp.int32).at[0, :slots].set(block_of.reshape(-1))
+    x, wq, small, ids = start(n, 0, inputs.reshape(toks, width), w_qkv, small, ids)
+    x, w_gateup, cotangent, w_out, w_down = lax.optimization_barrier((x, w_gateup, cotangent, w_out, w_down))
+    token_rows = x.astype(F32)
+    small = small.reshape(n, -1)
     gain_one, shift_one, gain_two, shift_two = (
         small[:, k * rows : (k + 1) * rows].reshape(width) for k in range(4)
     )
     bias = small[:, 4 * rows :].reshape(3, n, 2, hw)
     bias = pick(pick(bias, 1, me), 1, core).reshape(1, 3 * hw)
-    blocks = lax.all_gather(block_of.reshape(-1), EVERY, axis=0, tiled=True)
-    blocks = pick(blocks.reshape(n, -1), 0, plane)
+    blocks = ids[:, 0, :slots].reshape(-1)
     order = jnp.arange(blocks.shape[0], dtype=jnp.int32)
     slot_of = jnp.sum(jnp.where(blocks[None, :] == order[:, None], order[None, :], 0), axis=1)
-    wgu = columns(w_gateup, 2, units)
+
+    mine = split_columns(n, w_gateup)
+    wgu = jnp.zeros((2, n, rows, units), BF16)
+    wgu = lax.dynamic_update_index_in_dim(wgu, pick(mine, 0, me), me, 1)
+    for j in range(1, n):
+        got = lax.ppermute(pick(mine, 0, (me + j) % n), "dp", [(i, (i + j) % n) for i in range(n)])
+        wgu = lax.dynamic_update_index_in_dim(wgu, got, (me + n - j) % n, 1)
+    wgu = wgu.reshape(2, n * rows, units)
     wo = pick(w_out.reshape(2, hw, width), 0, core)
     wd = pick(w_down.reshape(2, units, width), 0, core)
+    cot = swap(cotangent.reshape(toks, width))
     tables = rotary_tables(blocks.shape[0] * blk)
 
     normed_out, normed_one, inverse_one = layer_norm(token_rows, gain_one, shift_one)
-    hidden_one = gather(normed_out.astype(BF16))
-    proj = nn(hidden_one, wq)
+    hidden_one, proj = gather_dot(n, 1, normed_out.astype(BF16), wq, False, F32)
+    proj, cot = lax.optimization_barrier((proj, cot))
+    cot_all = lax.all_gather(cot, PLANE, axis=0, tiled=True)
     qs, ks, vs, att, lse = attend(slot_of, proj, bias, tables, blk)
-    middle = token_rows + scatter(nn(att, wo))
+    middle = token_rows + dot_scatter(n, 2, [(att, wo)], False)
     normed_out_two, normed_two, inverse_two = layer_norm(middle, gain_two, shift_two)
-    hidden_two = gather(normed_out_two.astype(BF16))
-    cot_all = gather(cot)
-    gate_up = nn(hidden_two, wgu)
-    gate, upper = gate_up[:, :units], gate_up[:, units:]
-    sig = jax.nn.sigmoid(gate)
-    act = (gate * sig * upper).astype(BF16)
-    grad_act = nt(cot_all, wd)
-    grad_gate = grad_act * upper * sig * (1.0 + gate * (1.0 - sig))
-    grad_up = grad_act * gate * sig
-    grad_gu = jnp.concatenate([grad_gate, grad_up], axis=1).astype(BF16)
-    grad_hidden_two = scatter(nt(grad_gu, wgu))
-    outputs = (middle + scatter(nn(act, wd))).astype(BF16)
-    outputs = swap(outputs)
+    hidden_two, act, grad_gate, grad_up = gather_mlp(n, 3, normed_out_two.astype(BF16), wgu, cot_all, wd)
+    grad_down = tn(act, cot_all).astype(BF16)
+    grad_gateup = jnp.stack([tn(hidden_two, grad_gate), tn(hidden_two, grad_up)]).astype(BF16)
+    grad_gate, grad_up, grad_down, grad_gateup = lax.optimization_barrier((grad_gate, grad_up, grad_down, grad_gateup))
+    down_part = rows_first(grad_down)
+    gateup_part = columns_first(grad_gateup)
+    grad_hidden_two = dot_scatter(n, 4, [(grad_gate, wgu[0]), (grad_up, wgu[1])], True)
     gain_two_term = jnp.sum(grad_hidden_two * normed_two, axis=0)
     shift_two_term = jnp.sum(grad_hidden_two, axis=0)
     grad_middle = cot.astype(F32) + norm_back(grad_hidden_two, normed_two, inverse_two, gain_two)
-    grad_middle_all = gather(grad_middle.astype(BF16))
-    grad_att = nt(grad_middle_all, wo).astype(BF16)
+    grad_middle_all, grad_att = gather_dot(n, 5, grad_middle.astype(BF16), wo, True, BF16)
     gq, gk, gv, bias_terms = attend_back(slot_of, qs, ks, vs, att, grad_att, lse, tables, blk)
     grad_proj = jnp.concatenate([gq, gk, gv], axis=1)
-    grad_hidden_one = scatter(nt(grad_proj, wq))
+    grad_proj, gateup_part, down_part = lax.optimization_barrier((grad_proj, gateup_part, down_part))
+    grad_hidden_one = dot_scatter(n, 6, [(grad_proj, wq)], True)
     gain_one_term = jnp.sum(grad_hidden_one * normed_one, axis=0)
     shift_one_term = jnp.sum(grad_hidden_one, axis=0)
     grad_inputs = grad_middle + norm_back(grad_hidden_one, normed_one, inverse_one, gain_one)
-    grad_inputs = swap(grad_inputs.astype(BF16)).astype(F32)
-
-    def by_rows(g):
-        part = lax.psum_scatter(g.astype(BF16), "pl", scatter_dimension=0, tiled=True)
-        return lax.all_gather(part, ("core", "pl"), axis=0, tiled=True).astype(F32)
-
-    def by_columns(g, parts, wide):
-        sub = rows // n
-        g = g.astype(BF16).reshape(n, n, sub, parts * wide).transpose(1, 0, 2, 3).reshape(n * rows, parts * wide)
-        part = lax.psum_scatter(g, "pl", scatter_dimension=0, tiled=True)
-        part = lax.all_to_all(part, "dp", 0, 0, tiled=True)
-        whole = lax.all_gather(part, ("core", "pl"), axis=0, tiled=True)
-        whole = whole.reshape(2, n, n, sub, parts, wide).transpose(1, 3, 4, 2, 0, 5)
-        return whole.reshape(rows, parts * n * 2 * wide).astype(F32)
-
-    grad_down = by_rows(tn(act, cot_all))
-    grad_gateup = by_columns(tn(hidden_two, grad_gu), 2, units)
-    grad_out = by_rows(tn(att, grad_middle_all))
-    grad_qkv = by_columns(tn(hidden_one, grad_proj), 3, hw)
+    grad_inputs = grad_inputs.astype(BF16)
+    grad_inputs, act = lax.optimization_barrier((grad_inputs, act))
+    outputs = swap((middle + dot_scatter(n, 8, [(act, wd)], False)).astype(BF16))
+    grad_inputs = swap(grad_inputs).astype(F32)
+
+    grad_down = last(down_part)
+    grad_gateup = columns_last(gateup_part, 2, units)
+    grad_out = last(rows_first(tn(att, grad_middle_all)))
+    grad_qkv = columns_last(columns_first(tn(hidden_one, grad_proj).astype(BF16)[None]), 3, hw)
     bias_term = bias_terms[:3].reshape(3, 1, hw)
     at = me * 2 + core
     spots = (jnp.arange(2 * n, dtype=jnp.int32) == at)[None, :, None]
@@ -391,7 +1094,7 @@
         [a.reshape(n, rows) for a in (gain_one_term, shift_one_term, gain_two_term, shift_two_term)] + [bias_term],
         axis=1,
     )
-    tiny = pick(lax.psum(tiny, EVERY), 0, me)
+    tiny = total(n, 7, tiny.reshape(n, -1, 128)).reshape(-1)
     terms = [tiny[k * rows : (k + 1) * rows] for k in range(4)]
     return (
         outputs.reshape(inputs.shape),

time: 1610 us -> 1200 us (0.75)
  Pallas kernels: 91.9 us -> 860 us
  waiting for transfers between devices: 692 us -> 113 us
  blocking collectives: 350 us -> 15.5 us
  local copies, waits for them, and re-layouts: 212 us -> 87.5 us
  matrix products: 146 us -> 41.7 us
  starting transfers between devices: 58.1 us -> 12 us
    pallas_call x0 -> x12, Pallas kernels: none -> 769 us  [the longest x1 221 us: total(): pl.pallas_call(functools.partial(total_kernel, n), out_shape=jax.ShapeDty...]
    reduce_scatter x8 -> x4, waiting for transfers between devices: 399 us -> 96 us  [the longest x2 96 us: columns_first(): part = lax.psum_scatter(g, 'pl', scatter_dimension=0, tiled=True)]
    all_gather x8 -> x5, waiting for transfers between devices: 292 us -> 14.2 us  [the longest x2 14.2 us: last(): return lax.all_gather(part, ('core', 'pl'), axis=0, tiled=True).astype(F32)]
    all_to_all x3 -> x1, blocking collectives: 201 us -> 15.5 us  [columns_first(): return lax.all_to_all(part, 'dp', 0, 0, tiled=True)]
    dot_general x8 -> x0, matrix products: 101 us -> none  [the longest x4 52 us: nt(): lax.dot_general(a, b, (((1,), (1,)), ((), ())), preferred_element_type=F32)]
    unnamed x60 -> x69, local copies, waits for them, and re-layouts: 102 us -> 7.87 us
    unnamed x1 -> x0, blocking collectives: 79.8 us -> none
    convert_element_type x4 -> x0, local copies, waits for them, and re-layouts: 77.7 us -> none  [by_columns(): return whole.reshape(rows, parts * n * 2 * wide).astype(F32)]
  transfers between devices with their start and end apart: 21 -> 16, of which waited for: 10 -> 3; matrix products, arithmetic and copies ran while one was open for 18% -> 9% of each run, Pallas kernels for 3% -> 59%
where the time goes in v2:
time: 1200 us; the launch traced here: 1190 us
  Pallas kernels  860 us (72%)
  waiting for transfers between devices  113 us (9%)
  local copies, waits for them, and re-layouts  87.5 us (7%)
  other arithmetic  50.3 us (4%)
  matrix products  41.7 us (3%)
  blocking collectives  15.5 us (1%)
  between operations  14.7 us (1%)
  starting transfers between devices  12 us (1%)
    pallas_call x1, Pallas kernels, total(): pl.pallas_call(functools.partial(total_kernel, n), out_shape=jax.ShapeDty...  221 us
    pallas_call x4, Pallas kernels, dot_scatter(): pl.pallas_call(functools.partial(dot_scatter_kernel, n, count, trans), ou...  210 us
    pallas_call x2, Pallas kernels, gather_dot(): pl.pallas_call(functools.partial(gather_dot_kernel, n, trans), out_shape=...  142 us
    reduce_scatter x2, waiting for transfers between devices, columns_first(): part = lax.psum_scatter(g, 'pl', scatter_dimension=0, tiled=True)  96 us
    pallas_call x1, Pallas kernels, start(): pl.pallas_call(functools.partial(start_kernel, n), out_shape=(jax.ShapeDt...  86.1 us
    pallas_call x2, Pallas kernels, assemble(): pl.pallas_call(functools.partial(assemble_kernel, wide), grid=(n, n, part...  51.1 us
    pallas_call x1, Pallas kernels, attend_back(): pl.pallas_call(functools.partial(attend_back_kernel, blk, tile), out_shap...  50.4 us
    pallas_call x1, Pallas kernels, gather_mlp(): pl.pallas_call(functools.partial(gather_mlp_kernel, n), out_shape=(jax.Sh...  49.1 us
  transfers between devices with their start and end apart: 16, of which 3 were waited for; matrix products, arithmetic and copies ran while one was open for 9% of the time, Pallas kernels for 59%

profile of v2, /device:TPU:0, one launch (start us, length us, event | category | flops | bytes accessed | tf_op | source)
XLA Modules:
  0.0 1194.9 jit_solution(10471231120553314316)
XLA Ops:
  11.9 86.1 %start.1 = (bf16[256,2048]{1,0:T(8,128)(2,1)}, bf16[2048,768]{1,0:T(8,128)(2,1)}, f32[4,28,128]{2,1,0:T(8,128)}, s32[8,8,128]{2,1,0:T(8,128)}) custom-call(bf16[256,2048]{1,0:T(8,128)(2,1)} %bitcast.119, bf16[512,6144]{1,0:T(8,128)(2,1)} %w_ref.1, f32[28,128]{1,0:T(8,128)} %bitcast.139, s32[8,128]{1,0:T(8,128)} %scatter.4.block_ref), custom_call_target="tpu_custom_call" | custom-call | bytes 255000000 | tf_op jit(solution)/shard_map/start/pallas_call | solution.py:832
  98.0 2.0 collective-permute-start
  105.5 86.4 %gather_dot.2 = (bf16[8,256,2048]{2,1,0:T(8,128)(2,1)}, f32[8,256,768]{2,1,0:T(8,128)}) custom-call(bf16[256,2048]{1,0:T(8,128)(2,1)} %fusion.9.x_ref, bf16[2048,768]{1,0:T(8,128)(2,1)} %get-tuple-element.64.w_ref.refs_1_), custom_call_target="tpu_custom_call" | custom-call | flops 6442450944 | bytes 142800000 | tf_op jit(solution)/shard_map/gather_dot/pallas_call | solution.py:467
  193.0 9.4 split_columns.1
  202.4 4.3 constant_dynamic-slice_fusion
  206.8 2.5 copy.51
  209.3 2.5 copy.53
  211.8 2.0 collective-permute-start.2
  219.4 2.1 bitcast_dynamic-update-slice_fusion
  223.4 2.0 dynamic-slice_bitcast_fusion.d_ref.refs_1_
  225.4 5.0 fusion.18
  230.4 41.4 %attend.1 = (bf16[2048,256]{1,0:T(8,128)(2,1)}, bf16[2048,256]{1,0:T(8,128)(2,1)}, bf16[2048,256]{1,0:T(8,128)(2,1)}, bf16[2048,256]{1,0:T(8,128)(2,1)}, f32[2048,256]{1,0:T(8,128)}) custom-call(s32[16]{0:T(128)} %select_reduce_fusion.slot_ref, f32[2048,768]{1,0:T(8,128)} %bitcast.99, f32[2048,768]{1,0:T(8,128)} %bitcast.100, f32[2048,768]{1,0:T(8,128)} %bitcast.101, ...), custom_call_target="tpu_custom_call" | custom-call | bytes 139400000 | tf_op jit(solution)/shard_map/attend/pallas_call | solution.py:154
  271.8 65.1 %dot_scatter.4 = f32[256,2048]{1,0:T(8,128)} custom-call(bf16[8,256,256]{2,1,0:T(8,128)(2,1)} %bitcast.107, bf16[256,2048]{1,0:T(8,128)(2,1)} %dynamic-slice_bitcast_fusion.1.refs_1_.w_ref), custom_call_target="tpu_custom_call" | custom-call | flops 2147483648 | bytes 153000000 | tf_op jit(solution)/shard_map/dot_scatter/pallas_call | solution.py:696
  342.3 2.6 copy.54
  344.9 2.6 copy.56
  352.6 49.1 %gather_mlp.1 = (bf16[8,256,2048]{2,1,0:T(8,128)(2,1)}, bf16[8,256,704]{2,1,0:T(8,128)(2,1)}, bf16[8,256,704]{2,1,0:T(8,128)(2,1)}, bf16[8,256,704]{2,1,0:T(8,128)(2,1)}) custom-call(bf16[256,2048]{1,0:T(8,128)(2,1)} %add_convert_fusion.1.x_ref, bf16[2,2048,704]{2,1,0:T(8,128)(2,1)} %bitcast.103, bf16[8,256,2048]{2,1,0:T(8,128)(2,1)} %bitcast.140, ...), custom_call_target="tpu_custom_call" | custom-call | flops 17716740096 | bytes 163200000 | tf_op jit(solution)/shard_map/gather_mlp/pallas_call | solution.py:544
  401.8 9.9 fusion.1
  411.7 6.7 fusion
  418.5 3.0 pad_maximum_fusion
  421.5 7.7 convolution_convert_fusion.1
  429.2 10.3 reshape.269
  439.5 6.7 copy.73
  446.9 6.4 fusion.25
  453.3 50.6 %dot_scatter.5 = f32[256,2048]{1,0:T(8,128)} custom-call(bf16[8,256,704]{2,1,0:T(8,128)(2,1)} %get-tuple-element.73, bf16[8,256,704]{2,1,0:T(8,128)(2,1)} %get-tuple-element.74, bf16[2048,704]{1,0:T(8,128)(2,1)} %bitcast.112, bf16[2048,704]{1,0:T(8,128)(2,1)} %bitcast.111), custom_call_target="tpu_custom_call" | custom-call | flops 11811160064 | bytes 153000000 | tf_op jit(solution)/shard_map/dot_scatter/pallas_call | solution.py:696
  503.9 3.3 multiply_reduce_fusion
  507.5 3.8 fusion.23
  511.3 36.8 %reduce-scatter.5.cloned.1.call-done = bf16[1,4,2,128,704]{3,4,2,1,0:T(8,128)(2,1)} async-done(((bf16[4,4,2,128,704]{3,4,2,1,0:T(8,128)(2,1)}), bf16[1,4,2,128,704]{3,4,2,1,0:T(8,128)(2,1)}) %reduce-scatter.5.cloned.1.call-update) | async-done | bytes 1441808 | tf_op jit(solution)/shard_map/reduce_scatter | solution.py:1016
  548.0 2.8 copy.60
  552.7 3.7 all-to-all-start
  556.4 55.5 %gather_dot.3 = (bf16[8,256,2048]{2,1,0:T(8,128)(2,1)}, bf16[8,256,256]{2,1,0:T(8,128)(2,1)}) custom-call(bf16[256,2048]{1,0:T(8,128)(2,1)} %get-tuple-element.105.x_ref, bf16[256,2048]{1,0:T(8,128)(2,1)} %dynamic-slice_bitcast_fusion.1.refs_1_.w_ref), custom_call_target="tpu_custom_call" | custom-call | flops 2147483648 | bytes 142800000 | tf_op jit(solution)/shard_map/gather_dot/pallas_call | solution.py:467
  611.9 6.7 convolution_convert_fusion.2
  618.7 50.4 %attend_back.1 = (bf16[2048,256]{1,0:T(8,128)(2,1)}, bf16[2048,256]{1,0:T(8,128)(2,1)}, bf16[2048,256]{1,0:T(8,128)(2,1)}, f32[8,256]{1,0:T(8,128)}) custom-call(s32[16]{0:T(128)} %select_reduce_fusion.slot_ref, bf16[2048,256]{1,0:T(8,128)(2,1)} %get-tuple-element.79.qs, bf16[2048,256]{1,0:T(8,128)(2,1)} %get-tuple-element.80.ks, ...), custom_call_target="tpu_custom_call" | custom-call | bytes 170000000 | tf_op jit(solution)/shard_map/attend_back/pallas_call | solution.py:264
  669.1 3.1 pad_maximum_fusion.1
  672.3 10.7 convolution_convert_fusion
  686.4 59.2 %reduce-scatter.9.cloned.1.call-done = bf16[1,4,1,128,768]{4,3,1,2,0:T(8,128)(2,1)} async-done(((bf16[4,4,1,128,768]{4,3,1,2,0:T(8,128)(2,1)}), bf16[1,4,1,128,768]{4,3,1,2,0:T(8,128)(2,1)}) %reduce-scatter.9.cloned.1.call-update) | async-done | bytes 786448 | tf_op jit(solution)/shard_map/reduce_scatter | solution.py:1016
  745.6 15.5 %all_to_all.10 = bf16[4,128,768]{2,1,0:T(8,128)(2,1)} all-to-all(bf16[4,128,768]{2,1,0:T(8,128)(2,1)} %bitcast.123), channel_id=1, replica_groups=mesh['dp'=4,'pl'=4,'core'=2] {'dp'}, dimensions={0} | all-to-all | bytes 1572864 | tf_op jit(solution)/shard_map/all_to_all | solution.py:1018
  762.0 14.2 %all-gather.10.cloned.1.call-done = bf16[512,2048]{1,0:T(8,128)(2,1)} async-done(((bf16[64,2048]{1,0:T(8,128)(2,1)}), bf16[512,2048]{1,0:T(8,128)(2,1)}) %all-gather.10.cloned.1.call-update) | async-done | bytes 2097168 | tf_op jit(solution)/shard_map/all_gather | solution.py:1011
  776.1 4.1 convert_element_type.66
  780.3 47.7 %dot_scatter.6 = f32[256,2048]{1,0:T(8,128)} custom-call(bf16[8,256,768]{2,1,0:T(8,128)(2,1)} %bitcast.109, bf16[2048,768]{1,0:T(8,128)(2,1)} %get-tuple-element.64.w_ref.refs_1_), custom_call_target="tpu_custom_call" | custom-call | flops 6442450944 | bytes 153000000 | tf_op jit(solution)/shard_map/dot_scatter/pallas_call | solution.py:696
  828.0 2.7 fusion.15
  830.7 3.4 fusion.14
  834.1 46.3 %dot_scatter.7 = f32[256,2048]{1,0:T(8,128)} custom-call(bf16[8,256,704]{2,1,0:T(8,128)(2,1)} %get-tuple-element.75, bf16[704,2048]{1,0:T(8,128)(2,1)} %dynamic-slice_bitcast_fusion.d_ref.refs_1_), custom_call_target="tpu_custom_call" | custom-call | flops 5905580032 | bytes 153000000 | tf_op jit(solution)/shard_map/dot_scatter/pallas_call | solution.py:696
  880.4 2.6 add_convert_fusion
  886.4 221.2 %total.1 = f32[28,128]{1,0:T(8,128)} custom-call(f32[4,28,128]{2,1,0:T(8,128)} %reshape.280.a_ref), custom_call_target="tpu_custom_call" | custom-call | bytes 40800000 | tf_op jit(solution)/shard_map/total/pallas_call | solution.py:910
  1111.9 8.8 convert_element_type.67
  1120.6 27.4 %assemble.2 = f32[512,6144]{1,0:T(8,128)} custom-call(bf16[2,4,4,1,128,768]{5,4,3,2,1,0:T(8,128)(2,1)} %bitcast.108), custom_call_target="tpu_custom_call" | custom-call | bytes 40800000 | tf_op jit(solution)/shard_map/assemble/pallas_call | solution.py:942
  1148.0 15.5 %copy.62 = bf16[32,256,704]{2,1,0:T(8,128)(2,1)} copy(bf16[32,256,704]{1,2,0:T(8,128)(2,1)} %all-gather.12.cloned.1.call-done) | data formatting | bytes 23068672 | tf_op jit(solution)/shard_map/all_gather | solution.py:1021
  1163.5 23.7 %assemble.3 = f32[512,11264]{1,0:T(8,128)} custom-call(bf16[2,4,4,2,128,704]{5,4,3,2,1,0:T(8,128)(2,1)} %bitcast.102), custom_call_target="tpu_custom_call" | custom-call | bytes 40800000 | tf_op jit(solution)/shard_map/assemble/pallas_call | solution.py:942
  (154 shorter events, 44.8 us)
Async XLA Ops:
  7.2 345.5 %all-gather.6.cloned.1.call-start = ((), (), s32[]{:S(2)}) async-start(), calls=%async_computation.6 | async-start | bytes 9437184 | tf_op jit(solution)/shard_map/all_gather | solution.py:1058
  10.7 1.3 copy-start.16
  98.0 6.1 copy-start.2
  98.0 93.9 %collective-permute-start = (bf16[256,2048]{1,0:T(8,128)(2,1)}, bf16[256,2048]{1,0:T(8,128)(2,1)S(1)}, u32[]{:S(2)}, u32[]{:S(2)}) collective-permute-start(bf16[256,2048]{1,0:T(8,128)(2,1)} %bitcast.3), channel_id=1, source_target_pairs={{0,0},{2,8},{4,16},{6,24},{8,2},{10,10},{12,18},{14,26},{16,4},{18... | collective-permute-start | bytes 3145736 | tf_op jit(solution)/shard_map/ppermute | solution.py:1004
  100.9 4.6 copy-start.12
  102.4 89.5 %copy-start.14 = (f32[256]{0:T(256)}, f32[256]{0:T(256)S(1)}, u32[]{:S(2)}) copy-start(f32[256]{0:T(256)S(1)} %broadcast_multiply_fusion.5) | copy-start | bytes 3076
  104.1 87.8 %copy-start.17 = (f32[256]{0:T(256)}, f32[256]{0:T(256)S(1)}, u32[]{:S(2)}) copy-start(f32[256]{0:T(256)S(1)} %add_rsqrt_fusion.1) | copy-start | bytes 3076
  191.9 1.0 copy-start.10
  192.9 355.1 %reduce-scatter.5.cloned.1.call-start = ((), (), s32[]{:S(2)}) async-start(), calls=%async_computation.7 | async-start | bytes 7208960 | tf_op jit(solution)/shard_map/reduce_scatter | solution.py:1016
  209.3 131.3 %collective-permute-start.1 = (bf16[2,512,704]{1,2,0:T(8,128)(2,1)}, bf16[2,512,704]{1,2,0:T(8,128)(2,1)}, u32[]{:S(2)}, u32[]{:S(2)}) collective-permute-start(bf16[2,512,704]{1,2,0:T(8,128)(2,1)} %bitcast.116), channel_id=1, source_target_pairs={{0,8},{8,16},{16,24},{24,0},{1,9},{9,17},{17,25},{25,1},{2,10},{10... | collective-permute-start | bytes 4325384 | tf_op jit(solution)/shard_map/ppermute | solution.py:1047
  211.8 130.5 %collective-permute-start.2 = (bf16[2,512,704]{1,2,0:T(8,128)(2,1)}, bf16[2,512,704]{1,2,0:T(8,128)(2,1)}, u32[]{:S(2)}, u32[]{:S(2)}) collective-permute-start(bf16[2,512,704]{1,2,0:T(8,128)(2,1)} %bitcast.117), channel_id=1, source_target_pairs={{0,16},{8,24},{16,0},{24,8},{1,17},{9,25},{17,1},{25,9},{2,18},{10... | collective-permute-start | bytes 4325384 | tf_op jit(solution)/shard_map/ppermute | solution.py:1047
  215.4 129.5 %collective-permute-start.3 = (bf16[2,512,704]{1,2,0:T(8,128)(2,1)}, bf16[2,512,704]{1,2,0:T(8,128)(2,1)}, u32[]{:S(2)}, u32[]{:S(2)}) collective-permute-start(bf16[2,512,704]{1,2,0:T(8,128)(2,1)} %bitcast.118), channel_id=1, source_target_pairs={{0,24},{8,0},{16,8},{24,16},{1,25},{9,1},{17,9},{25,17},{2,26},{10... | collective-permute-start | bytes 4325384 | tf_op jit(solution)/shard_map/ppermute | solution.py:1047
  218.3 5.1 slice-start
  218.9 4.5 slice-start.1
  219.4 2.6 copy-start.11
  221.5 3.9 copy-start.3
  338.8 1.9 copy-start
  347.4 2.0 copy-start.7
  349.4 2.0 copy-start.8
  401.8 9.9 copy-start.21
  401.8 9.9 copy-start.22
  401.8 19.7 %slice-start.2 = ((s8[8388608]{0:T(1024)(128)(4,1)}), s8[4194304]{0:T(1024)(128)(4,1)S(1)}, s32[]{:S(2)}) async-start(s8[8388608]{0:T(1024)(128)(4,1)} %bitcast.141), calls=%async_computation.17 | async-start | bytes 8388608
  411.7 9.8 slice-start.3
  418.5 3.0 copy-start.20
  446.1 226.1 %reduce-scatter.7.cloned.1.call-start = ((), (), s32[]{:S(2)}) async-start(), calls=%async_computation.8 | async-start | bytes 3604480 | tf_op jit(solution)/shard_map/reduce_scatter | solution.py:1008
  503.9 3.3 copy-start.1
  503.9 3.5 copy-start.4
  552.7 119.6 %all-to-all-start = ((bf16[4,256,704]{1,2,0:T(8,128)(2,1)}), bf16[4,256,704]{1,2,0:T(8,128)(2,1)S(1)}, u32[]{:S(2)}, u32[]{:S(2)}) async-start(bf16[4,256,704]{1,2,0:T(8,128)(2,1)} %reshape.270), calls=%async_computation.1 | async-start | bytes 2883584 | tf_op jit(solution)/shard_map/all_to_all | solution.py:1018
  556.4 128.7 %reduce-scatter.11.cloned.1.call-start = ((), (), s32[]{:S(2)}) async-start(), calls=%async_computation.11 | async-start | bytes 1310720 | tf_op jit(solution)/shard_map/reduce_scatter | solution.py:1008
  556.4 55.5 %copy-start.6 = (bf16[2048,256]{1,0:T(8,128)(2,1)S(1)}, bf16[2048,256]{1,0:T(8,128)(2,1)}, u32[]{:S(2)}) copy-start(bf16[2048,256]{1,0:T(8,128)(2,1)} %get-tuple-element.68.att) | copy-start | bytes 3145732
  618.6 126.9 %reduce-scatter.9.cloned.1.call-start = ((), (), s32[]{:S(2)}) async-start(), calls=%async_computation.9 | async-start | bytes 3932160 | tf_op jit(solution)/shard_map/reduce_scatter | solution.py:1016
  672.3 10.8 copy-start.9
  685.0 91.2 %all-gather.10.cloned.1.call-start = ((), (), s32[]{:S(2)}) async-start(), calls=%async_computation.12 | async-start | bytes 2359296 | tf_op jit(solution)/shard_map/all_gather | solution.py:1011
  685.5 426.3 %all-gather.14.cloned.1.call-start = ((), (), s32[]{:S(2)}) async-start(), calls=%async_computation.14 | async-start | bytes 6488064 | tf_op jit(solution)/shard_map/all_gather | solution.py:1011
  686.3 75.6 %copy-start.19 = (f32[8,256]{1,0:T(8,128)S(1)}, f32[8,256]{1,0:T(8,128)}, u32[]{:S(2)}) copy-start(f32[8,256]{1,0:T(8,128)} %get-tuple-element.92) | copy-start | bytes 24580
  686.3 434.3 %all-gather.8.cloned.1.call-start = ((), (), s32[]{:S(2)}) async-start(), calls=%async_computation.10 | async-start | bytes 7077888 | tf_op jit(solution)/shard_map/all_gather | solution.py:1021
  761.1 387.0 %all-gather.12.cloned.1.call-start = ((), (), s32[]{:S(2)}) async-start(), calls=%async_computation.13 | async-start | bytes 12976128 | tf_op jit(solution)/shard_map/all_gather | solution.py:1021
  780.3 47.7 %copy-start.13 = (f32[1,4,4,128]{3,1,2,0:T(4,128)S(1)}, f32[1,4,4,128]{3,1,2,0:T(4,128)}, u32[]{:S(2)}) copy-start(f32[1,4,4,128]{3,1,2,0:T(4,128)} %copy-done.12) | copy-start | bytes 24580
  780.3 47.7 %copy-start.15 = (f32[256]{0:T(256)S(1)}, f32[256]{0:T(256)}, u32[]{:S(2)}) copy-start(f32[256]{0:T(256)} %copy-done.14) | copy-start | bytes 3076
  780.3 47.7 %copy-start.18 = (f32[256]{0:T(256)S(1)}, f32[256]{0:T(256)}, u32[]{:S(2)}) copy-start(f32[256]{0:T(256)} %copy-done.17) | copy-start | bytes 3076
  828.0 2.7 copy-start.5
  883.0 227.3 %collective-permute-start.4 = (bf16[256,2048]{1,0:T(8,128)(2,1)S(1)}, bf16[256,2048]{1,0:T(8,128)(2,1)S(1)}, u32[]{:S(2)}, u32[]{:S(2)}) collective-permute-start(bf16[256,2048]{1,0:T(8,128)(2,1)S(1)} %add_convert_fusion), channel_id=1, source_target_pairs={{0,0},{2,8},{4,16},{6,24},{8,2},{10,10},{12,18},{14,26},{16,4},{18... | collective-permute-start | bytes 3145736 | tf_op jit(solution)/shard_map/ppermute | solution.py:1004
  883.8 226.5 %collective-permute-start.5 = (bf16[256,2048]{1,0:T(8,128)(2,1)}, bf16[256,2048]{1,0:T(8,128)(2,1)S(1)}, u32[]{:S(2)}, u32[]{:S(2)}) collective-permute-start(bf16[256,2048]{1,0:T(8,128)(2,1)} %fusion.14), channel_id=1, source_target_pairs={{0,0},{2,8},{4,16},{6,24},{8,2},{10,10},{12,18},{14,26},{16,4},{18... | collective-permute-start | bytes 3145736 | tf_op jit(solution)/shard_map/ppermute | solution.py:1004
Sparse Core Ops, SparseCore 0:
  193.1 108.2 all-gather.5
  446.3 101.7 reduce-scatter.4
  550.3 56.8 reduce-scatter.6
  618.8 27.3 reduce-scatter.10
  685.1 60.4 reduce-scatter.8
  747.0 29.0 all-gather.9
  777.7 59.7 all-gather.13
  839.1 157.4 all-gather.7
  998.2 132.1 all-gather.11

commit v3 on v2

--- a/solution.py
+++ b/solution.py
@@ -324,79 +324,80 @@
     return width
 
 
-def gather_blocks(n, x_ref, buf, s_in, s_ring, r_ring, s_part, r_part, ready, use):
-    dp, core, at = plane_ids(n)
-    rows = x_ref.shape[0]
-    half = rows // 2
-    mid = n // 2
-    slot = lambda off, flip: 2 * at(off) + (core if flip == 0 else 1 - core)
-    right, left, mate = {"dp": at(1)}, {"dp": at(-1)}, {"core": 1 - core}
-    load_x = pltpu.make_async_copy(x_ref, buf.at[slot(0, 0)], s_in)
-    load_x.start()
-    greet((right, left, mate))
-    load_x.wait()
-    top, low = pl.ds(0, half), pl.ds(half, half)
-
-    def push(src_slot, part, where, send, recv):
-        view = buf.at[src_slot] if part is None else buf.at[src_slot, part]
-        remote(view, view, send, recv, where).start()
-
-    def sent(part, send):
-        view = buf.at[0] if part is None else buf.at[0, part]
-        remote(view, view, send, r_ring.at[0, 0], right).wait_send()
-
-    def arrive(src_slot, part, sem):
-        view = buf.at[src_slot] if part is None else buf.at[src_slot, part]
-        remote(view, view, s_ring.at[0, 0], sem, right).wait_recv()
-
-    own = slot(0, 0)
-    push(own, None, right, s_ring.at[0, 0], r_ring.at[1, 0])
-    push(own, None, left, s_ring.at[0, 1], r_ring.at[1, 1])
-    push(own, None, mate, s_part.at[0, 0], r_part.at[0, 0])
-
-    def ring_step(d):
+class Gather:
+    def __init__(self, n, x_ref, buf, s_in, s_ring, r_ring, s_part, r_part, use):
+        self.n, self.mid, self.x_ref, self.buf, self.s_in, self.use = n, n // 2, x_ref, buf, s_in, use
+        self.s_ring, self.r_ring, self.s_part, self.r_part = s_ring, r_ring, s_part, r_part
+        self.dp, self.core, self.at = plane_ids(n)
+        self.ends = ({"dp": self.at(1)}, {"dp": self.at(-1)}, {"core": 1 - self.core})
+        half = x_ref.shape[0] // 2
+        self.parts = (pl.ds(0, half), pl.ds(half, half))
+
+    def slot(self, off, flip):
+        return 2 * self.at(off) + (self.core if flip == 0 else 1 - self.core)
+
+    def view(self, src, part):
+        return self.buf.at[src] if part is None else self.buf.at[src, part]
+
+    def push(self, src, part, where, send, recv):
+        remote(self.view(src, part), self.view(src, part), send, recv, where).start()
+
+    def sent(self, part, send):
+        remote(self.view(0, part), self.view(0, part), send, self.r_ring.at[0, 0], self.ends[0]).wait_send()
+
+    def arrive(self, src, part, sem):
+        remote(self.view(src, part), self.view(src, part), self.s_ring.at[0, 0], sem, self.ends[0]).wait_recv()
+
+    def begin(self):
+        own = self.slot(0, 0)
+        load = pltpu.make_async_copy(self.x_ref, self.buf.at[own], self.s_in)
+        load.start()
+        greet(self.ends)
+        load.wait()
+        self.push(own, None, self.ends[0], self.s_ring.at[0, 0], self.r_ring.at[1, 0])
+        self.push(own, None, self.ends[1], self.s_ring.at[0, 1], self.r_ring.at[1, 1])
+        self.push(own, None, self.ends[2], self.s_part.at[0, 0], self.r_part.at[0, 0])
+
+    def ring_step(self, d):
+        mid = self.mid
         for side, sign in ((0, -1), (1, 1)):
-            src = slot(sign * d, 0)
-            onward = right if side == 0 else left
+            src = self.slot(sign * d, 0)
+            onward, part = self.ends[side], self.parts[side]
             if d < mid:
-                arrive(src, None, r_ring.at[d, side])
-                if d + 1 < mid:
-                    push(src, None, onward, s_ring.at[d, side], r_ring.at[d + 1, side])
-                else:
-                    push(src, top if side == 0 else low, onward, s_ring.at[d, side], r_ring.at[mid, side])
-                push(src, None, mate, s_part.at[d, side], r_part.at[d, side])
+                self.arrive(src, None, self.r_ring.at[d, side])
+                whole = None if d + 1 < mid else part
+                self.push(src, whole, onward, self.s_ring.at[d, side], self.r_ring.at[d + 1, side])
+                self.push(src, None, self.ends[2], self.s_part.at[d, side], self.r_part.at[d, side])
             else:
-                part = top if side == 0 else low
-                arrive(src, part, r_ring.at[mid, side])
-                push(src, part, mate, s_part.at[mid, side], r_part.at[mid, side])
-
-    def mate_step(d):
+                self.arrive(src, part, self.r_ring.at[mid, side])
+                self.push(src, part, self.ends[2], self.s_part.at[mid, side], self.r_part.at[mid, side])
+
+    def mate_step(self, d):
         if d == 0:
-            arrive(slot(0, 1), None, r_part.at[0, 0])
-        elif d < mid:
-            arrive(slot(-d, 1), None, r_part.at[d, 0])
-            arrive(slot(d, 1), None, r_part.at[d, 1])
+            self.arrive(self.slot(0, 1), None, self.r_part.at[0, 0])
+        elif d < self.mid:
+            self.arrive(self.slot(-d, 1), None, self.r_part.at[d, 0])
+            self.arrive(self.slot(d, 1), None, self.r_part.at[d, 1])
         else:
-            arrive(slot(d, 1), top, r_part.at[d, 0])
-            arrive(slot(d, 1), low, r_part.at[d, 1])
-
-    ready()
-
-    def body(step, carry):
+            self.arrive(self.slot(d, 1), self.parts[0], self.r_part.at[d, 0])
+            self.arrive(self.slot(d, 1), self.parts[1], self.r_part.at[d, 1])
+
+    def step(self, step):
+        mid, core = self.mid, self.core
         for d in range(1, mid + 1):
             first = 2 + 4 * (d - 1)
 
             @pl.when(step == first)
             def _():
-                ring_step(d)
+                self.ring_step(d)
 
             @pl.when(step == first + (2 if d < mid else 1))
             def _():
-                mate_step(d)
+                self.mate_step(d)
 
         @pl.when(step == 1)
         def _():
-            mate_step(0)
+            self.mate_step(0)
 
         later = jnp.maximum(step - 2, 0)
         d = jnp.where(step < 2, 0, 1 + later // 4)
@@ -404,17 +405,153 @@
         last = jnp.where(step < 2, 1, d // mid)
         flip = jnp.where(last == 1, kind, kind // 2)
         off = jnp.where(kind % 2 == 0, -d, d)
-        use(step, 2 * at(off) + core + flip - 2 * core * flip)
+        self.use(step, 2 * self.at(off) + core + flip - 2 * core * flip)
+
+    def end(self):
+        mid = self.mid
+        for d in range(mid + 1):
+            for side in range(2):
+                part = self.parts[side]
+                if d < mid:
+                    self.sent(part if d + 1 == mid and d > 0 else None, self.s_ring.at[d, side])
+                if d > 0 or side == 0:
+                    self.sent(part if d == mid else None, self.s_part.at[d, side])
+
+
+def gather_blocks(n, x_ref, buf, s_in, s_ring, r_ring, s_part, r_part, ready, use):
+    run = Gather(n, x_ref, buf, s_in, s_ring, r_ring, s_part, r_part, use)
+    run.begin()
+    ready()
+
+    def body(step, carry):
+        run.step(step)
         return carry
 
     lax.fori_loop(0, 2 * n, body, 0)
-    for d in range(mid + 1):
-        for side in range(2):
-            part = top if side == 0 else low
-            if d < mid:
-                sent(part if d + 1 == mid and d > 0 else None, s_ring.at[d, side])
-            if d > 0 or side == 0:
-                sent(part if d == mid else None, s_part.at[d, side])
+    run.end()
+
+
+class Swap:
+    def __init__(self, n, pairs, relay, s_src, r_relay, s_fwd, r_dst):
+        self.n, self.pairs, self.relay = n, pairs, relay
+        self.s_src, self.r_relay, self.s_fwd, self.r_dst = s_src, r_relay, s_fwd, r_dst
+        self.dp, self.plane = lax.axis_index("dp"), lax.axis_index("pl")
+        self.away = self.dp != self.plane
+        half = pairs[0][0].shape[0] // 2
+        self.parts = (pl.ds(0, half), pl.ds(half, half))
+
+    def knock(self, signal):
+        @pl.when(self.away)
+        def _():
+            signal({"dp": self.plane})
+            signal({"pl": self.dp})
+
+        @pl.when(jnp.logical_not(self.away))
+        def _():
+            for j in range(1, self.n):
+                signal({"dp": (self.dp + j) % self.n})
+                signal({"pl": (self.dp + j) % self.n})
+
+    def knocks(self):
+        return jnp.where(self.away, 2, 2 * (self.n - 1))
+
+    def first(self, i, path):
+        src = self.pairs[i][0].at[self.parts[path]]
+        dst = self.relay.at[i, path, self.dp if path == 0 else self.plane]
+        to = {"dp": self.plane} if path == 0 else {"pl": self.dp}
+        sem = self.r_relay.at[i, path, self.dp if path == 0 else self.plane]
+        return remote(src, dst, self.s_src.at[i, path], sem, to)
+
+    def landed(self, i, path, j):
+        view = self.relay.at[i, path, j]
+        return remote(view, view, self.s_src.at[i, path], self.r_relay.at[i, path, j], {"dp": j})
+
+    def second(self, i, path, j):
+        dst = self.pairs[i][1].at[self.parts[path]]
+        to = {"pl": j} if path == 0 else {"dp": j}
+        return remote(self.relay.at[i, path, j], dst, self.s_fwd.at[i, path, j], self.r_dst.at[i, path], to)
+
+    def own(self, i, path, out):
+        view = self.relay.at[i, path, self.dp]
+        if out:
+            return pltpu.make_async_copy(view, self.pairs[i][1].at[self.parts[path]], self.r_dst.at[i, path])
+        return pltpu.make_async_copy(self.pairs[i][0].at[self.parts[path]], view, self.s_src.at[i, path])
+
+    def send(self, i):
+        for path in range(2):
+
+            @pl.when(self.away)
+            def _():
+                self.first(i, path).start()
+
+            @pl.when(jnp.logical_not(self.away))
+            def _():
+                self.own(i, path, False).start()
+
+    def pass_on(self, i):
+        @pl.when(jnp.logical_not(self.away))
+        def _():
+            for j in range(1, self.n):
+                for path in range(2):
+                    src = (self.dp + j) % self.n
+                    self.landed(i, path, src).wait_recv()
+                    self.second(i, path, src).start()
+            for path in range(2):
+                self.own(i, path, False).wait()
+                self.own(i, path, True).start()
+
+    def finish(self, i):
+        @pl.when(self.away)
+        def _():
+            for path in range(2):
+                self.second(i, path, 0).wait_recv()
+                self.first(i, path).wait_send()
+
+        @pl.when(jnp.logical_not(self.away))
+        def _():
+            for path in range(2):
+                self.own(i, path, True).wait()
+                for j in range(1, self.n):
+                    self.second(i, path, (self.dp + j) % self.n).wait_send()
+
+
+def swap_scratch(n, count, rows, depth):
+    dma = pltpu.SemaphoreType.DMA
+    return [
+        pltpu.VMEM((count, 2, n, rows // 2, depth), BF16),
+        dma((count, 2)),
+        dma((count, 2, n)),
+        dma((count, 2, n)),
+        dma((count, 2)),
+    ]
+
+
+def swap_kernel(n, count, *refs):
+    run = Swap(n, list(zip(refs[:count], refs[count : 2 * count])), *refs[2 * count :])
+    barrier = pltpu.get_barrier_semaphore()
+    run.knock(lambda where: pl.semaphore_signal(barrier, inc=1, device_id=where, device_id_type=MESH_ID))
+    pl.semaphore_wait(barrier, run.knocks())
+    for i in range(count):
+        run.send(i)
+    for i in range(count):
+        run.pass_on(i)
+    for i in range(count):
+        run.finish(i)
+
+
+def swap_blocks(n, cid, *items):
+    count = len(items)
+    rows, depth = items[0].shape
+    return pl.pallas_call(
+        functools.partial(swap_kernel, n, count),
+        out_shape=tuple(jax.ShapeDtypeStruct(a.shape, a.dtype) for a in items),
+        in_specs=[pl.BlockSpec(memory_space=HBM)] * count,
+        out_specs=[pl.BlockSpec(memory_space=HBM)] * count,
+        scratch_shapes=swap_scratch(n, count, rows, depth),
+        compiler_params=pltpu.CompilerParams(collective_id=cid, has_side_effects=True),
+        cost_estimate=cost(50 * count, 0),
+        name="swap_blocks",
+    )(*items)
 
 
 def gather_dot_kernel(
@@ -723,21 +860,18 @@
 
 
 def start_kernel(
-    n, x_ref, w_ref, small_ref, block_ref, x_out, w_out, small_out, block_out, xv, wv, s_own, s_x, r_x, s_w, r_w, s_s, r_s, s_b, r_b
+    n, x_ref, c_ref, w_ref, small_ref, block_ref, x_out, c_out, w_out, small_out, block_out, wv, s_own, s_w, r_w, s_s, r_s, s_b, r_b, *refs
 ):
     dp, plane, core = (lax.axis_index(a) for a in EVERY)
     rows = w_ref.shape[0]
     width = w_ref.shape[1] // 3
     wide = width // (2 * n)
     away = dp != plane
-    across = {"dp": plane, "pl": dp, "core": core}
+    move = Swap(n, [(x_ref, x_out), (c_ref, c_out)], *refs)
     barrier = pltpu.get_barrier_semaphore()
 
     def knock(where):
         pl.semaphore_signal(barrier, inc=1, device_id=where, device_id_type=MESH_ID)
-
-    def send_x():
-        return remote(x_ref, x_out, s_x, r_x, across)
 
     def send_w(j, part):
         to = (dp + j) % n
@@ -775,17 +909,16 @@
             def _():
                 knock({"dp": plane, "pl": (dp + n - i) % n, "core": (core + k) % 2})
 
+    move.knock(knock)
+    pl.semaphore_wait(barrier, jnp.where(away, 3 * n - 1, 3 * n - 2) + move.knocks())
+    move.send(0)
+
     @pl.when(away)
     def _():
-        knock(across)
-        pl.semaphore_wait(barrier, 3 * n)
-        send_x().start()
         send_b(0, 0).start()
 
     @pl.when(jnp.logical_not(away))
     def _():
-        pl.semaphore_wait(barrier, 3 * n - 2)
-        pltpu.make_async_copy(x_ref, xv, s_own.at[5]).start()
         own_b.start()
 
     for i in range(n):
@@ -801,12 +934,13 @@
         own_w(part, False).wait()
         own_w(part, True).start()
 
+    move.send(1)
+    move.pass_on(0)
+    move.pass_on(1)
+
     @pl.when(jnp.logical_not(away))
     def _():
-        pltpu.make_async_copy(x_ref, xv, s_own.at[5]).wait()
-        pltpu.make_async_copy(xv, x_out, s_own.at[5]).start()
         own_b.wait()
-        pltpu.make_async_copy(xv, x_out, s_own.at[5]).wait()
 
     own_s.wait()
     for part in range(3):
@@ -823,128 +957,135 @@
     @pl.when(away)
     def _():
         send_b(0, 0).wait()
-        send_x().wait()
-
-
-def start(n, cid, x, w, small, block):
+
+    move.finish(0)
+    move.finish(1)
+
+
+def start(n, cid, x, c, w, small, block):
     rows, wide = w.shape[0], w.shape[1] // (6 * n)
     dma = pltpu.SemaphoreType.DMA
     return pl.pallas_call(
         functools.partial(start_kernel, n),
         out_shape=(
             jax.ShapeDtypeStruct(x.shape, x.dtype),
+            jax.ShapeDtypeStruct(c.shape, c.dtype),
             jax.ShapeDtypeStruct((n * rows, 3 * wide), w.dtype),
             jax.ShapeDtypeStruct((n,) + small.shape, small.dtype),
             jax.ShapeDtypeStruct((2 * n,) + block.shape, block.dtype),
         ),
-        in_specs=[pl.BlockSpec(memory_space=HBM)] * 4,
-        out_specs=[pl.BlockSpec(memory_space=HBM)] * 4,
+        in_specs=[pl.BlockSpec(memory_space=HBM)] * 5,
+        out_specs=[pl.BlockSpec(memory_space=HBM)] * 5,
         scratch_shapes=[
-            pltpu.VMEM(x.shape, x.dtype),
             pltpu.VMEM((3, rows, wide), w.dtype),
             dma((6,)),
-            dma,
-            dma,
             dma((n, 3)),
             dma((n, 3)),
             dma((n,)),
             dma((n,)),
             dma((n, 2)),
             dma((n, 2)),
-        ],
-        compiler_params=pltpu.CompilerParams(collective_id=cid, has_side_effects=True),
-        cost_estimate=cost(75, 0),
+        ]
+        + swap_scratch(n, 2, x.shape[0], x.shape[1]),
+        compiler_params=pltpu.CompilerParams(
+            collective_id=cid, has_side_effects=True, vmem_limit_bytes=56 * 2**20
+        ),
+        cost_estimate=cost(95, 0),
         name="start",
-    )(x, w, small, block)
-
-
-def total_kernel(n, a_ref, o_ref, mine, others, part, sums, s_in, s_a, r_a, s_b, r_b, s_out):
-    dp, plane, core = (lax.axis_index(a) for a in EVERY)
-    barrier = pltpu.get_barrier_semaphore()
-    load = pltpu.make_async_copy(a_ref, mine, s_in)
-    load.start()
-    peers = [{"dp": (dp + j) % n} for j in range(1, n)]
-    stack = [(z, k) for z in range(n) for k in range(2) if z + k > 0]
-    for j in range(1, n):
-        pl.semaphore_signal(barrier, inc=1, device_id={"dp": (dp + n - j) % n}, device_id_type=MESH_ID)
-    for z, k in stack:
-        where = {"pl": (plane + n - z) % n, "core": (core + k) % 2}
-        pl.semaphore_signal(barrier, inc=1, device_id=where, device_id_type=MESH_ID)
-    pl.semaphore_wait(barrier, 3 * n - 2)
-    load.wait()
-
-    def send_a(j):
-        to = (dp + j) % n
-        return remote(mine.at[to], others.at[j], s_a.at[j], r_a.at[j], {"dp": to})
-
-    def send_b(i):
-        z, k = stack[i]
-        where = {"pl": (plane + z) % n, "core": (core + k) % 2}
-        return remote(part, sums.at[i], s_b.at[i], r_b.at[i], where)
-
-    for j in range(1, n):
-        send_a(j).start()
-    value = mine[dp]
-    for j in range(1, n):
-        send_a(j).wait_recv()
-        value = value + others[j]
-    part[...] = value
-    for i in range(len(stack)):
-        send_b(i).start()
-    for i in range(len(stack)):
-        send_b(i).wait_recv()
-        value = value + sums[i]
-    for j in range(1, n):
-        send_a(j).wait_send()
-    for i in range(len(stack)):
-        send_b(i).wait_send()
-    mine[0] = value
-    put = pltpu.make_async_copy(mine.at[0], o_ref, s_out)
-    put.start()
-    put.wait()
-
-
-def total(n, cid, a):
+    )(x, c, w, small, block)
+
+
+class Total:
+    def __init__(self, n, a_ref, o_ref, mine, others, part, sums, s_in, s_a, r_a, s_b, r_b):
+        self.n, self.a_ref, self.o_ref = n, a_ref, o_ref
+        self.mine, self.others, self.part, self.sums = mine, others, part, sums
+        self.s_in, self.s_a, self.r_a, self.s_b, self.r_b = s_in, s_a, r_a, s_b, r_b
+        self.dp, self.plane, self.core = (lax.axis_index(a) for a in EVERY)
+        self.stack = [(z, k) for z in range(n) for k in range(2) if z + k > 0]
+
+    def send_a(self, j):
+        to = (self.dp + j) % self.n
+        return remote(self.mine.at[to], self.others.at[j], self.s_a.at[j], self.r_a.at[j], {"dp": to})
+
+    def send_b(self, i):
+        z, k = self.stack[i]
+        where = {"pl": (self.plane + z) % self.n, "core": (self.core + k) % 2}
+        return remote(self.part, self.sums.at[i], self.s_b.at[i], self.r_b.at[i], where)
+
+    def knock(self, signal):
+        for j in range(1, self.n):
+            signal({"dp": (self.dp + self.n - j) % self.n})
+        for z, k in self.stack:
+            signal({"pl": (self.plane + self.n - z) % self.n, "core": (self.core + k) % 2})
+
+    def knocks(self):
+        return 3 * self.n - 2
+
+    def begin(self):
+        load = pltpu.make_async_copy(self.a_ref, self.mine, self.s_in)
+        load.start()
+        load.wait()
+        for j in range(1, self.n):
+            self.send_a(j).start()
+
+    def middle(self):
+        value = self.mine[self.dp]
+        for j in range(1, self.n):
+            self.send_a(j).wait_recv()
+            value = value + self.others[j]
+        self.part[...] = value
+        for i in range(len(self.stack)):
+            self.send_b(i).start()
+
+    def end(self):
+        value = self.part[...]
+        for i in range(len(self.stack)):
+            self.send_b(i).wait_recv()
+            value = value + self.sums[i]
+        for j in range(1, self.n):
+            self.send_a(j).wait_send()
+        for i in range(len(self.stack)):
+            self.send_b(i).wait_send()
+        self.mine[0] = value
+        put = pltpu.make_async_copy(self.mine.at[0], self.o_ref, self.s_in)
+        put.start()
+        put.wait()
+
+
+def total_scratch(n, shape):
     dma = pltpu.SemaphoreType.DMA
-    shape = a.shape[1:]
+    return [
+        pltpu.VMEM((n,) + shape, F32),
+        pltpu.VMEM((n,) + shape, F32),
+        pltpu.VMEM(shape, F32),
+        pltpu.VMEM((2 * n - 1,) + shape, F32),
+        dma,
+        dma((n,)),
+        dma((n,)),
+        dma((2 * n - 1,)),
+        dma((2 * n - 1,)),
+    ]
+
+
+def assemble_kernel(n, parts, wide, in_ref, out_ref):
+    for p in range(parts):
+        for j in range(n):
+            for k in range(2):
+                at = ((p * n + j) * 2 + k) * wide
+                piece = in_ref[k, 0, j, p] if in_ref.shape[3] == parts else in_ref[k, 0, j, 0, :, p * wide : (p + 1) * wide]
+                out_ref[:, at : at + wide] = piece.astype(F32)
+
+
+def assemble(n, whole, parts, wide):
+    chunks, sub = whole.shape[1], whole.shape[4]
+    total_cols = parts * n * 2 * wide
     return pl.pallas_call(
-        functools.partial(total_kernel, n),
-        out_shape=jax.ShapeDtypeStruct(shape, F32),
-        in_specs=[pl.BlockSpec(memory_space=HBM)],
-        out_specs=pl.BlockSpec(memory_space=HBM),
-        scratch_shapes=[
-            pltpu.VMEM(a.shape, F32),
-            pltpu.VMEM(a.shape, F32),
-            pltpu.VMEM(shape, F32),
-            pltpu.VMEM((2 * n - 1,) + shape, F32),
-            dma,
-            dma((n,)),
-            dma((n,)),
-            dma((2 * n - 1,)),
-            dma((2 * n - 1,)),
-            dma,
-        ],
-        compiler_params=pltpu.CompilerParams(collective_id=cid, has_side_effects=True),
-        cost_estimate=cost(12, 0),
-        name="total",
-    )(a)
-
-
-def assemble_kernel(wide, in_ref, out_ref):
-    for k in range(2):
-        out_ref[:, k * wide : (k + 1) * wide] = in_ref[k, 0, 0, 0].astype(F32)
-
-
-def assemble(n, whole, parts, wide):
-    sub = whole.shape[4]
-    apart = whole.shape[3] == parts
-    at = (lambda z, j, p: (0, z, j, p, 0, 0)) if apart else (lambda z, j, p: (0, z, j, 0, 0, p))
-    return pl.pallas_call(
-        functools.partial(assemble_kernel, wide),
-        grid=(n, n, parts),
-        out_shape=jax.ShapeDtypeStruct((n * sub, parts * n * 2 * wide), F32),
-        in_specs=[pl.BlockSpec((2, 1, 1, 1, sub, wide), at)],
-        out_specs=pl.BlockSpec((sub, 2 * wide), lambda z, j, p: (z, p * n + j)),
+        functools.partial(assemble_kernel, n, parts, wide),
+        grid=(chunks,),
+        out_shape=jax.ShapeDtypeStruct((chunks * sub, total_cols), F32),
+        in_specs=[pl.BlockSpec((2, 1) + whole.shape[2:], lambda z: (0, z, 0, 0, 0, 0))],
+        out_specs=pl.BlockSpec((sub, total_cols), lambda z: (z, 0)),
+        compiler_params=pltpu.CompilerParams(vmem_limit_bytes=48 * 2**20),
         cost_estimate=cost(12, 0),
         name="assemble",
     )(whole)
@@ -974,6 +1115,266 @@
         cost_estimate=cost(8, 0),
         name="split_columns",
     )(w)
+
+
+class Stack:
+    def __init__(self, n, count, g_ref, h_ref, gres, hres, refs):
+        self.n, self.count = n, count
+        self.g_ref, self.h_ref, self.gres, self.hres = g_ref, h_ref, gres, hres
+        self.g, self.gin, self.h, self.hin, self.sems, self.cross, self.sides = refs
+        self.dp, self.plane, self.core = (lax.axis_index(a) for a in EVERY)
+        self.mate = {"core": 1 - self.core}
+        self.high = self.h_ref.shape[0]
+        self.wide = self.h_ref.shape[1] // count
+
+    LOAD, SENT, CAME, OWN, ON, BACK, GIVE, GOT = range(8)
+
+    def sem(self, kind, c, which):
+        return self.sems.at[kind, c, which]
+
+    def load(self, c, which):
+        if which == 0:
+            return pltpu.make_async_copy(self.g_ref.at[:, :, c], self.g.at[c], self.sem(self.LOAD, c, 0))
+        src = self.h_ref.at[:, pl.ds(pl.multiple_of(c * self.wide, 128), self.wide)]
+        return pltpu.make_async_copy(src, self.h.at[c], self.sem(self.LOAD, c, 1))
+
+    def hslot(self, c, core):
+        rows = pl.ds(pl.multiple_of(core * self.high, 16), self.high)
+        return self.hres.at[rows, pl.ds(pl.multiple_of(c * self.wide, 128), self.wide)]
+
+    def along(self, c, which, up):
+        to = {"pl": self.plane + (1 if up else -1)}
+        src, dst = (self.g, self.gin) if which == 0 else (self.h, self.hin)
+        return remote(src.at[c], dst.at[c], self.sem(self.SENT, c, which), self.sem(self.CAME, c, which), to)
+
+    def owner(self, c, j):
+        to = (self.dp + j) % self.n
+        src, dst = self.g.at[c, :, to], self.gres.at[self.core, c, self.dp]
+        if j == 0:
+            return pltpu.make_async_copy(src, dst, self.sem(self.OWN, c, 0))
+        return remote(src, dst, self.cross.at[0, c, j], self.cross.at[1, c, j], {"dp": to})
+
+    def keep(self, c):
+        return pltpu.make_async_copy(self.h.at[c], self.hslot(c, self.core), self.sem(self.OWN, c, 1))
+
+    def back(self, c, which, up, first):
+        to = {"pl": self.plane + (1 if up else -1)}
+        if which == 0:
+            src = dst = self.gres.at[self.core, c]
+        else:
+            dst = self.hslot(c, self.core)
+            src = self.h.at[c] if first else dst
+        return remote(src, dst, self.sem(self.ON, c, which), self.sem(self.BACK, c, which), to)
+
+    def give(self, c, which, first):
+        if which == 0:
+            src = dst = self.gres.at[self.core, c]
+        else:
+            dst = self.hslot(c, self.core)
+            src = self.h.at[c] if first else dst
+        return remote(src, dst, self.sem(self.GIVE, c, which), self.sem(self.GOT, c, which), self.mate)
+
+    def begin(self, knock):
+        n = self.n
+        for c in range(self.count // 2):
+            for chunk in (c, self.count // 2 + c):
+                for which in range(2):
+                    self.load(chunk, which).start()
+        for j in range(1, n):
+            knock({"dp": (self.dp + j) % n})
+        knock(self.mate)
+
+        @pl.when(self.plane > 0)
+        def _():
+            knock({"pl": self.plane - 1})
+
+        @pl.when(self.plane < n - 1)
+        def _():
+            knock({"pl": self.plane + 1})
+
+    def knocks(self):
+        ends = (self.plane == 0) | (self.plane == self.n - 1)
+        return jnp.where(ends, self.n + 1, self.n + 2)
+
+    def forward(self, c, place, up):
+        last = place == self.n - 1
+        for which in range(2):
+            self.load(c, which).wait()
+
+        @pl.when(place > 0)
+        def _():
+            for which in range(2):
+                self.along(c, which, up).wait_recv()
+            self.g[c] = (self.g[c].astype(F32) + self.gin[c].astype(F32)).astype(BF16)
+            self.h[c] = (self.h[c].astype(F32) + self.hin[c].astype(F32)).astype(BF16)
+
+        @pl.when(jnp.logical_not(last))
+        def _():
+            for which in range(2):
+                self.along(c, which, up).start()
+
+        @pl.when(last)
+        def _():
+            for j in range(self.n):
+                self.owner(c, j).start()
+            self.keep(c).start()
+            self.back(c, 1, not up, True).start()
+            self.give(c, 1, True).start()
+
+    def homeward(self, c, place, up):
+        @pl.when(place == self.n - 1)
+        def _():
+            self.owner(c, 0).wait()
+            for j in range(1, self.n):
+                self.owner(c, j).wait_recv()
+            self.back(c, 0, up, True).start()
+            self.give(c, 0, True).start()
+
+        @pl.when(place < self.n - 1)
+        def _():
+            for which in (1, 0):
+                self.back(c, which, up, False).wait_recv()
+
+                @pl.when(place > 0)
+                def _():
+                    self.back(c, which, up, False).start()
+
+                self.give(c, which, False).start()
+
+    def steps(self):
+        return self.count // 2 + 2 * self.n - 1
+
+    def step(self, s):
+        n, half = self.n, self.count // 2
+        for up in (True, False):
+            place = self.plane if up else n - 1 - self.plane
+            base = half if up else 0
+            c = s - place
+
+            @pl.when((c >= 0) & (c < half))
+            def _():
+                self.forward(base + c, place, up)
+
+        for up in (True, False):
+            place = self.plane if up else n - 1 - self.plane
+            base = half if up else 0
+            c = s - n - (n - 1 - place)
+
+            @pl.when((c >= 0) & (c < half))
+            def _():
+                self.homeward(base + c, place, not up)
+
+    def end(self):
+        n, half = self.n, self.count // 2
+        for up in (True, False):
+            place = self.plane if up else n - 1 - self.plane
+            base = half if up else 0
+
+            def drain(i, carry):
+                c = base + i
+                for which in range(2):
+                    self.give(c, which, True).wait_recv()
+                    self.give(c, which, True).wait_send()
+
+                @pl.when(place < n - 1)
+                def _():
+                    for which in range(2):
+                        self.along(c, which, up).wait_send()
+
+                @pl.when(place == n - 1)
+                def _():
+                    for j in range(1, n):
+                        self.owner(c, j).wait_send()
+                    self.keep(c).wait()
+
+                @pl.when(place > 0)
+                def _():
+                    for which in range(2):
+                        self.back(c, which, not up, False).wait_send()
+
+                return carry
+
+            lax.fori_loop(0, half, drain, 0)
+
+
+def stack_scratch(n, count, parts, sub, wide, high, width):
+    dma = pltpu.SemaphoreType.DMA
+    cols = width // count
+    return [
+        pltpu.VMEM((count, parts, n, sub, wide), BF16),
+        pltpu.VMEM((count, parts, n, sub, wide), BF16),
+        pltpu.VMEM((count, high, cols), BF16),
+        pltpu.VMEM((count, high, cols), BF16),
+        dma((8, count, 2)),
+        dma((2, count, n)),
+        dma((1,)),
+    ]
+
+
+def finish_kernel(n, count, g_ref, h_ref, t_ref, x_ref, c_ref, gres, hres, t_out, x_out, c_out, *refs):
+    run = Stack(n, count, g_ref, h_ref, gres, hres, refs[:7])
+    small = Total(n, t_ref, t_out, *refs[7:16])
+    move = Swap(n, [(x_ref, x_out), (c_ref, c_out)], *refs[16:])
+    barrier = pltpu.get_barrier_semaphore()
+
+    def knock(where):
+        pl.semaphore_signal(barrier, inc=1, device_id=where, device_id_type=MESH_ID)
+
+    run.begin(knock)
+    small.knock(knock)
+    move.knock(knock)
+    pl.semaphore_wait(barrier, run.knocks() + small.knocks() + move.knocks())
+    small.begin()
+    move.send(0)
+    move.send(1)
+
+    def body(s, carry):
+        run.step(s)
+
+        @pl.when(s == 2)
+        def _():
+            small.middle()
+
+        for i in range(2):
+
+            @pl.when(s == 4 + 2 * i)
+            def _():
+                move.pass_on(i)
+
+        return carry
+
+    lax.fori_loop(0, run.steps(), body, 0)
+    small.end()
+    move.finish(0)
+    move.finish(1)
+    run.end()
+
+
+def finish(n, cid, g, h, t, x, c):
+    parts, _, rows, wide = g.shape
+    high, width = h.shape
+    count = width // 128
+    sub = rows // count
+    return pl.pallas_call(
+        functools.partial(finish_kernel, n, count),
+        out_shape=(
+            jax.ShapeDtypeStruct((2, count, n, parts, sub, wide), BF16),
+            jax.ShapeDtypeStruct((2 * high, width), BF16),
+            jax.ShapeDtypeStruct(t.shape[1:], F32),
+            jax.ShapeDtypeStruct(x.shape, BF16),
+            jax.ShapeDtypeStruct(c.shape, BF16),
+        ),
+        in_specs=[pl.BlockSpec(memory_space=HBM)] * 5,
+        out_specs=[pl.BlockSpec(memory_space=HBM)] * 5,
+        scratch_shapes=stack_scratch(n, count, parts, sub, wide, high, width)
+        + total_scratch(n, t.shape[1:])
+        + swap_scratch(n, 2, x.shape[0], x.shape[1]),
+        compiler_params=pltpu.CompilerParams(
+            collective_id=cid, has_side_effects=True, vmem_limit_bytes=60 * 2**20
+        ),
+        cost_estimate=cost(200, 0),
+        name="finish",
+    )(g.reshape(parts, n, count, sub, wide), h, t, x, c)
 
 
 def local(
@@ -1000,8 +1401,6 @@
     me, plane, core = (lax.axis_index(a) for a in EVERY)
     hw = width // (2 * n)
     units = w_down.shape[0] // 2
-    swap_pairs = [(s * n + z, z * n + s) for s in range(n) for z in range(n)]
-    swap = lambda a: lax.ppermute(a, ("dp", "pl"), swap_pairs)
     pick = lambda a, axis, at: lax.dynamic_index_in_dim(a, at, axis, keepdims=False)
 
     def rows_first(g):
@@ -1014,8 +1413,7 @@
         parts, _, wide = g.shape
         g = g.reshape(parts, n, n, rows // n, wide).transpose(2, 1, 0, 3, 4)
         part = lax.psum_scatter(g, "pl", scatter_dimension=0, tiled=True)
-        part = part.reshape(n, parts * rows // n, wide)
-        return lax.all_to_all(part, "dp", 0, 0, tiled=True)
+        return part.reshape(n, parts * rows // n, wide)
 
     def columns_last(part, parts, wide):
         whole = lax.all_gather(part, ("core", "pl"), axis=0, tiled=True)
@@ -1027,8 +1425,8 @@
 
     small = jnp.concatenate([first_gain, first_shift, second_gain, second_shift, qkv_bias]).reshape(-1, 128)
     ids = jnp.zeros((8, 128), jnp.int32).at[0, :slots].set(block_of.reshape(-1))
-    x, wq, small, ids = start(n, 0, inputs.reshape(toks, width), w_qkv, small, ids)
-    x, w_gateup, cotangent, w_out, w_down = lax.optimization_barrier((x, w_gateup, cotangent, w_out, w_down))
+    x, cot, wq, small, ids = start(n, 0, inputs.reshape(toks, width), cotangent.reshape(toks, width), w_qkv, small, ids)
+    x, w_gateup, w_out, w_down = lax.optimization_barrier((x, w_gateup, w_out, w_down))
     token_rows = x.astype(F32)
     small = small.reshape(n, -1)
     gain_one, shift_one, gain_two, shift_two = (
@@ -1049,7 +1447,6 @@
     wgu = wgu.reshape(2, n * rows, units)
     wo = pick(w_out.reshape(2, hw, width), 0, core)
     wd = pick(w_down.reshape(2, units, width), 0, core)
-    cot = swap(cotangent.reshape(toks, width))
     tables = rotary_tables(blocks.shape[0] * blk)
 
     normed_out, normed_one, inverse_one = layer_norm(token_rows, gain_one, shift_one)
@@ -1073,19 +1470,19 @@
     gq, gk, gv, bias_terms = attend_back(slot_of, qs, ks, vs, att, grad_att, lse, tables, blk)
     grad_proj = jnp.concatenate([gq, gk, gv], axis=1)
     grad_proj, gateup_part, down_part = lax.optimization_barrier((grad_proj, gateup_part, down_part))
+    gateup_part = lax.all_to_all(gateup_part, "dp", 0, 0, tiled=True)
+    grad_qkv = tn(hidden_one, grad_proj).astype(BF16)
+    grad_out = tn(att, grad_middle_all).astype(BF16)
     grad_hidden_one = dot_scatter(n, 6, [(grad_proj, wq)], True)
     gain_one_term = jnp.sum(grad_hidden_one * normed_one, axis=0)
     shift_one_term = jnp.sum(grad_hidden_one, axis=0)
     grad_inputs = grad_middle + norm_back(grad_hidden_one, normed_one, inverse_one, gain_one)
     grad_inputs = grad_inputs.astype(BF16)
     grad_inputs, act = lax.optimization_barrier((grad_inputs, act))
-    outputs = swap((middle + dot_scatter(n, 8, [(act, wd)], False)).astype(BF16))
-    grad_inputs = swap(grad_inputs).astype(F32)
+    outputs = (middle + dot_scatter(n, 8, [(act, wd)], False)).astype(BF16)
 
     grad_down = last(down_part)
     grad_gateup = columns_last(gateup_part, 2, units)
-    grad_out = last(rows_first(tn(att, grad_middle_all)))
-    grad_qkv = columns_last(columns_first(tn(hidden_one, grad_proj).astype(BF16)[None]), 3, hw)
     bias_term = bias_terms[:3].reshape(3, 1, hw)
     at = me * 2 + core
     spots = (jnp.arange(2 * n, dtype=jnp.int32) == at)[None, :, None]
@@ -1094,7 +1491,13 @@
         [a.reshape(n, rows) for a in (gain_one_term, shift_one_term, gain_two_term, shift_two_term)] + [bias_term],
         axis=1,
     )
-    tiny = total(n, 7, tiny.reshape(n, -1, 128)).reshape(-1)
+    grad_qkv, grad_out, tiny, outputs, grad_inputs = finish(
+        n, 7, grad_qkv.reshape(1, n, rows, 3 * hw), grad_out, tiny.reshape(n, -1, 128), outputs, grad_inputs
+    )
+    grad_qkv = assemble(n, grad_qkv, 3, hw)
+    grad_out = grad_out.astype(F32)
+    grad_inputs = grad_inputs.astype(F32)
+    tiny = tiny.reshape(-1)
     terms = [tiny[k * rows : (k + 1) * rows] for k in range(4)]
     return (
         outputs.reshape(inputs.shape),

time: 1200 us -> 1080 us (0.900)
  waiting for transfers between devices: 113 us -> 0.78 us
  Pallas kernels: 860 us -> 845 us
    reduce_scatter x2 -> x1, waiting for transfers between devices: 96 us -> 0.01 us  [columns_first(): part = lax.psum_scatter(g, 'pl', scatter_dimension=0, tiled=True)]
    pallas_call x2, Pallas kernels: 142 us -> 81.3 us  [gather_dot(): pl.pallas_call(functools.partial(gather_dot_kernel, n, trans), out_shape=...]
    pallas_call x1, Pallas kernels: 86.1 us -> 121 us  [start(): pl.pallas_call(functools.partial(start_kernel, n), out_shape=(jax.ShapeDt...]
    all_gather x2 -> x1, waiting for transfers between devices: 14.2 us -> 0.01 us  [last(): return lax.all_gather(part, ('core', 'pl'), axis=0, tiled=True).astype(F32)]
  transfers between devices with their start and end apart: 16 -> 8, of which waited for: 3 -> 0; matrix products, arithmetic and copies ran while one was open for 9% -> 11% of each run, Pallas kernels for 59% -> 58%
where the time goes in v3:
time: 1080 us; the launch traced here: 1070 us
  Pallas kernels  845 us (78%)
  local copies, waits for them, and re-layouts  93 us (9%)
  other arithmetic  51.5 us (5%)
  matrix products  41.6 us (4%)
  blocking collectives  22.3 us (2%)
  between operations  14.6 us (1%)
    pallas_call x1, Pallas kernels, finish(): pl.pallas_call(functools.partial(finish_kernel, n, count), out_shape=(jax...  259 us
    pallas_call x4, Pallas kernels, dot_scatter(): pl.pallas_call(functools.partial(dot_scatter_kernel, n, count, trans), ou...  208 us
    pallas_call x1, Pallas kernels, start(): pl.pallas_call(functools.partial(start_kernel, n), out_shape=(jax.ShapeDt...  121 us
    pallas_call x2, Pallas kernels, gather_dot(): pl.pallas_call(functools.partial(gather_dot_kernel, n, trans), out_shape=...  81.3 us
    pallas_call x1, Pallas kernels, attend_back(): pl.pallas_call(functools.partial(attend_back_kernel, blk, tile), out_shap...  50.2 us
    pallas_call x1, Pallas kernels, gather_mlp(): pl.pallas_call(functools.partial(gather_mlp_kernel, n), out_shape=(jax.Sh...  50.1 us
    dot_general x5, matrix products, tn(): lax.dot_general(a, b, (((0,), (0,)), ((), ())), preferred_element_type=F32)  41.6 us
    pallas_call x1, Pallas kernels, attend(): pl.pallas_call(functools.partial(attend_kernel, blk, tile), out_shape=(ou...  41.4 us
  transfers between devices with their start and end apart: 8, of which 0 were waited for; matrix products, arithmetic and copies ran while one was open for 11% of the time, Pallas kernels for 58%

profile of v3, /device:TPU:0, one launch (start us, length us, event | category | flops | bytes accessed | tf_op | source)
XLA Modules:
  0.0 1073.7 jit_solution(7050576409598700702)
XLA Ops:
  11.9 121.1 %start.1 = (bf16[256,2048]{1,0:T(8,128)(2,1)}, bf16[256,2048]{1,0:T(8,128)(2,1)}, bf16[2048,768]{1,0:T(8,128)(2,1)}, f32[4,28,128]{2,1,0:T(8,128)}, s32[8,8,128]{2,1,0:T(8,128)}) custom-call(bf16[256,2048]{1,0:T(8,128)(2,1)} %bitcast.111, bf16[256,2048]{1,0:T(8,128)(2,1)} %bitcast.112, bf16[512,6144]{1,0:T(8,128)(2,1)} %w_ref.1, f32[28,128]{1,0:T(8,128)} %bitcast.129, ...), custom_call_target="tpu_custom_call" | custom-call | bytes 323000000 | tf_op jit(solution)/shard_map/start/pallas_call | solution.py:968
  138.7 39.5 %gather_dot.2 = (bf16[8,256,2048]{2,1,0:T(8,128)(2,1)}, f32[8,256,768]{2,1,0:T(8,128)}) custom-call(bf16[256,2048]{1,0:T(8,128)(2,1)} %fusion.9.x_ref, bf16[2048,768]{1,0:T(8,128)(2,1)} %get-tuple-element.68.w_ref.refs_1_), custom_call_target="tpu_custom_call" | custom-call | flops 6442450944 | bytes 142800000 | tf_op jit(solution)/shard_map/gather_dot/pallas_call | solution.py:604
  178.3 9.0 split_columns.1
  187.3 4.8 constant_dynamic-slice_fusion
  192.1 2.5 copy.47
  196.0 2.5 copy.49
  200.8 2.7 collective-permute-start.2
  205.7 5.0 fusion.18
  210.7 41.4 %attend.1 = (bf16[2048,256]{1,0:T(8,128)(2,1)}, bf16[2048,256]{1,0:T(8,128)(2,1)}, bf16[2048,256]{1,0:T(8,128)(2,1)}, bf16[2048,256]{1,0:T(8,128)(2,1)}, f32[2048,256]{1,0:T(8,128)}) custom-call(s32[16]{0:T(128)} %select_reduce_fusion.slot_ref, f32[2048,768]{1,0:T(8,128)} %bitcast.94, f32[2048,768]{1,0:T(8,128)} %bitcast.95, f32[2048,768]{1,0:T(8,128)} %bitcast.96, ...), custom_call_target="tpu_custom_call" | custom-call | bytes 139400000 | tf_op jit(solution)/shard_map/attend/pallas_call | solution.py:154
  252.1 3.1 broadcast_in_dim.93
  255.2 2.8 bitcast_dynamic-update-slice_fusion
  259.0 65.6 %dot_scatter.4 = f32[256,2048]{1,0:T(8,128)} custom-call(bf16[8,256,256]{2,1,0:T(8,128)(2,1)} %bitcast.100, bf16[256,2048]{1,0:T(8,128)(2,1)} %dynamic-slice_bitcast_fusion.1.refs_1_.w_ref), custom_call_target="tpu_custom_call" | custom-call | flops 2147483648 | bytes 153000000 | tf_op jit(solution)/shard_map/dot_scatter/pallas_call | solution.py:833
  324.7 1.9 fusion.24
  326.9 4.1 dynamic-slice_bitcast_fusion.d_ref.refs_1_
  332.5 1.7 copy.48
  334.2 2.6 copy.50
  336.8 2.6 copy.52
  344.5 50.1 %gather_mlp.1 = (bf16[8,256,2048]{2,1,0:T(8,128)(2,1)}, bf16[8,256,704]{2,1,0:T(8,128)(2,1)}, bf16[8,256,704]{2,1,0:T(8,128)(2,1)}, bf16[8,256,704]{2,1,0:T(8,128)(2,1)}) custom-call(bf16[256,2048]{1,0:T(8,128)(2,1)} %add_convert_fusion.1.x_ref, bf16[2,2048,704]{2,1,0:T(8,128)(2,1)} %bitcast.16.w_ref, bf16[8,256,2048]{2,1,0:T(8,128)(2,1)} %bitcast.130, ...), custom_call_target="tpu_custom_call" | custom-call | flops 17716740096 | bytes 163200000 | tf_op jit(solution)/shard_map/gather_mlp/pallas_call | solution.py:681
  394.6 9.9 fusion.1
  404.5 6.7 fusion
  411.3 3.0 pad_maximum_fusion
  414.3 7.7 convolution_convert_fusion.1
  422.0 10.3 reshape.264
  432.4 6.7 copy.67
  439.8 6.3 fusion.25
  446.2 50.9 %dot_scatter.5 = f32[256,2048]{1,0:T(8,128)} custom-call(bf16[8,256,704]{2,1,0:T(8,128)(2,1)} %get-tuple-element.82, bf16[8,256,704]{2,1,0:T(8,128)(2,1)} %get-tuple-element.83, bf16[2048,704]{1,0:T(8,128)(2,1)} %bitcast.104, bf16[2048,704]{1,0:T(8,128)(2,1)} %bitcast.103), custom_call_target="tpu_custom_call" | custom-call | flops 11811160064 | bytes 153000000 | tf_op jit(solution)/shard_map/dot_scatter/pallas_call | solution.py:833
  497.1 3.9 multiply_reduce_fusion
  501.0 3.8 fusion.23
  504.8 41.8 %gather_dot.3 = (bf16[8,256,2048]{2,1,0:T(8,128)(2,1)}, bf16[8,256,256]{2,1,0:T(8,128)(2,1)}) custom-call(bf16[256,2048]{1,0:T(8,128)(2,1)} %get-tuple-element.115.x_ref, bf16[256,2048]{1,0:T(8,128)(2,1)} %dynamic-slice_bitcast_fusion.1.refs_1_.w_ref), custom_call_target="tpu_custom_call" | custom-call | flops 2147483648 | bytes 142800000 | tf_op jit(solution)/shard_map/gather_dot/pallas_call | solution.py:604
  546.5 50.2 %attend_back.1 = (bf16[2048,256]{1,0:T(8,128)(2,1)}, bf16[2048,256]{1,0:T(8,128)(2,1)}, bf16[2048,256]{1,0:T(8,128)(2,1)}, f32[8,256]{1,0:T(8,128)}) custom-call(s32[16]{0:T(128)} %select_reduce_fusion.slot_ref, bf16[2048,256]{1,0:T(8,128)(2,1)} %get-tuple-element.74.qs, bf16[2048,256]{1,0:T(8,128)(2,1)} %get-tuple-element.75.ks, ...), custom_call_target="tpu_custom_call" | custom-call | bytes 170000000 | tf_op jit(solution)/shard_map/attend_back/pallas_call | solution.py:264
  596.7 3.1 pad_maximum_fusion.1
  599.9 4.0 copy.56
  603.8 3.6 reshape.265
  607.6 22.3 %all_to_all.5 = bf16[4,256,704]{1,2,0:T(8,128)(2,1)} all-to-all(bf16[4,256,704]{1,2,0:T(8,128)(2,1)S(1)} %reshape.265), channel_id=1, replica_groups=mesh['dp'=4,'pl'=4,'core'=2] {'dp'}, dimensions={0} | all-to-all | bytes 2883584 | tf_op jit(solution)/shard_map/all_to_all | solution.py:1473
  631.5 6.8 convolution_convert_fusion.2.h_ref
  638.3 45.9 %dot_scatter.6 = f32[256,2048]{1,0:T(8,128)} custom-call(bf16[8,256,768]{2,1,0:T(8,128)(2,1)} %bitcast.101, bf16[2048,768]{1,0:T(8,128)(2,1)} %get-tuple-element.68.w_ref.refs_1_), custom_call_target="tpu_custom_call" | custom-call | flops 6442450944 | bytes 153000000 | tf_op jit(solution)/shard_map/dot_scatter/pallas_call | solution.py:833
  684.2 2.7 fusion.11
  687.6 3.4 fusion.15.c_ref
  691.0 45.4 %dot_scatter.7 = f32[256,2048]{1,0:T(8,128)} custom-call(bf16[8,256,704]{2,1,0:T(8,128)(2,1)} %get-tuple-element.84, bf16[704,2048]{1,0:T(8,128)(2,1)} %dynamic-slice_bitcast_fusion.d_ref.refs_1_), custom_call_target="tpu_custom_call" | custom-call | flops 5905580032 | bytes 153000000 | tf_op jit(solution)/shard_map/dot_scatter/pallas_call | solution.py:833
  736.5 3.7 add_convert_fusion.x_ref
  740.1 10.5 convolution_convert_fusion
  750.7 258.9 %finish.1 = (bf16[2,16,4,1,32,768]{5,4,3,2,1,0:T(8,128)(2,1)}, bf16[512,2048]{1,0:T(8,128)(2,1)}, f32[28,128]{1,0:T(8,128)}, bf16[256,2048]{1,0:T(8,128)(2,1)}, bf16[256,2048]{1,0:T(8,128)(2,1)}) custom-call(bf16[1,4,16,32,768]{4,3,2,1,0:T(8,128)(2,1)} %bitcast.102, bf16[256,2048]{1,0:T(8,128)(2,1)} %convolution_convert_fusion.2.h_ref, ...), custom_call_target="tpu_custom_call" | custom-call | bytes 680000000 | tf_op jit(solution)/shard_map/finish/pallas_call | solution.py:1358
  1009.5 2.8 convert.11
  1012.3 12.2 %assemble.2 = f32[512,6144]{1,0:T(8,128)} custom-call(bf16[2,16,4,1,32,768]{5,4,3,2,1,0:T(8,128)(2,1)} %get-tuple-element.103.in_ref), custom_call_target="tpu_custom_call" | custom-call | bytes 40800000 | tf_op jit(solution)/shard_map/assemble/pallas_call | solution.py:1082
  1024.6 2.5 convert_element_type.66
  1028.3 8.7 convert_element_type.67
  1037.0 16.0 %copy.57 = bf16[32,256,704]{2,1,0:T(8,128)(2,1)} copy(bf16[32,256,704]{1,2,0:T(8,128)(2,1)} %all-gather.6.cloned.1.call-done) | data formatting | bytes 23068672 | tf_op jit(solution)/shard_map/all_gather | solution.py:1419
  1053.0 13.0 %assemble.3 = f32[512,11264]{1,0:T(8,128)} custom-call(bf16[2,4,4,2,128,704]{5,4,3,2,1,0:T(8,128)(2,1)} %bitcast.97), custom_call_target="tpu_custom_call" | custom-call | bytes 40800000 | tf_op jit(solution)/shard_map/assemble/pallas_call | solution.py:1082
  (124 shorter events, 29.5 us)
Async XLA Ops:
  7.2 337.3 %all-gather.4.cloned.1.call-start = ((), (), s32[]{:S(2)}) async-start(), calls=%async_computation.3 | async-start | bytes 9437184 | tf_op jit(solution)/shard_map/all_gather | solution.py:1455
  10.7 1.3 copy-start.14
  133.1 4.1 copy-start.2
  135.6 42.6 %copy-start.12 = (f32[256]{0:T(256)}, f32[256]{0:T(256)S(1)}, u32[]{:S(2)}) copy-start(f32[256]{0:T(256)S(1)} %broadcast_multiply_fusion.5) | copy-start | bytes 3076
  137.2 41.0 %copy-start.16 = (f32[256]{0:T(256)}, f32[256]{0:T(256)S(1)}, u32[]{:S(2)}) copy-start(f32[256]{0:T(256)S(1)} %add_rsqrt_fusion.1) | copy-start | bytes 3076
  178.2 421.6 %reduce-scatter.3.cloned.1.call-start = ((), (), s32[]{:S(2)}) async-start(), calls=%async_computation.4 | async-start | bytes 7208960 | tf_op jit(solution)/shard_map/reduce_scatter | solution.py:1415
  194.6 137.9 %collective-permute-start = (bf16[2,512,704]{1,2,0:T(8,128)(2,1)}, bf16[2,512,704]{1,2,0:T(8,128)(2,1)}, u32[]{:S(2)}, u32[]{:S(2)}) collective-permute-start(bf16[2,512,704]{1,2,0:T(8,128)(2,1)} %bitcast.106), channel_id=1, source_target_pairs={{0,8},{8,16},{16,24},{24,0},{1,9},{9,17},{17,25},{25,1},{2,10},{10... | collective-permute-start | bytes 4325384 | tf_op jit(solution)/shard_map/ppermute | solution.py:1445
  198.6 135.6 %collective-permute-start.1 = (bf16[2,512,704]{1,2,0:T(8,128)(2,1)}, bf16[2,512,704]{1,2,0:T(8,128)(2,1)}, u32[]{:S(2)}, u32[]{:S(2)}) collective-permute-start(bf16[2,512,704]{1,2,0:T(8,128)(2,1)} %bitcast.107), channel_id=1, source_target_pairs={{0,16},{8,24},{16,0},{24,8},{1,17},{9,25},{17,1},{25,9},{2,18},{10... | collective-permute-start | bytes 4325384 | tf_op jit(solution)/shard_map/ppermute | solution.py:1445
  200.8 136.0 %collective-permute-start.2 = (bf16[2,512,704]{1,2,0:T(8,128)(2,1)}, bf16[2,512,704]{1,2,0:T(8,128)(2,1)}, u32[]{:S(2)}, u32[]{:S(2)}) collective-permute-start(bf16[2,512,704]{1,2,0:T(8,128)(2,1)} %bitcast.108), channel_id=1, source_target_pairs={{0,24},{8,0},{16,8},{24,16},{1,25},{9,1},{17,9},{25,17},{2,26},{10... | collective-permute-start | bytes 4325384 | tf_op jit(solution)/shard_map/ppermute | solution.py:1445
  255.2 2.8 copy-start.11
  326.5 4.5 copy-start
  339.3 2.0 copy-start.6
  341.3 2.0 copy-start.7
  394.6 9.9 copy-start.19
  394.6 9.9 copy-start.20
  394.6 19.7 %slice-start = ((s8[8388608]{0:T(1024)(128)(4,1)}), s8[4194304]{0:T(1024)(128)(4,1)S(1)}, s32[]{:S(2)}) async-start(s8[8388608]{0:T(1024)(128)(4,1)} %bitcast.131), calls=%async_computation.8 | async-start | bytes 8388608
  404.5 9.8 slice-start.1
  411.2 3.0 copy-start.18
  439.0 168.5 %reduce-scatter.5.cloned.1.call-start = ((), (), s32[]{:S(2)}) async-start(), calls=%async_computation.5 | async-start | bytes 3604480 | tf_op jit(solution)/shard_map/reduce_scatter | solution.py:1407
  439.8 588.5 %all-gather.8.cloned.1.call-start = ((), (), s32[]{:S(2)}) async-start(), calls=%async_computation.7 | async-start | bytes 6488064 | tf_op jit(solution)/shard_map/all_gather | solution.py:1410
  497.1 3.9 copy-start.1
  497.1 3.9 copy-start.3
  607.5 23.9 %copy-start.5 = (bf16[2048,256]{1,0:T(8,128)(2,1)S(1)}, bf16[2048,256]{1,0:T(8,128)(2,1)}, u32[]{:S(2)}) copy-start(bf16[2048,256]{1,0:T(8,128)(2,1)} %get-tuple-element.77.att) | copy-start | bytes 3145732
  607.6 429.4 %all-gather.6.cloned.1.call-start = ((), (), s32[]{:S(2)}) async-start(), calls=%async_computation.6 | async-start | bytes 12976128 | tf_op jit(solution)/shard_map/all_gather | solution.py:1419
  638.2 45.9 %copy-start.13 = (f32[256]{0:T(256)S(1)}, f32[256]{0:T(256)}, u32[]{:S(2)}) copy-start(f32[256]{0:T(256)} %copy-done.12) | copy-start | bytes 3076
  638.2 45.9 %copy-start.17 = (f32[256]{0:T(256)S(1)}, f32[256]{0:T(256)}, u32[]{:S(2)}) copy-start(f32[256]{0:T(256)} %copy-done.16) | copy-start | bytes 3076
  684.1 3.5 copy-start.4
  736.4 3.7 copy-start.8
  1012.3 12.2 %copy-start.9 = (bf16[512,2048]{1,0:T(8,128)(2,1)S(1)}, bf16[512,2048]{1,0:T(8,128)(2,1)}, u32[]{:S(2)}) copy-start(bf16[512,2048]{1,0:T(8,128)(2,1)} %get-tuple-element.104) | copy-start | bytes 6291460
  1024.6 2.5 copy-start.15
  1053.0 13.0 %copy-start.10 = (bf16[256,2048]{1,0:T(8,128)(2,1)S(1)}, bf16[256,2048]{1,0:T(8,128)(2,1)}, u32[]{:S(2)}) copy-start(bf16[256,2048]{1,0:T(8,128)(2,1)} %get-tuple-element.100) | copy-start | bytes 3145732
Sparse Core Ops, SparseCore 0:
  178.4 117.8 all-gather.3
  439.2 102.2 reduce-scatter.2
  543.8 56.8 reduce-scatter.4
  607.7 61.1 all-gather.7
  670.3 156.6 all-gather.5

commit v4 on v3

--- a/solution.py
+++ b/solution.py
@@ -69,110 +69,8 @@
     return lax.dot_general(a, b, (((0,), (0,)), ((), ())), preferred_element_type=F32)
 
 
-def attend_kernel(
-    blk, tile, slot_ref, pq, pk, pv, bq, bk, bv, cos_t, low_t, high_t, qs, ks, vs, att, lse, acc, top, osc
-):
-    length = pq.shape[0]
-
-    def sort_block(b, carry):
-        src = pl.ds(pl.multiple_of(slot_ref[b] * blk, blk), blk)
-        dst = pl.ds(pl.multiple_of(b * blk, blk), blk)
-        c, lo, hi = cos_t[dst, :], low_t[dst, :], high_t[dst, :]
-        q = pq[src, :] + bq[...]
-        k = pk[src, :] + bk[...]
-        q = q * c + roll_pair(q, -(ROT // 2)) * lo + roll_pair(q, ROT // 2) * hi
-        k = k * c + roll_pair(k, -(ROT // 2)) * lo + roll_pair(k, ROT // 2) * hi
-        qs[dst, :] = q.astype(BF16)
-        ks[dst, :] = k.astype(BF16)
-        vs[dst, :] = (pv[src, :] + bv[...]).astype(BF16)
-        return carry
-
-    lax.fori_loop(0, length // blk, sort_block, 0)
-    rows = lax.broadcasted_iota(jnp.int32, (tile, tile), 0)
-    cols = lax.broadcasted_iota(jnp.int32, (tile, tile), 1)
-    masks = [head_mask((tile, PAIR), h) for h in range(2)]
-
-    def q_step(qi, carry):
-        q_at = pl.ds(pl.multiple_of(qi * tile, tile), tile)
-        q = qs[q_at, :]
-        acc[...] = jnp.zeros_like(acc)
-        top[...] = jnp.full(top.shape, -1e30, F32)
-
-        def one(kj, diagonal):
-            k_at = pl.ds(pl.multiple_of(kj * tile, tile), tile)
-            k, v = ks[k_at, :], vs[k_at, :]
-            for h in range(2):
-                qm = jnp.where(masks[h], q, 0).astype(BF16)
-                s = nt(qm, k) * SCALE
-                if diagonal:
-                    s = jnp.where(cols <= rows, s, -jnp.inf)
-                old = top[h]
-                new = jnp.maximum(old, jnp.max(s, axis=1, keepdims=True))
-                p = jnp.exp(s - new[:, :1]).astype(BF16)
-                ve = jnp.where(masks[h], v, 1).astype(BF16)
-                acc[h] = acc[h] * jnp.exp(old - new) + nn(p, ve)
-                top[h] = new
-
-        def k_step(kj, c):
-            one(kj, False)
-            return c
-
-        lax.fori_loop(0, qi, k_step, 0)
-        one(qi, True)
-        a0, a1 = acc[0], acc[1]
-        sum0 = roll_pair(a0, HEAD_DIM)
-        sum1 = roll_pair(a1, HEAD_DIM)
-        total = jnp.where(masks[0], sum0, sum1)
-        mixed = jnp.where(masks[0], a0, a1) / total
-        osc[q_at, :] = mixed.astype(BF16)
-        lse[q_at, :] = jnp.where(masks[0], top[0], top[1]) + jnp.log(total)
-        return carry
-
-    lax.fori_loop(0, length // tile, q_step, 0)
-
-    def place_block(b, carry):
-        dst = pl.ds(pl.multiple_of(slot_ref[b] * blk, blk), blk)
-        att[dst, :] = osc[pl.ds(pl.multiple_of(b * blk, blk), blk), :]
-        return carry
-
-    lax.fori_loop(0, length // blk, place_block, 0)
-
-
-def attend(slot_of, proj, bias, tables, blk):
-    length, width = proj.shape
-    pairs = width // (3 * PAIR)
-    tile = min(512, length)
-    whole = lambda f: pl.BlockSpec((length, PAIR), f)
-    table = pl.BlockSpec((length, PAIR), lambda p, s: (0, 0), pipeline_mode=pl.Buffered(1))
-    in_specs = (
-        [whole(lambda p, s, o=o: (0, o * pairs + p)) for o in range(3)]
-        + [pl.BlockSpec((1, PAIR), lambda p, s, o=o: (0, o * pairs + p)) for o in range(3)]
-        + [table] * 3
-    )
-    out = jax.ShapeDtypeStruct((length, pairs * PAIR), BF16)
-    own = whole(lambda p, s: (0, p))
-    return pl.pallas_call(
-        functools.partial(attend_kernel, blk, tile),
-        out_shape=(out, out, out, out, jax.ShapeDtypeStruct((length, pairs * PAIR), F32)),
-        grid_spec=pltpu.PrefetchScalarGridSpec(
-            num_scalar_prefetch=1,
-            grid=(pairs,),
-            in_specs=in_specs,
-            out_specs=[own] * 5,
-            scratch_shapes=[
-                pltpu.VMEM((2, tile, PAIR), F32),
-                pltpu.VMEM((2, tile, PAIR), F32),
-                pltpu.VMEM((length, PAIR), BF16),
-            ],
-        ),
-        compiler_params=pltpu.CompilerParams(vmem_limit_bytes=56 * 2**20),
-        cost_estimate=cost(41, 0),
-        name="attend",
-    )(slot_of, proj, proj, proj, bias, bias, bias, *tables)
-
-
 def attend_back_kernel(
-    blk, tile, slot_ref, qs, ks, vs, att, gat, lse, cos_t, low_t, high_t, gq, gk, gv, bias, dos, dlt, dq, dk, dv
+    blk, tile, slot_ref, qs, ks, vs, att, gat, lse, cos_t, low_t, high_t, out, bias, dos, dlt, dq, dk, dv
 ):
     length = qs.shape[0]
     bmask = head_mask((blk, PAIR), 0)
@@ -232,10 +130,10 @@
             dst = pl.ds(pl.multiple_of(slot_ref[b] * blk, blk), blk)
             g = dk[sub, :] * SCALE
             g = g * cos_t[pos, :] - roll_pair(g, -(ROT // 2)) * low_t[pos, :] - roll_pair(g, ROT // 2) * high_t[pos, :]
-            gk[dst, :] = g.astype(BF16)
+            out[1, dst, :] = g.astype(BF16)
             bias[1:2, :] += jnp.sum(g, axis=0, keepdims=True)
             w = dv[sub, :]
-            gv[dst, :] = w.astype(BF16)
+            out[2, dst, :] = w.astype(BF16)
             bias[2:3, :] += jnp.sum(w, axis=0, keepdims=True)
         return carry
 
@@ -247,7 +145,7 @@
         dst = pl.ds(pl.multiple_of(slot_ref[b] * blk, blk), blk)
         g = dq[pos, :] * SCALE
         g = g * cos_t[pos, :] - roll_pair(g, -(ROT // 2)) * low_t[pos, :] - roll_pair(g, ROT // 2) * high_t[pos, :]
-        gq[dst, :] = g.astype(BF16)
+        out[0, dst, :] = g.astype(BF16)
         bias[0:1, :] += jnp.sum(g, axis=0, keepdims=True)
         return carry
 
@@ -260,15 +158,17 @@
     tile = min(512, length)
     own = pl.BlockSpec((length, PAIR), lambda p, s: (0, p))
     table = pl.BlockSpec((length, PAIR), lambda p, s: (0, 0), pipeline_mode=pl.Buffered(1))
-    out = jax.ShapeDtypeStruct((length, width), BF16)
     return pl.pallas_call(
         functools.partial(attend_back_kernel, blk, tile),
-        out_shape=(out, out, out, jax.ShapeDtypeStruct((8, width), F32)),
+        out_shape=(jax.ShapeDtypeStruct((3, length, width), BF16), jax.ShapeDtypeStruct((8, width), F32)),
         grid_spec=pltpu.PrefetchScalarGridSpec(
             num_scalar_prefetch=1,
             grid=(pairs,),
             in_specs=[own] * 6 + [table] * 3,
-            out_specs=[own] * 3 + [pl.BlockSpec((8, PAIR), lambda p, s: (0, p))],
+            out_specs=[
+                pl.BlockSpec((3, length, PAIR), lambda p, s: (0, 0, p)),
+                pl.BlockSpec((8, PAIR), lambda p, s: (0, p)),
+            ],
             scratch_shapes=[
                 pltpu.VMEM((length, PAIR), BF16),
                 pltpu.VMEM((length, PAIR), F32),
@@ -304,11 +204,19 @@
     return dp, core, at
 
 
-def greet(ids):
+def greet(ids, more=None):
     barrier = pltpu.get_barrier_semaphore()
+
+    def knock(where):
+        pl.semaphore_signal(barrier, inc=1, device_id=where, device_id_type=MESH_ID)
+
     for where in ids:
-        pl.semaphore_signal(barrier, inc=1, device_id=where, device_id_type=MESH_ID)
-    pl.semaphore_wait(barrier, len(ids))
+        knock(where)
+    if more is None:
+        pl.semaphore_wait(barrier, len(ids))
+    else:
+        more.knock(knock)
+        pl.semaphore_wait(barrier, len(ids) + more.knocks())
 
 
 def remote(src, dst, send, recv, where):
@@ -348,11 +256,11 @@
     def arrive(self, src, part, sem):
         remote(self.view(src, part), self.view(src, part), self.s_ring.at[0, 0], sem, self.ends[0]).wait_recv()
 
-    def begin(self):
+    def begin(self, more=None):
         own = self.slot(0, 0)
         load = pltpu.make_async_copy(self.x_ref, self.buf.at[own], self.s_in)
         load.start()
-        greet(self.ends)
+        greet(self.ends, more)
         load.wait()
         self.push(own, None, self.ends[0], self.s_ring.at[0, 0], self.r_ring.at[1, 0])
         self.push(own, None, self.ends[1], self.s_ring.at[0, 1], self.r_ring.at[1, 1])
@@ -418,17 +326,27 @@
                     self.sent(part if d == mid else None, self.s_part.at[d, side])
 
 
-def gather_blocks(n, x_ref, buf, s_in, s_ring, r_ring, s_part, r_part, ready, use):
+def gather_blocks(n, x_ref, buf, s_in, s_ring, r_ring, s_part, r_part, ready, use, move=None):
     run = Gather(n, x_ref, buf, s_in, s_ring, r_ring, s_part, r_part, use)
-    run.begin()
+    run.begin(move)
+    if move is not None:
+        move.send(0)
     ready()
 
     def body(step, carry):
         run.step(step)
+        if move is not None:
+
+            @pl.when(step == n)
+            def _():
+                move.pass_on(0)
+
         return carry
 
     lax.fori_loop(0, 2 * n, body, 0)
     run.end()
+    if move is not None:
+        move.finish(0)
 
 
 class Swap:
@@ -555,34 +473,39 @@
 
 
 def gather_dot_kernel(
-    n, trans, x_ref, w_ref, all_ref, res_ref, buf, wv, stage, s_ring, r_ring, s_part, r_part, s_in, s_out, s_res
+    n, trans, moving, *refs
 ):
+    move = None
+    if moving:
+        move = Swap(n, [(refs[2], refs[5])], *refs[-5:])
+        refs = refs[:2] + refs[3:5] + refs[6:-5]
+    x_ref, w_ref, all_ref, res_ref, buf, wv, stage, s_ring, r_ring, s_part, r_part, s_in, s_out, s_res = refs
     load_w = pltpu.make_async_copy(w_ref, wv, s_in.at[0])
     load_w.start()
-    width = res_ref.shape[-1]
-    tile = col_tile(width)
-
-    def put(keep, where):
-        return pltpu.make_async_copy(stage.at[keep], res_ref.at[where], s_res.at[keep])
+    count = res_ref.shape[0]
+
+    def put(keep, k, where):
+        return pltpu.make_async_copy(stage.at[keep, k], res_ref.at[k, where], s_res.at[keep, k])
 
     def use(step, where):
         keep = step % 2
 
         @pl.when(step >= 2)
         def _():
-            put(keep, where).wait()
+            for k in range(count):
+                put(keep, k, where).wait()
 
         pltpu.make_async_copy(buf.at[where], all_ref.at[where], s_out.at[step]).start()
         block = buf[where]
-        for c in range(width // tile):
-            cols = pl.ds(c * tile, tile)
-            part = nt(block, wv[cols, :]) if trans else nn(block, wv[:, cols])
-            stage[keep, :, cols] = part.astype(stage.dtype)
-        put(keep, where).start()
-
-    gather_blocks(n, x_ref, buf, s_in.at[1], s_ring, r_ring, s_part, r_part, load_w.wait, use)
+        for k in range(count):
+            part = nt(block, wv[k]) if trans else nn(block, wv[k])
+            stage[keep, k] = part.astype(stage.dtype)
+            put(keep, k, where).start()
+
+    gather_blocks(n, x_ref, buf, s_in.at[1], s_ring, r_ring, s_part, r_part, load_w.wait, use, move)
     for keep in range(2):
-        put(keep, 0).wait()
+        for k in range(count):
+            put(keep, k, 0).wait()
     for step in range(2 * n):
         pltpu.make_async_copy(buf.at[0], all_ref.at[0], s_out.at[step]).wait()
 
@@ -597,48 +520,73 @@
     return [dma((mid, 2)), dma((mid + 1, 2)), dma((mid + 1, 2)), dma((mid + 1, 2))]
 
 
-def gather_dot(n, cid, x, w, trans, dtype):
+def gather_dot(n, cid, x, w, trans, dtype, moved=None):
     rows, depth = x.shape
-    width = w.shape[0] if trans else w.shape[1]
+    count = w.shape[0]
+    width = w.shape[1] if trans else w.shape[2]
     dma = pltpu.SemaphoreType.DMA
-    everything, result = pl.pallas_call(
-        functools.partial(gather_dot_kernel, n, trans),
-        out_shape=(
+    extra = [] if moved is None else [moved]
+    everything, result, *moved = pl.pallas_call(
+        functools.partial(gather_dot_kernel, n, trans, len(extra)),
+        out_shape=[
             jax.ShapeDtypeStruct((2 * n, rows, depth), x.dtype),
-            jax.ShapeDtypeStruct((2 * n, rows, width), dtype),
-        ),
-        in_specs=[pl.BlockSpec(memory_space=HBM)] * 2,
-        out_specs=[pl.BlockSpec(memory_space=HBM)] * 2,
+            jax.ShapeDtypeStruct((count, 2 * n, rows, width), dtype),
+        ]
+        + [jax.ShapeDtypeStruct(a.shape, a.dtype) for a in extra],
+        in_specs=[pl.BlockSpec(memory_space=HBM)] * (2 + len(extra)),
+        out_specs=[pl.BlockSpec(memory_space=HBM)] * (2 + len(extra)),
         scratch_shapes=[
             pltpu.VMEM((2 * n, rows, depth), x.dtype),
             pltpu.VMEM(w.shape, w.dtype),
-            pltpu.VMEM((2, rows, width), dtype),
+            pltpu.VMEM((2, count, rows, width), dtype),
         ]
         + ring_sems(n)
-        + [dma((2,)), dma((2 * n,)), dma((2,))],
+        + [dma((2,)), dma((2 * n,)), dma((2, count))]
+        + [a for b in extra for a in swap_scratch(n, 1, b.shape[0], b.shape[1])],
         compiler_params=pltpu.CompilerParams(
             collective_id=cid, has_side_effects=True, vmem_limit_bytes=60 * 2**20
         ),
-        cost_estimate=cost(42, 4 * n * rows * depth * width),
+        cost_estimate=cost(42, 4 * n * rows * depth * width * count),
         name="gather_dot",
-    )(x, w)
-    return everything.reshape(2 * n * rows, depth), result.reshape(2 * n * rows, width)
+    )(x, w, *extra)
+    out = (everything.reshape(2 * n * rows, depth), result.reshape(count, 2 * n * rows, width))
+    return out + tuple(moved)
+
+
+def place_rows(n, refs, wv, sem):
+    dp, side = lax.axis_index("dp"), lax.axis_index("pl") % 2
+    rows = refs[0].shape[1]
+    half = rows // 2
+    at = pl.ds(pl.multiple_of(dp * rows, 128), rows)
+    copies = [pltpu.make_async_copy(refs[0], wv.at[:, at], sem.at[0])]
+    for j in range(1, n):
+        for other in range(2):
+            first = ((dp + n - j) % n) * rows + half * (side + other - 2 * side * other)
+            at = pl.ds(pl.multiple_of(first, 128), half)
+            k = 2 * j - 1 + other
+            copies.append(pltpu.make_async_copy(refs[k], wv.at[:, at], sem.at[k]))
+    return copies
 
 
 def gather_mlp_kernel(
-    n, x_ref, w_ref, c_ref, d_ref, all_ref, act_ref, gg_ref, gu_ref, buf, wv, dv, cv, stage, s_ring, r_ring, s_part, r_part, s_in, s_c, s_out, s_res
+    n, x_ref, c_ref, d_ref, *refs
 ):
-    load_w = pltpu.make_async_copy(w_ref, wv, s_in.at[0])
-    load_d = pltpu.make_async_copy(d_ref, dv, s_in.at[2])
-    load_w.start()
+    count = 2 * n - 1
+    w_refs = refs[:count]
+    all_ref, act_ref, gu_ref, buf, wv, dv, cv, act, grad = refs[count : count + 9]
+    s_ring, r_ring, s_part, r_part, s_in, s_w, s_c, s_out, s_res = refs[count + 9 :]
+    load_d = pltpu.make_async_copy(d_ref, dv, s_in.at[0])
     load_d.start()
-    outs = (act_ref, gg_ref, gu_ref)
+    for load in place_rows(n, w_refs, wv, s_w):
+        load.start()
 
     def put(keep, k, where):
-        return pltpu.make_async_copy(stage.at[keep, k], outs[k].at[where], s_res.at[keep, k])
+        src, dst = (act, act_ref) if k == 0 else (grad, gu_ref)
+        return pltpu.make_async_copy(src.at[keep], dst.at[where], s_res.at[keep, k])
 
     def ready():
-        load_w.wait()
+        for load in place_rows(n, w_refs, wv, s_w):
+            load.wait()
         load_d.wait()
 
     def use(step, where):
@@ -648,143 +596,140 @@
 
         @pl.when(step >= 2)
         def _():
-            for k in range(3):
+            for k in range(2):
                 put(keep, k, where).wait()
 
         pltpu.make_async_copy(buf.at[where], all_ref.at[where], s_out.at[step]).start()
-        block = buf[where]
-        gate = nn(block, wv[0])
-        upper = nn(block, wv[1])
+        both = nn(buf[where], wv[0])
+        units = act.shape[-1]
+        gate, upper = both[:, :units], both[:, units:]
         load_c.wait()
         back = nt(cv[...], dv[...])
         sig = 1.0 / (1.0 + jnp.exp(-gate))
         swish = gate * sig
-        stage[keep, 0] = (swish * upper).astype(BF16)
-        stage[keep, 1] = (back * upper * sig * (1.0 + gate * (1.0 - sig))).astype(BF16)
-        stage[keep, 2] = (back * swish).astype(BF16)
-        for k in range(3):
+        act[keep] = (swish * upper).astype(BF16)
+        grad[keep, :, :units] = (back * upper * sig * (1.0 + gate * (1.0 - sig))).astype(BF16)
+        grad[keep, :, units:] = (back * swish).astype(BF16)
+        for k in range(2):
             put(keep, k, where).start()
 
     gather_blocks(n, x_ref, buf, s_in.at[1], s_ring, r_ring, s_part, r_part, ready, use)
     for keep in range(2):
-        for k in range(3):
+        for k in range(2):
             put(keep, k, 0).wait()
     for step in range(2 * n):
         pltpu.make_async_copy(buf.at[0], all_ref.at[0], s_out.at[step]).wait()
 
 
-def gather_mlp(n, cid, x, w, cot, wd):
+def gather_mlp(n, cid, x, pieces, cot, wd):
     rows, depth = x.shape
     units = wd.shape[0]
     dma = pltpu.SemaphoreType.DMA
-    out = jax.ShapeDtypeStruct((2 * n, rows, units), BF16)
-    res = pl.pallas_call(
+    everything, act, grad = pl.pallas_call(
         functools.partial(gather_mlp_kernel, n),
-        out_shape=(jax.ShapeDtypeStruct((2 * n, rows, depth), x.dtype), out, out, out),
-        in_specs=[pl.BlockSpec(memory_space=HBM)] * 4,
-        out_specs=[pl.BlockSpec(memory_space=HBM)] * 4,
+        out_shape=(
+            jax.ShapeDtypeStruct((2 * n, rows, depth), x.dtype),
+            jax.ShapeDtypeStruct((2 * n, rows, units), BF16),
+            jax.ShapeDtypeStruct((2 * n, rows, 2 * units), BF16),
+        ),
+        in_specs=[pl.BlockSpec(memory_space=HBM)] * (3 + len(pieces)),
+        out_specs=[pl.BlockSpec(memory_space=HBM)] * 3,
         scratch_shapes=[
             pltpu.VMEM((2 * n, rows, depth), x.dtype),
-            pltpu.VMEM(w.shape, w.dtype),
+            pltpu.VMEM((1, depth, 2 * units), BF16),
             pltpu.VMEM(wd.shape, wd.dtype),
             pltpu.VMEM((rows, depth), BF16),
-            pltpu.VMEM((2, 3, rows, units), BF16),
+            pltpu.VMEM((2, rows, units), BF16),
+            pltpu.VMEM((2, rows, 2 * units), BF16),
         ]
         + ring_sems(n)
-        + [dma((3,)), dma, dma((2 * n,)), dma((2, 3))],
+        + [dma((2,)), dma((2 * n,)), dma, dma((2 * n,)), dma((2, 2))],
         compiler_params=pltpu.CompilerParams(
             collective_id=cid, has_side_effects=True, vmem_limit_bytes=60 * 2**20
         ),
         cost_estimate=cost(48, 12 * n * rows * depth * units),
         name="gather_mlp",
-    )(x, w, cot.reshape(2 * n, rows, depth), wd)
-    return [a.reshape(2 * n * rows, -1) for a in res]
-
-
-def dot_scatter_kernel(
-    n, count, trans, *refs
-):
-    a_refs, w_refs, out_ref = refs[:count], refs[count : 2 * count], refs[2 * count]
-    avs, wvs = refs[2 * count + 1 : 3 * count + 1], refs[3 * count + 1 : 4 * count + 1]
-    to_mate, from_mate, hop, from_ring, acc, s_a, s_w, s_part, r_part, s_ring, r_ring, s_o = refs[4 * count + 1 :]
-    dp, core, at = plane_ids(n)
-    rows = acc.shape[0]
-    half = rows // 2
-    mid = n // 2
-    right, left, mate = {"dp": at(1)}, {"dp": at(-1)}, {"core": 1 - core}
-    offsets = [mid]
-    for d in range(mid - 1, 0, -1):
-        offsets += [d, -d]
-    offsets += [0]
-
-    def offset_of(j):
-        d = mid - (j + 1) // 2
-        return jnp.where(j % 2 == 1, d, -d)
-
-    loads = [pltpu.make_async_copy(w_refs[k], wvs[k], s_w.at[k]) for k in range(count)]
-    for load in loads:
-        load.start()
-
-    def slot_of(step):
+    )(x, cot.reshape(2 * n, rows, depth), wd, *pieces)
+    toks = 2 * n * rows
+    return everything.reshape(toks, depth), act.reshape(toks, units), grad.reshape(1, toks, 2 * units)
+
+
+class Scatter:
+    def __init__(self, n, trans, a_ref, loads, wv, refs):
+        self.n, self.trans, self.a_ref, self.loads, self.wv = n, trans, a_ref, loads, wv
+        self.av, self.hop, self.from_mate, self.from_ring, self.acc = refs[:5]
+        self.s_a, self.s_part, self.r_part, self.s_ring, self.r_ring = refs[5:]
+        self.dp, self.core, self.at = plane_ids(n)
+        self.ends = ({"dp": self.at(1)}, {"dp": self.at(-1)})
+        self.mate = {"core": 1 - self.core}
+        self.mid = n // 2
+        half = self.acc.shape[0] // 2
+        self.parts = (pl.ds(0, half), pl.ds(half, half))
+
+    def load_a(self, step):
         j, own = step // 2, step % 2
-        who = core + (1 - own) - 2 * core * (1 - own)
-        return 2 * at(offset_of(j)) + who
-
-    def load_a(step, k):
-        return pltpu.make_async_copy(a_refs[k].at[slot_of(step)], avs[k].at[step], s_a.at[step, k])
-
-    for step in range(2 * n):
-        for k in range(count):
-            load_a(step, k).start()
-    greet((right, left, mate))
-    for load in loads:
-        load.wait()
-    depth = out_ref.shape[-1]
-    tile = col_tile(depth)
-    top, low = pl.ds(0, half), pl.ds(half, half)
-    waits = []
-
-    def hand(j):
-        return remote(to_mate.at[j], from_mate.at[j], s_part.at[j], r_part.at[j], mate)
-
-    def ring(j, part, side, send, recv):
-        src = hop.at[j] if part is None else hop.at[j, part]
-        dst = from_ring.at[recv, side] if part is None else from_ring.at[recv, side, part]
-        return remote(src, dst, s_ring.at[send, side], r_ring.at[recv, side], right if side == 0 else left)
-
-    def body(step, carry):
+        d = self.mid - (j + 1) // 2
+        off = jnp.where(j % 2 == 1, d, -d)
+        who = self.core + (1 - own) - 2 * self.core * (1 - own)
+        return pltpu.make_async_copy(self.a_ref.at[:, 2 * self.at(off) + who], self.av.at[step], self.s_a.at[step])
+
+    def hand(self, j):
+        return remote(self.hop.at[j], self.from_mate.at[j], self.s_part.at[j], self.r_part.at[j], self.mate)
+
+    def ring(self, j, part, side, send, recv):
+        src = self.hop.at[j] if part is None else self.hop.at[j, part]
+        dst = self.from_ring.at[recv, side] if part is None else self.from_ring.at[recv, side, part]
+        return remote(src, dst, self.s_ring.at[send, side], self.r_ring.at[recv, side], self.ends[side])
+
+    def begin(self):
+        for load in self.loads:
+            load.start()
+        for step in range(2 * self.n):
+            self.load_a(step).start()
+
+    def knock(self, signal):
+        for where in self.ends + (self.mate,):
+            signal(where)
+
+    def ready(self):
+        for load in self.loads:
+            load.wait()
+
+    def product(self, step, cols):
+        total = None
+        for p in range(self.av.shape[1]):
+            block = self.av[step, p]
+            part = nt(block, self.wv[p, cols, :]) if self.trans else nn(block, self.wv[p, :, cols])
+            total = part if total is None else total + part
+        return total
+
+    def step(self, step):
+        mid = self.mid
         j, own = step // 2, step % 2
-        for k in range(count):
-            load_a(step, k).wait()
-
-        def product(cols):
-            total = None
-            for k in range(count):
-                block = avs[k][step]
-                part = nt(block, wvs[k][cols, :]) if trans else nn(block, wvs[k][:, cols])
-                total = part if total is None else total + part
-            return total
+        self.load_a(step).wait()
+        depth = self.acc.shape[1]
+        tile = col_tile(depth)
 
         @pl.when(own == 0)
         def _():
             for c in range(depth // tile):
                 cols = pl.ds(c * tile, tile)
-                to_mate[j, :, cols] = product(cols).astype(BF16)
-            hand(j).start()
+                self.hop[j, :, cols] = self.product(step, cols).astype(BF16)
+            self.hand(j).start()
 
         @pl.when(own == 1)
         def _():
-            hand(j).wait_recv()
+            self.hand(j).wait()
             for c in range(depth // tile):
                 cols = pl.ds(c * tile, tile)
-                part = product(cols) + from_mate[j, :, cols].astype(F32)
-                acc[:, cols] = part
-                hop[j, :, cols] = part.astype(BF16)
+                part = self.product(step, cols) + self.from_mate[j, :, cols].astype(F32)
+                self.acc[:, cols] = part
+                self.hop[j, :, cols] = part.astype(BF16)
 
             @pl.when(j == 0)
             def _():
-                ring(0, top, 0, 0, mid - 1).start()
-                ring(0, low, 1, 0, mid - 1).start()
+                for side in range(2):
+                    self.ring(0, self.parts[side], side, 0, mid - 1).start()
 
             for d in range(mid - 1, 0, -1):
                 first = 1 + 2 * (mid - 1 - d)
@@ -792,82 +737,102 @@
                 @pl.when(j == first + 1)
                 def _():
                     for side in range(2):
-                        k = first + side
-                        if d == mid - 1:
-                            part = top if side == 0 else low
-                            ring(0, part, side, 0, d).wait_recv()
-                            hop[k, part, :] = (
-                                hop[k, part, :].astype(F32) + from_ring[d, side, part, :].astype(F32)
-                            ).astype(BF16)
-                        else:
-                            ring(k - 2, None, side, 0, d).wait_recv()
-                            hop[k] = (hop[k].astype(F32) + from_ring[d, side].astype(F32)).astype(BF16)
-                        ring(k, None, side, mid - d, d - 1).start()
-
+                        self.add(first + side, d, side)
+
+    def add(self, k, d, side):
+        if d == self.mid - 1:
+            part = self.parts[side]
+            self.ring(0, part, side, 0, d).wait_recv()
+            both = self.hop[k, part, :].astype(F32) + self.from_ring[d, side, part, :].astype(F32)
+            self.hop[k, part, :] = both.astype(BF16)
+        else:
+            self.ring(k - 2, None, side, 0, d).wait_recv()
+            self.hop[k] = (self.hop[k].astype(F32) + self.from_ring[d, side].astype(F32)).astype(BF16)
+        self.ring(k, None, side, self.mid - d, d - 1).start()
+
+    def result(self):
+        for side in range(2):
+            self.ring(self.n - 3 + side, None, side, self.mid - 1, 0).wait_recv()
+        self.acc[...] += self.from_ring[0, 0].astype(F32) + self.from_ring[0, 1].astype(F32)
+
+    def end(self):
+        mid = self.mid
+        for side in range(2):
+            self.ring(0, self.parts[side], side, 0, mid - 1).wait_send()
+        for d in range(mid - 1, 0, -1):
+            for side in range(2):
+                self.ring(1 + 2 * (mid - 1 - d) + side, None, side, mid - d, d - 1).wait_send()
+
+
+def scatter_scratch(n, parts, rows, inner, depth):
+    dma = pltpu.SemaphoreType.DMA
+    mid = n // 2
+    return [
+        pltpu.VMEM((2 * n, parts, rows, inner), BF16),
+        pltpu.VMEM((n, rows, depth), BF16),
+        pltpu.VMEM((n, rows, depth), BF16),
+        pltpu.VMEM((mid, 2, rows, depth), BF16),
+        pltpu.VMEM((rows, depth), F32),
+        dma((2 * n,)),
+        dma((n,)),
+        dma((n,)),
+        dma((mid, 2)),
+        dma((mid, 2)),
+    ]
+
+
+def dot_scatter_kernel(n, count, trans, *refs):
+    a_refs, w_refs = refs[0], refs[1 : 1 + count]
+    out_ref, wv, s_w, s_o = refs[1 + count : 5 + count]
+    loads = place_rows(n, w_refs, wv, s_w) if count > 1 else [pltpu.make_async_copy(w_refs[0], wv, s_w.at[0])]
+    run = Scatter(n, trans, a_refs, loads, wv, refs[5 + count :])
+    run.begin()
+    greet(run.ends + (run.mate,))
+    run.ready()
+
+    def body(step, carry):
+        run.step(step)
         return carry
 
     lax.fori_loop(0, 2 * n, body, 0)
-    for side in range(2):
-        ring(n - 2 + side - 1, None, side, mid - 1, 0).wait_recv()
-    acc[...] += from_ring[0, 0].astype(F32) + from_ring[0, 1].astype(F32)
-    put = pltpu.make_async_copy(acc, out_ref, s_o)
+    run.result()
+    put = pltpu.make_async_copy(run.acc, out_ref, s_o)
     put.start()
-    for j in range(n):
-        hand(j).wait_send()
-    ring(0, top, 0, 0, mid - 1).wait_send()
-    ring(0, low, 1, 0, mid - 1).wait_send()
-    for d in range(mid - 1, 0, -1):
-        for side in range(2):
-            ring(1 + 2 * (mid - 1 - d) + side, None, side, mid - d, d - 1).wait_send()
+    run.end()
     put.wait()
 
 
-def dot_scatter(n, cid, terms, trans):
-    depth = terms[0][1].shape[0] if trans else terms[0][1].shape[1]
-    rows = terms[0][0].shape[0] // (2 * n)
-    mid = n // 2
-    count = len(terms)
+def dot_scatter(n, cid, a, pieces, trans):
+    parts, toks, inner = a.shape
+    rows = toks // (2 * n)
+    count = len(pieces)
+    w_rows = pieces[0].shape[1] * (n if count > 1 else 1)
+    w_shape = (parts, w_rows, pieces[0].shape[2])
+    depth = w_rows if trans else w_shape[2]
     dma = pltpu.SemaphoreType.DMA
-    lhs = [a.reshape(2 * n, rows, a.shape[1]) for a, _ in terms]
-    rhs = [w for _, w in terms]
     return pl.pallas_call(
         functools.partial(dot_scatter_kernel, n, count, trans),
         out_shape=jax.ShapeDtypeStruct((rows, depth), F32),
-        in_specs=[pl.BlockSpec(memory_space=HBM)] * (2 * count),
+        in_specs=[pl.BlockSpec(memory_space=HBM)] * (1 + count),
         out_specs=pl.BlockSpec(memory_space=HBM),
-        scratch_shapes=[pltpu.VMEM(a.shape, BF16) for a in lhs]
-        + [pltpu.VMEM(w.shape, BF16) for w in rhs]
-        + [
-            pltpu.VMEM((n, rows, depth), BF16),
-            pltpu.VMEM((n, rows, depth), BF16),
-            pltpu.VMEM((n, rows, depth), BF16),
-            pltpu.VMEM((mid, 2, rows, depth), BF16),
-            pltpu.VMEM((rows, depth), F32),
-            dma((2 * n, count)),
-            dma((count,)),
-            dma((n,)),
-            dma((n,)),
-            dma((mid, 2)),
-            dma((mid, 2)),
-            dma,
-        ],
+        scratch_shapes=[pltpu.VMEM(w_shape, BF16), dma((2 * n,)), dma] + scatter_scratch(n, parts, rows, inner, depth),
         compiler_params=pltpu.CompilerParams(
             collective_id=cid, has_side_effects=True, vmem_limit_bytes=62 * 2**20
         ),
-        cost_estimate=cost(45, 4 * n * rows * depth * sum(a.shape[2] for a in lhs)),
+        cost_estimate=cost(45, 2 * parts * toks * inner * depth),
         name="dot_scatter",
-    )(*lhs, *rhs)
+    )(a.reshape(parts, 2 * n, rows, inner), *pieces)
 
 
 def start_kernel(
-    n, x_ref, c_ref, w_ref, small_ref, block_ref, x_out, c_out, w_out, small_out, block_out, wv, s_own, s_w, r_w, s_s, r_s, s_b, r_b, *refs
+    n, x_ref, w_ref, small_ref, block_ref, x_out, w_out, small_out, block_out, wv, s_own, s_w, r_w, s_s, r_s, s_b, r_b, *refs
 ):
     dp, plane, core = (lax.axis_index(a) for a in EVERY)
     rows = w_ref.shape[0]
     width = w_ref.shape[1] // 3
     wide = width // (2 * n)
     away = dp != plane
-    move = Swap(n, [(x_ref, x_out), (c_ref, c_out)], *refs)
+    move = Swap(n, [(x_ref, x_out)], *refs)
     barrier = pltpu.get_barrier_semaphore()
 
     def knock(where):
@@ -876,7 +841,7 @@
     def send_w(j, part):
         to = (dp + j) % n
         at = pl.multiple_of(part * width + to * (2 * wide) + core * wide, 128)
-        dst = w_out.at[pl.ds(pl.multiple_of(dp * rows, 128), rows), pl.ds(part * wide, wide)]
+        dst = w_out.at[part, pl.ds(pl.multiple_of(dp * rows, 128), rows)]
         return remote(w_ref.at[:, pl.ds(at, wide)], dst, s_w.at[j, part], r_w.at[j, part], {"dp": to})
 
     def send_s(j):
@@ -890,7 +855,7 @@
     def own_w(part, back):
         at = pl.multiple_of(part * width + dp * (2 * wide) + core * wide, 128)
         src = w_ref.at[:, pl.ds(at, wide)]
-        dst = w_out.at[pl.ds(pl.multiple_of(dp * rows, 128), rows), pl.ds(part * wide, wide)]
+        dst = w_out.at[part, pl.ds(pl.multiple_of(dp * rows, 128), rows)]
         if back:
             return pltpu.make_async_copy(wv.at[part], dst, s_own.at[part])
         return pltpu.make_async_copy(src, wv.at[part], s_own.at[part])
@@ -930,13 +895,11 @@
     for j in range(1, n):
         for part in range(3):
             send_w(j, part).start()
+    move.pass_on(0)
     for part in range(3):
         own_w(part, False).wait()
         own_w(part, True).start()
 
-    move.send(1)
-    move.pass_on(0)
-    move.pass_on(1)
 
     @pl.when(jnp.logical_not(away))
     def _():
@@ -959,23 +922,21 @@
         send_b(0, 0).wait()
 
     move.finish(0)
-    move.finish(1)
-
-
-def start(n, cid, x, c, w, small, block):
+
+
+def start(n, cid, x, w, small, block):
     rows, wide = w.shape[0], w.shape[1] // (6 * n)
     dma = pltpu.SemaphoreType.DMA
     return pl.pallas_call(
         functools.partial(start_kernel, n),
         out_shape=(
             jax.ShapeDtypeStruct(x.shape, x.dtype),
-            jax.ShapeDtypeStruct(c.shape, c.dtype),
-            jax.ShapeDtypeStruct((n * rows, 3 * wide), w.dtype),
+            jax.ShapeDtypeStruct((3, n * rows, wide), w.dtype),
             jax.ShapeDtypeStruct((n,) + small.shape, small.dtype),
             jax.ShapeDtypeStruct((2 * n,) + block.shape, block.dtype),
         ),
-        in_specs=[pl.BlockSpec(memory_space=HBM)] * 5,
-        out_specs=[pl.BlockSpec(memory_space=HBM)] * 5,
+        in_specs=[pl.BlockSpec(memory_space=HBM)] * 4,
+        out_specs=[pl.BlockSpec(memory_space=HBM)] * 4,
         scratch_shapes=[
             pltpu.VMEM((3, rows, wide), w.dtype),
             dma((6,)),
@@ -986,13 +947,13 @@
             dma((n, 2)),
             dma((n, 2)),
         ]
-        + swap_scratch(n, 2, x.shape[0], x.shape[1]),
+        + swap_scratch(n, 1, x.shape[0], x.shape[1]),
         compiler_params=pltpu.CompilerParams(
             collective_id=cid, has_side_effects=True, vmem_limit_bytes=56 * 2**20
         ),
         cost_estimate=cost(95, 0),
         name="start",
-    )(x, c, w, small, block)
+    )(x, w, small, block)
 
 
 class Total:
@@ -1067,54 +1028,110 @@
     ]
 
 
-def assemble_kernel(n, parts, wide, in_ref, out_ref):
+def assemble_kernel(n, parts, wide, lead, in_ref, out_ref):
+    me = lax.axis_index("dp")
     for p in range(parts):
         for j in range(n):
             for k in range(2):
                 at = ((p * n + j) * 2 + k) * wide
-                piece = in_ref[k, 0, j, p] if in_ref.shape[3] == parts else in_ref[k, 0, j, 0, :, p * wide : (p + 1) * wide]
+                if lead == 0:
+                    piece = in_ref[k, 0, j, p]
+                else:
+                    piece = in_ref[0, k, (me + n - j) % n, :, p * wide : (p + 1) * wide]
                 out_ref[:, at : at + wide] = piece.astype(F32)
 
 
-def assemble(n, whole, parts, wide):
-    chunks, sub = whole.shape[1], whole.shape[4]
+def assemble(n, whole, parts, wide, lead):
+    chunks, sub = whole.shape[1 - lead], whole.shape[4 - lead]
     total_cols = parts * n * 2 * wide
+    block = (2, 1) if lead == 0 else (1, 2)
+    at = (lambda z: (0, z, 0, 0, 0, 0)) if lead == 0 else (lambda z: (z, 0, 0, 0, 0))
     return pl.pallas_call(
-        functools.partial(assemble_kernel, n, parts, wide),
+        functools.partial(assemble_kernel, n, parts, wide, lead),
         grid=(chunks,),
         out_shape=jax.ShapeDtypeStruct((chunks * sub, total_cols), F32),
-        in_specs=[pl.BlockSpec((2, 1) + whole.shape[2:], lambda z: (0, z, 0, 0, 0, 0))],
+        in_specs=[pl.BlockSpec(block + whole.shape[2:], at)],
         out_specs=pl.BlockSpec((sub, total_cols), lambda z: (z, 0)),
-        compiler_params=pltpu.CompilerParams(vmem_limit_bytes=48 * 2**20),
+        compiler_params=pltpu.CompilerParams(vmem_limit_bytes=56 * 2**20),
         cost_estimate=cost(12, 0),
         name="assemble",
     )(whole)
 
 
-def split_columns_kernel(units, w_ref, o_ref):
+def split_columns_kernel(units, to_ref, gate_ref, up_ref, o_ref):
     core = lax.axis_index("core")
     for k in range(2):
 
         @pl.when(core == k)
         def _():
-            o_ref[0, 0] = w_ref[:, k * units : (k + 1) * units]
-
-
-def split_columns(n, w):
+            o_ref[0, :, :units] = gate_ref[:, k * units : (k + 1) * units]
+            o_ref[0, :, units:] = up_ref[:, k * units : (k + 1) * units]
+
+
+def split_columns(n, w, to, half=None):
     rows = w.shape[0]
     units = w.shape[1] // (4 * n)
     if (2 * units) % 128:
         mine = w.reshape(rows, 2, n, 2, units)
-        return lax.dynamic_index_in_dim(mine, lax.axis_index("core"), 3, keepdims=False).transpose(2, 1, 0, 3)
+        mine = lax.dynamic_index_in_dim(mine, lax.axis_index("core"), 3, keepdims=False)
+        mine = lax.dynamic_index_in_dim(mine, to, 2, keepdims=False).reshape(1, rows, 2 * units)
+        if half is None:
+            return mine
+        return lax.dynamic_slice_in_dim(mine, half * (rows // 2), rows // 2, 1)
+    if half is None:
+        half = jnp.zeros((), jnp.int32)
+    else:
+        rows = rows // 2
     return pl.pallas_call(
         functools.partial(split_columns_kernel, units),
-        grid=(n, 2),
-        out_shape=jax.ShapeDtypeStruct((n, 2, rows, units), w.dtype),
-        in_specs=[pl.BlockSpec((rows, 2 * units), lambda j, p: (0, p * n + j))],
-        out_specs=pl.BlockSpec((1, 1, rows, units), lambda j, p: (j, p, 0, 0)),
-        cost_estimate=cost(8, 0),
+        grid_spec=pltpu.PrefetchScalarGridSpec(
+            num_scalar_prefetch=1,
+            grid=(1,),
+            in_specs=[
+                pl.BlockSpec((rows, 2 * units), lambda i, t: (t[1], t[0])),
+                pl.BlockSpec((rows, 2 * units), lambda i, t: (t[1], n + t[0])),
+            ],
+            out_specs=pl.BlockSpec((1, rows, 2 * units), lambda i, t: (0, 0, 0)),
+        ),
+        out_shape=jax.ShapeDtypeStruct((1, rows, 2 * units), w.dtype),
+        cost_estimate=cost(2, 0),
         name="split_columns",
-    )(w)
+    )(jnp.stack([to, half]).astype(jnp.int32), w, w)
+
+
+def weight_grad_kernel(planes, h_ref, g_ref, o_ref):
+    parts, _, wide = g_ref.shape
+    sub = h_ref.shape[1] // planes
+    for p in range(parts):
+        out = tn(h_ref[...], g_ref[p]).astype(BF16)
+        if planes == 1:
+            o_ref[p, 0] = out
+        else:
+            for z in range(planes):
+                o_ref[z, 0, :, p * wide : (p + 1) * wide] = out[z * sub : (z + 1) * sub]
+
+
+def weight_grad(n, planes, h, g):
+    parts, toks, wide = g.shape
+    rows = h.shape[1] // n
+    if planes == 1:
+        shape, block, at = (parts, n, rows, wide), (parts, 1, rows, wide), lambda r: (0, r, 0, 0)
+    else:
+        sub = rows // planes
+        shape, block, at = (planes, n, sub, parts * wide), (planes, 1, sub, parts * wide), lambda r: (0, r, 0, 0)
+    return pl.pallas_call(
+        functools.partial(weight_grad_kernel, planes),
+        grid=(n,),
+        in_specs=[
+            pl.BlockSpec((toks, rows), lambda r: (0, r)),
+            pl.BlockSpec((parts, toks, wide), lambda r: (0, 0, 0), pipeline_mode=pl.Buffered(1)),
+        ],
+        out_specs=pl.BlockSpec(block, at),
+        out_shape=jax.ShapeDtypeStruct(shape, BF16),
+        compiler_params=pltpu.CompilerParams(vmem_limit_bytes=56 * 2**20),
+        cost_estimate=cost(16, 2 * parts * toks * h.shape[1] * wide),
+        name="weight_grad",
+    )(h, g)
 
 
 class Stack:
@@ -1125,7 +1142,7 @@
         self.dp, self.plane, self.core = (lax.axis_index(a) for a in EVERY)
         self.mate = {"core": 1 - self.core}
         self.high = self.h_ref.shape[0]
-        self.wide = self.h_ref.shape[1] // count
+        self.wide = 2 * self.h_ref.shape[1] // count
 
     LOAD, SENT, CAME, OWN, ON, BACK, GIVE, GOT = range(8)
 
@@ -1135,12 +1152,16 @@
     def load(self, c, which):
         if which == 0:
             return pltpu.make_async_copy(self.g_ref.at[:, :, c], self.g.at[c], self.sem(self.LOAD, c, 0))
-        src = self.h_ref.at[:, pl.ds(pl.multiple_of(c * self.wide, 128), self.wide)]
+        src = self.h_ref.at[self.corner(c, 0)]
         return pltpu.make_async_copy(src, self.h.at[c], self.sem(self.LOAD, c, 1))
 
+    def corner(self, c, core):
+        half = self.high // 2
+        first = pl.multiple_of(core * self.high + (c % 2) * half, 16)
+        return pl.ds(first, half), pl.ds(pl.multiple_of((c // 2) * self.wide, 128), self.wide)
+
     def hslot(self, c, core):
-        rows = pl.ds(pl.multiple_of(core * self.high, 16), self.high)
-        return self.hres.at[rows, pl.ds(pl.multiple_of(c * self.wide, 128), self.wide)]
+        return self.hres.at[self.corner(c, core)]
 
     def along(self, c, which, up):
         to = {"pl": self.plane + (1 if up else -1)}
@@ -1299,22 +1320,29 @@
 
 def stack_scratch(n, count, parts, sub, wide, high, width):
     dma = pltpu.SemaphoreType.DMA
-    cols = width // count
+    cols = 2 * width // count
     return [
         pltpu.VMEM((count, parts, n, sub, wide), BF16),
         pltpu.VMEM((count, parts, n, sub, wide), BF16),
-        pltpu.VMEM((count, high, cols), BF16),
-        pltpu.VMEM((count, high, cols), BF16),
+        pltpu.VMEM((count, high // 2, cols), BF16),
+        pltpu.VMEM((count, high // 2, cols), BF16),
         dma((8, count, 2)),
         dma((2, count, n)),
         dma((1,)),
     ]
 
 
-def finish_kernel(n, count, g_ref, h_ref, t_ref, x_ref, c_ref, gres, hres, t_out, x_out, c_out, *refs):
+def finish_kernel(
+    n, count, g_ref, h_ref, t_ref, x_ref, a_ref, w_ref, m_ref, gres, hres, t_out, x_out, c_out, wv, base, s_own, *refs
+):
     run = Stack(n, count, g_ref, h_ref, gres, hres, refs[:7])
     small = Total(n, t_ref, t_out, *refs[7:16])
-    move = Swap(n, [(x_ref, x_out), (c_ref, c_out)], *refs[16:])
+    load_m = pltpu.make_async_copy(m_ref, base, s_own.at[0])
+    load_m.start()
+    down = Scatter(n, False, a_ref, [pltpu.make_async_copy(w_ref, wv, s_own.at[1])], wv, refs[21:])
+    result = down.hop.at[n - 1]
+    move = Swap(n, [(x_ref, x_out), (result, c_out)], *refs[16:21])
+    down.begin()
     barrier = pltpu.get_barrier_semaphore()
 
     def knock(where):
@@ -1323,10 +1351,11 @@
     run.begin(knock)
     small.knock(knock)
     move.knock(knock)
-    pl.semaphore_wait(barrier, run.knocks() + small.knocks() + move.knocks())
+    down.knock(knock)
+    pl.semaphore_wait(barrier, run.knocks() + small.knocks() + move.knocks() + 3)
+    down.ready()
     small.begin()
     move.send(0)
-    move.send(1)
 
     def body(s, carry):
         run.step(s)
@@ -1335,11 +1364,24 @@
         def _():
             small.middle()
 
-        for i in range(2):
-
-            @pl.when(s == 4 + 2 * i)
-            def _():
-                move.pass_on(i)
+        @pl.when(s < 2 * n)
+        def _():
+            down.step(s)
+
+        @pl.when(s == 4)
+        def _():
+            move.pass_on(0)
+
+        @pl.when(s == 2 * n)
+        def _():
+            down.result()
+            load_m.wait()
+            result[...] = (base[...] + down.acc[...]).astype(BF16)
+            move.send(1)
+
+        @pl.when(s == 2 * n + 3)
+        def _():
+            move.pass_on(1)
 
         return carry
 
@@ -1348,13 +1390,16 @@
     move.finish(0)
     move.finish(1)
     run.end()
-
-
-def finish(n, cid, g, h, t, x, c):
+    down.end()
+
+
+def finish(n, cid, g, h, t, x, a, w, m):
     parts, _, rows, wide = g.shape
     high, width = h.shape
     count = width // 128
     sub = rows // count
+    toks, inner = a.shape
+    own, depth = m.shape
     return pl.pallas_call(
         functools.partial(finish_kernel, n, count),
         out_shape=(
@@ -1362,19 +1407,193 @@
             jax.ShapeDtypeStruct((2 * high, width), BF16),
             jax.ShapeDtypeStruct(t.shape[1:], F32),
             jax.ShapeDtypeStruct(x.shape, BF16),
-            jax.ShapeDtypeStruct(c.shape, BF16),
+            jax.ShapeDtypeStruct(m.shape, BF16),
         ),
-        in_specs=[pl.BlockSpec(memory_space=HBM)] * 5,
+        in_specs=[pl.BlockSpec(memory_space=HBM)] * 7,
         out_specs=[pl.BlockSpec(memory_space=HBM)] * 5,
-        scratch_shapes=stack_scratch(n, count, parts, sub, wide, high, width)
+        scratch_shapes=[
+            pltpu.VMEM((1,) + w.shape, BF16),
+            pltpu.VMEM((own, depth), F32),
+            pltpu.SemaphoreType.DMA((2,)),
+        ]
+        + stack_scratch(n, count, parts, sub, wide, high, width)
         + total_scratch(n, t.shape[1:])
-        + swap_scratch(n, 2, x.shape[0], x.shape[1]),
+        + swap_scratch(n, 2, x.shape[0], x.shape[1])
+        + scatter_scratch(n, 1, own, inner, depth),
+        compiler_params=pltpu.CompilerParams(
+            collective_id=cid, has_side_effects=True, vmem_limit_bytes=63 * 2**20
+        ),
+        cost_estimate=cost(200, 0),
+        name="finish",
+    )(g.reshape(parts, n, count, sub, wide), h, t, x, a.reshape(1, 2 * n, own, inner), w.reshape((1,) + w.shape), m)
+
+
+def attend_kernel(
+    n, tile, qs, ks, vs, cot_ref, att, lse, cot_all, acc, top, buf, s_ring, r_ring, s_part, r_part, s_in, s_out
+):
+    length = qs.shape[0]
+    pair, pairs = pl.program_id(0), pl.num_programs(0)
+
+    def use(step, where):
+        pltpu.make_async_copy(buf.at[where], cot_all.at[where], s_out.at[step]).start()
+
+    run = Gather(n, cot_ref, buf, s_in, s_ring, r_ring, s_part, r_part, use)
+
+    @pl.when(pair == 0)
+    def _():
+        run.begin()
+
+    rows = lax.broadcasted_iota(jnp.int32, (tile, tile), 0)
+    cols = lax.broadcasted_iota(jnp.int32, (tile, tile), 1)
+    masks = [head_mask((tile, PAIR), h) for h in range(2)]
+    steps = length // tile
+    half = steps * pairs // 2
+
+    def q_step(qi, carry):
+        at = pair * steps + qi
+        for when, first, count in ((half, 0, n), (half + half // 2, n, n // 2)):
+
+            @pl.when(at == when)
+            def _():
+                for r in range(count):
+                    run.step(first + r)
+
+        q_at = pl.ds(pl.multiple_of(qi * tile, tile), tile)
+        q = qs[q_at, :]
+        acc[...] = jnp.zeros_like(acc)
+        top[...] = jnp.full(top.shape, -1e30, F32)
+
+        def one(kj, diagonal):
+            k_at = pl.ds(pl.multiple_of(kj * tile, tile), tile)
+            k, v = ks[k_at, :], vs[k_at, :]
+            for h in range(2):
+                qm = jnp.where(masks[h], q * SCALE, 0).astype(BF16)
+                s = nt(qm, k)
+                if diagonal:
+                    s = jnp.where(cols <= rows, s, -jnp.inf)
+                old = top[h]
+                new = jnp.maximum(old, jnp.max(s, axis=1, keepdims=True))
+                p = jnp.exp(s - new[:, :1]).astype(BF16)
+                ve = jnp.where(masks[h], v, 1).astype(BF16)
+                acc[h] = acc[h] * jnp.exp(old - new) + nn(p, ve)
+                top[h] = new
+
+        def k_step(kj, c):
+            one(kj, False)
+            return c
+
+        lax.fori_loop(0, qi, k_step, 0)
+        one(qi, True)
+        a0, a1 = acc[0], acc[1]
+        total = jnp.where(masks[0], roll_pair(a0, HEAD_DIM), roll_pair(a1, HEAD_DIM))
+        att[q_at, :] = (jnp.where(masks[0], a0, a1) / total).astype(BF16)
+        lse[q_at, :] = jnp.where(masks[0], top[0], top[1]) + jnp.log(total)
+        return carry
+
+    lax.fori_loop(0, steps, q_step, 0)
+
+    @pl.when(pair == pairs - 1)
+    def _():
+        for r in range(n + n // 2, 2 * n):
+            run.step(r)
+        run.end()
+        for step in range(2 * n):
+            pltpu.make_async_copy(buf.at[0], cot_all.at[0], s_out.at[step]).wait()
+
+
+def attend(n, cid, qs, ks, vs, cot):
+    length, width = qs.shape
+    pairs = width // PAIR
+    tile = min(512, length)
+    rows, depth = cot.shape
+    dma = pltpu.SemaphoreType.DMA
+    hbm = pl.BlockSpec(memory_space=HBM)
+    own = pl.BlockSpec((length, PAIR), lambda p: (0, p))
+    return pl.pallas_call(
+        functools.partial(attend_kernel, n, tile),
+        grid=(pairs,),
+        out_shape=(
+            jax.ShapeDtypeStruct((length, width), BF16),
+            jax.ShapeDtypeStruct((length, width), F32),
+            jax.ShapeDtypeStruct((2 * n, rows, depth), BF16),
+        ),
+        in_specs=[own] * 3 + [hbm],
+        out_specs=[own] * 2 + [hbm],
+        scratch_shapes=[
+            pltpu.VMEM((2, tile, PAIR), F32),
+            pltpu.VMEM((2, tile, PAIR), F32),
+            pltpu.VMEM((2 * n, rows, depth), BF16),
+        ]
+        + ring_sems(n)
+        + [dma, dma((2 * n,))],
         compiler_params=pltpu.CompilerParams(
             collective_id=cid, has_side_effects=True, vmem_limit_bytes=60 * 2**20
         ),
-        cost_estimate=cost(200, 0),
-        name="finish",
-    )(g.reshape(parts, n, count, sub, wide), h, t, x, c)
+        cost_estimate=cost(42, 0),
+        name="attend",
+    )(qs, ks, vs, cot)
+
+
+def prepare_kernel(blk, slot_ref, proj, bias, cos_t, low_t, high_t, qs, ks, vs):
+    def sort_block(b, carry):
+        src = pl.ds(pl.multiple_of(slot_ref[b] * blk, blk), blk)
+        dst = pl.ds(pl.multiple_of(b * blk, blk), blk)
+        c, lo, hi = cos_t[dst, :], low_t[dst, :], high_t[dst, :]
+        q = proj[0, src, :] + bias[0]
+        k = proj[1, src, :] + bias[1]
+        q = q * c + roll_pair(q, -(ROT // 2)) * lo + roll_pair(q, ROT // 2) * hi
+        k = k * c + roll_pair(k, -(ROT // 2)) * lo + roll_pair(k, ROT // 2) * hi
+        qs[dst, :] = q.astype(BF16)
+        ks[dst, :] = k.astype(BF16)
+        vs[dst, :] = (proj[2, src, :] + bias[2]).astype(BF16)
+        return carry
+
+    lax.fori_loop(0, proj.shape[1] // blk, sort_block, 0)
+
+
+def prepare(slot_of, proj, bias, tables, blk):
+    _, length, width = proj.shape
+    table = pl.BlockSpec((length, PAIR), lambda p, s: (0, 0), pipeline_mode=pl.Buffered(1))
+    out = jax.ShapeDtypeStruct((length, width), BF16)
+    return pl.pallas_call(
+        functools.partial(prepare_kernel, blk),
+        out_shape=(out, out, out),
+        grid_spec=pltpu.PrefetchScalarGridSpec(
+            num_scalar_prefetch=1,
+            grid=(width // PAIR,),
+            in_specs=[
+                pl.BlockSpec((3, length, PAIR), lambda p, s: (0, 0, p)),
+                pl.BlockSpec((3, 1, PAIR), lambda p, s: (0, 0, p)),
+                table,
+                table,
+                table,
+            ],
+            out_specs=[pl.BlockSpec((length, PAIR), lambda p, s: (0, p))] * 3,
+        ),
+        compiler_params=pltpu.CompilerParams(vmem_limit_bytes=48 * 2**20),
+        cost_estimate=cost(6, 0),
+        name="prepare",
+    )(slot_of, proj, bias, *tables)
+
+
+def reorder_kernel(blk, from_ref, in_ref, out_ref):
+    def move(j, carry):
+        src = pl.ds(pl.multiple_of(from_ref[j] * blk, blk), blk)
+        out_ref[pl.ds(pl.multiple_of(j * blk, blk), blk), :] = in_ref[src, :]
+        return carry
+
+    lax.fori_loop(0, in_ref.shape[0] // blk, move, 0)
+
+
+def reorder(blocks, rows, blk):
+    whole = pl.BlockSpec(rows.shape, lambda i, s: (0, 0))
+    return pl.pallas_call(
+        functools.partial(reorder_kernel, blk),
+        out_shape=jax.ShapeDtypeStruct(rows.shape, rows.dtype),
+        grid_spec=pltpu.PrefetchScalarGridSpec(num_scalar_prefetch=1, grid=(1,), in_specs=[whole], out_specs=whole),
+        cost_estimate=cost(2, 0),
+        name="reorder",
+    )(blocks, rows)
 
 
 def local(
@@ -1403,29 +1622,9 @@
     units = w_down.shape[0] // 2
     pick = lambda a, axis, at: lax.dynamic_index_in_dim(a, at, axis, keepdims=False)
 
-    def rows_first(g):
-        return lax.psum_scatter(g.astype(BF16), "pl", scatter_dimension=0, tiled=True)
-
-    def last(part):
-        return lax.all_gather(part, ("core", "pl"), axis=0, tiled=True).astype(F32)
-
-    def columns_first(g):
-        parts, _, wide = g.shape
-        g = g.reshape(parts, n, n, rows // n, wide).transpose(2, 1, 0, 3, 4)
-        part = lax.psum_scatter(g, "pl", scatter_dimension=0, tiled=True)
-        return part.reshape(n, parts * rows // n, wide)
-
-    def columns_last(part, parts, wide):
-        whole = lax.all_gather(part, ("core", "pl"), axis=0, tiled=True)
-        whole = whole.reshape(2, n, n, -1, rows // n, part.shape[2])
-        if (2 * wide) % 128 == 0:
-            return assemble(n, whole, parts, wide)
-        whole = whole.reshape(2, n, n, whole.shape[3], rows // n, -1, wide).transpose(1, 4, 3, 5, 2, 0, 6)
-        return whole.reshape(rows, parts * n * 2 * wide).astype(F32)
-
     small = jnp.concatenate([first_gain, first_shift, second_gain, second_shift, qkv_bias]).reshape(-1, 128)
     ids = jnp.zeros((8, 128), jnp.int32).at[0, :slots].set(block_of.reshape(-1))
-    x, cot, wq, small, ids = start(n, 0, inputs.reshape(toks, width), cotangent.reshape(toks, width), w_qkv, small, ids)
+    x, wq, small, ids = start(n, 0, inputs.reshape(toks, width), w_qkv, small, ids)
     x, w_gateup, w_out, w_down = lax.optimization_barrier((x, w_gateup, w_out, w_down))
     token_rows = x.astype(F32)
     small = small.reshape(n, -1)
@@ -1433,56 +1632,65 @@
         small[:, k * rows : (k + 1) * rows].reshape(width) for k in range(4)
     )
     bias = small[:, 4 * rows :].reshape(3, n, 2, hw)
-    bias = pick(pick(bias, 1, me), 1, core).reshape(1, 3 * hw)
+    bias = pick(pick(bias, 1, me), 1, core).reshape(3, 1, hw)
     blocks = ids[:, 0, :slots].reshape(-1)
     order = jnp.arange(blocks.shape[0], dtype=jnp.int32)
     slot_of = jnp.sum(jnp.where(blocks[None, :] == order[:, None], order[None, :], 0), axis=1)
 
-    mine = split_columns(n, w_gateup)
-    wgu = jnp.zeros((2, n, rows, units), BF16)
-    wgu = lax.dynamic_update_index_in_dim(wgu, pick(mine, 0, me), me, 1)
-    for j in range(1, n):
-        got = lax.ppermute(pick(mine, 0, (me + j) % n), "dp", [(i, (i + j) % n) for i in range(n)])
-        wgu = lax.dynamic_update_index_in_dim(wgu, got, (me + n - j) % n, 1)
-    wgu = wgu.reshape(2, n * rows, units)
+    pieces = [split_columns(n, w_gateup, me)]
+    side = plane % 2
+    near = [
+        lax.ppermute(split_columns(n, w_gateup, (me + j) % n, side), "dp", [(i, (i + j) % n) for i in range(n)])
+        for j in range(1, n)
+    ]
     wo = pick(w_out.reshape(2, hw, width), 0, core)
     wd = pick(w_down.reshape(2, units, width), 0, core)
     tables = rotary_tables(blocks.shape[0] * blk)
 
     normed_out, normed_one, inverse_one = layer_norm(token_rows, gain_one, shift_one)
-    hidden_one, proj = gather_dot(n, 1, normed_out.astype(BF16), wq, False, F32)
-    proj, cot = lax.optimization_barrier((proj, cot))
-    cot_all = lax.all_gather(cot, PLANE, axis=0, tiled=True)
-    qs, ks, vs, att, lse = attend(slot_of, proj, bias, tables, blk)
-    middle = token_rows + dot_scatter(n, 2, [(att, wo)], False)
+    hidden_one, proj, cot = gather_dot(n, 1, normed_out.astype(BF16), wq, False, F32, cotangent.reshape(toks, width))
+    proj, *near = lax.optimization_barrier((proj, *near))
+    far = [lax.ppermute(a, "pl", [(i, i + 1 - 2 * (i % 2)) for i in range(n)]) for a in near]
+    qs, ks, vs = prepare(slot_of, proj, bias, tables, blk)
+    att, lse, cot_all = attend(n, 8, qs, ks, vs, cot)
+    att = reorder(blocks, att, blk)
+    cot_all = cot_all.reshape(-1, width)
+    att, *far = lax.optimization_barrier((att, *far))
+    for a, b in zip(near, far):
+        pieces += [a, b]
+    middle = token_rows + dot_scatter(n, 2, att[None], [wo[None]], False)
     normed_out_two, normed_two, inverse_two = layer_norm(middle, gain_two, shift_two)
-    hidden_two, act, grad_gate, grad_up = gather_mlp(n, 3, normed_out_two.astype(BF16), wgu, cot_all, wd)
-    grad_down = tn(act, cot_all).astype(BF16)
-    grad_gateup = jnp.stack([tn(hidden_two, grad_gate), tn(hidden_two, grad_up)]).astype(BF16)
-    grad_gate, grad_up, grad_down, grad_gateup = lax.optimization_barrier((grad_gate, grad_up, grad_down, grad_gateup))
-    down_part = rows_first(grad_down)
-    gateup_part = columns_first(grad_gateup)
-    grad_hidden_two = dot_scatter(n, 4, [(grad_gate, wgu[0]), (grad_up, wgu[1])], True)
+    hidden_two, act, grad_gu = gather_mlp(n, 3, normed_out_two.astype(BF16), pieces, cot_all, wd)
+    grad_gateup = weight_grad(n, n, hidden_two, grad_gu)
+    grad_gu, grad_gateup = lax.optimization_barrier((grad_gu, grad_gateup))
+    gateup_part = lax.psum_scatter(grad_gateup, "pl", scatter_dimension=0, tiled=True)
+    grad_hidden_two = dot_scatter(n, 4, grad_gu, pieces, True)
     gain_two_term = jnp.sum(grad_hidden_two * normed_two, axis=0)
     shift_two_term = jnp.sum(grad_hidden_two, axis=0)
     grad_middle = cot.astype(F32) + norm_back(grad_hidden_two, normed_two, inverse_two, gain_two)
-    grad_middle_all, grad_att = gather_dot(n, 5, grad_middle.astype(BF16), wo, True, BF16)
-    gq, gk, gv, bias_terms = attend_back(slot_of, qs, ks, vs, att, grad_att, lse, tables, blk)
-    grad_proj = jnp.concatenate([gq, gk, gv], axis=1)
-    grad_proj, gateup_part, down_part = lax.optimization_barrier((grad_proj, gateup_part, down_part))
-    gateup_part = lax.all_to_all(gateup_part, "dp", 0, 0, tiled=True)
-    grad_qkv = tn(hidden_one, grad_proj).astype(BF16)
-    grad_out = tn(att, grad_middle_all).astype(BF16)
-    grad_hidden_one = dot_scatter(n, 6, [(grad_proj, wq)], True)
+    grad_middle_all, grad_att = gather_dot(n, 5, grad_middle.astype(BF16), wo[None], True, BF16)
+    grad_att, gateup_part = lax.optimization_barrier((grad_att, gateup_part))
+    gateup_part = gateup_part.reshape(n, rows // n, 2 * units)
+    shares = [pick(gateup_part, 0, me)]
+    for j in range(1, n):
+        share = pick(gateup_part, 0, (me + j) % n)
+        shares.append(lax.ppermute(share, "dp", [(i, (i + j) % n) for i in range(n)]))
+    grad_att, *shares = lax.optimization_barrier((grad_att, *shares))
+    grad_proj, bias_terms = attend_back(slot_of, qs, ks, vs, att, grad_att[0], lse, tables, blk)
+    grad_hidden_one = dot_scatter(n, 6, grad_proj, [wq], True)
     gain_one_term = jnp.sum(grad_hidden_one * normed_one, axis=0)
     shift_one_term = jnp.sum(grad_hidden_one, axis=0)
     grad_inputs = grad_middle + norm_back(grad_hidden_one, normed_one, inverse_one, gain_one)
     grad_inputs = grad_inputs.astype(BF16)
-    grad_inputs, act = lax.optimization_barrier((grad_inputs, act))
-    outputs = (middle + dot_scatter(n, 8, [(act, wd)], False)).astype(BF16)
-
-    grad_down = last(down_part)
-    grad_gateup = columns_last(gateup_part, 2, units)
+    whole = lax.all_gather(jnp.stack(shares), ("pl", "core"), axis=0, tiled=True)
+    whole = whole.reshape(n, 2, n, rows // n, 2 * units)
+    if (2 * units) % 128 == 0:
+        grad_gateup = assemble(n, whole, 2, units, 1)
+    else:
+        whole = jnp.take(whole, (me + n - jnp.arange(n)) % n, axis=2).reshape(n, 2, n, rows // n, 2, units)
+        grad_gateup = whole.transpose(0, 3, 4, 2, 1, 5).reshape(rows, -1).astype(F32)
+    grad_qkv = weight_grad(n, 1, hidden_one, grad_proj)
+    grad_rows = jnp.concatenate([tn(att, grad_middle_all).astype(BF16), tn(act, cot_all).astype(BF16)], axis=0)
     bias_term = bias_terms[:3].reshape(3, 1, hw)
     at = me * 2 + core
     spots = (jnp.arange(2 * n, dtype=jnp.int32) == at)[None, :, None]
@@ -1491,11 +1699,13 @@
         [a.reshape(n, rows) for a in (gain_one_term, shift_one_term, gain_two_term, shift_two_term)] + [bias_term],
         axis=1,
     )
-    grad_qkv, grad_out, tiny, outputs, grad_inputs = finish(
-        n, 7, grad_qkv.reshape(1, n, rows, 3 * hw), grad_out, tiny.reshape(n, -1, 128), outputs, grad_inputs
+    grad_qkv, grad_rows, tiny, grad_inputs, outputs = finish(
+        n, 7, grad_qkv, grad_rows, tiny.reshape(n, -1, 128), grad_inputs, act, wd, middle
     )
-    grad_qkv = assemble(n, grad_qkv, 3, hw)
-    grad_out = grad_out.astype(F32)
+    grad_qkv = assemble(n, grad_qkv, 3, hw, 0)
+    grad_rows = grad_rows.reshape(2, -1, width)
+    grad_out = grad_rows[:, :hw].astype(F32).reshape(-1, width)
+    grad_down = grad_rows[:, hw:].astype(F32).reshape(-1, width)
     grad_inputs = grad_inputs.astype(F32)
     tiny = tiny.reshape(-1)
     terms = [tiny[k * rows : (k + 1) * rows] for k in range(4)]

time: 1080 us -> 984 us (0.911)
  local copies, waits for them, and re-layouts: 93 us -> 29.2 us
  matrix products: 41.6 us -> 15.3 us
  waiting for transfers between devices: 0.78 us -> 25.3 us
  blocking collectives: 22.3 us -> 0 us
  other arithmetic: 51.5 us -> 39 us
  Pallas kernels: 845 us -> 834 us
  starting transfers between devices: 5.04 us -> 16 us
    pallas_call x6 -> x13, Pallas kernels: 157 us -> 243 us  [the longest x2 120 us: gather_dot(): pl.pallas_call(functools.partial(gather_dot_kernel, n, trans, len(extra))...]
    pallas_call x4 -> x3, Pallas kernels: 208 us -> 144 us  [dot_scatter(): pl.pallas_call(functools.partial(dot_scatter_kernel, n, count, trans), ou...]
    pallas_call x1, Pallas kernels: 121 us -> 70.5 us  [start(): pl.pallas_call(functools.partial(start_kernel, n), out_shape=(jax.ShapeDt...]
    dot_general x5 -> x2, matrix products: 41.6 us -> 15.3 us  [tn(): lax.dot_general(a, b, (((0,), (0,)), ((), ())), preferred_element_type=F32)]
    all_to_all x1 -> x0, blocking collectives: 22.3 us -> none  [local(): gateup_part = lax.all_to_all(gateup_part, 'dp', 0, 0, tiled=True)]
    reshape x3 -> x0, local copies, waits for them, and re-layouts: 20.6 us -> none  [the longest x2 17 us: columns_first(): g = g.reshape(parts, n, n, rows // n, wide).transpose(2, 1, 0, 3, 4)]
    pallas_call x1, Pallas kernels: 259 us -> 276 us  [finish(): pl.pallas_call(functools.partial(finish_kernel, n, count), out_shape=(jax...]
    all_gather x1 -> x0, local copies, waits for them, and re-layouts: 16 us -> none  [columns_last(): whole = lax.all_gather(part, ('core', 'pl'), axis=0, tiled=True)]
  transfers between devices with their start and end apart: 8 -> 11, of which waited for: 0 -> 4; matrix products, arithmetic and copies ran while one was open for 11% -> 7% of each run, Pallas kernels for 58% -> 65%
where the time goes in v4:
time: 984 us; the launch traced here: 974 us
  Pallas kernels  834 us (85%)
  other arithmetic  39 us (4%)
  local copies, waits for them, and re-layouts  29.2 us (3%)
  waiting for transfers between devices  25.3 us (3%)
  starting transfers between devices  16 us (2%)
  matrix products  15.3 us (2%)
  between operations  14.9 us (2%)
    pallas_call x1, Pallas kernels, finish(): pl.pallas_call(functools.partial(finish_kernel, n, count), out_shape=(jax...  276 us
    pallas_call x3, Pallas kernels, dot_scatter(): pl.pallas_call(functools.partial(dot_scatter_kernel, n, count, trans), ou...  144 us
    pallas_call x2, Pallas kernels, gather_dot(): pl.pallas_call(functools.partial(gather_dot_kernel, n, trans, len(extra))...  120 us
    pallas_call x1, Pallas kernels, start(): pl.pallas_call(functools.partial(start_kernel, n), out_shape=(jax.ShapeDt...  70.5 us
    pallas_call x1, Pallas kernels, gather_mlp(): pl.pallas_call(functools.partial(gather_mlp_kernel, n), out_shape=(jax.Sh...  51.5 us
    pallas_call x1, Pallas kernels, attend_back(): pl.pallas_call(functools.partial(attend_back_kernel, blk, tile), out_shap...  50.1 us
    pallas_call x1, Pallas kernels, attend(): pl.pallas_call(functools.partial(attend_kernel, n, tile), grid=(pairs,),...  44.3 us
    pallas_call x2, Pallas kernels, weight_grad(): pl.pallas_call(functools.partial(weight_grad_kernel, planes), grid=(n,),...  29.9 us
  transfers between devices with their start and end apart: 11, of which 4 were waited for; matrix products, arithmetic and copies ran while one was open for 7% of the time, Pallas kernels for 65%

profile of v4, /device:TPU:0, one launch (start us, length us, event | category | flops | bytes accessed | tf_op | source)
XLA Modules:
  0.0 974.1 jit_solution(5005176320968900679)
XLA Ops:
  12.6 70.5 %start.1 = (bf16[256,2048]{1,0:T(8,128)(2,1)}, bf16[3,2048,256]{2,1,0:T(8,128)(2,1)}, f32[4,28,128]{2,1,0:T(8,128)}, s32[8,8,128]{2,1,0:T(8,128)}) custom-call(bf16[256,2048]{1,0:T(8,128)(2,1)} %bitcast.92, bf16[512,6144]{1,0:T(8,128)(2,1)} %w_ref.1, f32[28,128]{1,0:T(8,128)} %bitcast.111, s32[8,128]{1,0:T(8,128)} %scatter.4.block_ref), custom_call_target="tpu_custom_call" | custom-call | bytes 323000000 | tf_op jit(solution)/shard_map/start/pallas_call | solution.py:930
  83.7 3.0 split_columns.4
  87.3 3.0 split_columns.5
  90.9 3.2 split_columns.6
  94.0 2.9 collective-permute-start.2
  98.6 3.8 fusion.27.d_ref
  102.4 1.4 fusion.7.refs_0_
  104.5 3.8 split_columns.7.refs_0_.refs_1_
  108.5 79.7 %gather_dot.2 = (bf16[8,256,2048]{2,1,0:T(8,128)(2,1)}, f32[3,8,256,256]{3,2,1,0:T(8,128)}, bf16[256,2048]{1,0:T(8,128)(2,1)}) custom-call(bf16[256,2048]{1,0:T(8,128)(2,1)} %fusion.7.refs_0_, bf16[3,2048,256]{2,1,0:T(8,128)(2,1)} %get-tuple-element.72.refs_1_, bf16[256,2048]{1,0:T(8,128)(2,1)} %bitcast.113), custom_call_target="tpu_custom_call" | custom-call | flops 6442450944 | bytes 142800000 | tf_op jit(solution)/shard_map/gather_dot/pallas_call | solution.py:529
  188.2 6.6 collective-permute-start.3
  194.9 1.9 collective-permute-start.5
  196.8 2.3 constant_dynamic-slice_fusion.1.refs_1_
  199.1 4.8 fusion.16
  203.9 8.0 prepare.1
  214.9 44.3 %attend.1 = (bf16[2048,256]{1,0:T(8,128)(2,1)}, f32[2048,256]{1,0:T(8,128)}, bf16[8,256,2048]{2,1,0:T(8,128)(2,1)}) custom-call(bf16[2048,256]{1,0:T(8,128)(2,1)} %copy-done.2, bf16[2048,256]{1,0:T(8,128)(2,1)} %copy-done.3, bf16[2048,256]{1,0:T(8,128)(2,1)} %copy-done.4, bf16[256,2048]{1,0:T(8,128)(2,1)} %get-tuple-element.81.cot_ref), custom_call_target="tpu_custom_call" | custom-call | bytes 142800000 | tf_op jit(solution)/shard_map/attend/pallas_call | solution.py:1512
  259.3 3.0 reorder.1.att
  262.3 47.0 %dot_scatter.3 = f32[256,2048]{1,0:T(8,128)} custom-call(bf16[1,8,256,256]{3,2,1,0:T(8,128)(2,1)} %bitcast.82, bf16[1,256,2048]{2,1,0:T(8,128)(2,1)} %constant_dynamic-slice_fusion.1.refs_1_), custom_call_target="tpu_custom_call" | custom-call | flops 2147483648 | bytes 153000000 | tf_op jit(solution)/shard_map/dot_scatter/pallas_call | solution.py:813
  309.3 1.9 fusion.22
  311.5 1.4 add_convert_fusion.x_ref
  313.0 51.5 %gather_mlp.1 = (bf16[8,256,2048]{2,1,0:T(8,128)(2,1)}, bf16[8,256,704]{2,1,0:T(8,128)(2,1)}, bf16[8,256,1408]{2,1,0:T(8,128)(2,1)}) custom-call(bf16[256,2048]{1,0:T(8,128)(2,1)} %add_convert_fusion.x_ref, bf16[8,256,2048]{2,1,0:T(8,128)(2,1)} %get-tuple-element.88.c_ref, bf16[704,2048]{1,0:T(8,128)(2,1)} %fusion.27.d_ref, ...), custom_call_target="tpu_custom_call" | custom-call | flops 17716740096 | bytes 163200000 | tf_op jit(solution)/shard_map/gather_mlp/pallas_call | solution.py:628
  364.5 18.7 %weight_grad.2 = bf16[4,4,128,1408]{3,2,1,0:T(8,128)(2,1)} custom-call(bf16[2048,2048]{1,0:T(8,128)(2,1)} %bitcast.115, bf16[1,2048,1408]{2,1,0:T(8,128)(2,1)} %bitcast.116), custom_call_target="tpu_custom_call" | custom-call | flops 11811160064 | bytes 54400000 | tf_op jit(solution)/shard_map/weight_grad/pallas_call | solution.py:1122
  383.3 49.7 %dot_scatter.4 = f32[256,2048]{1,0:T(8,128)} custom-call(bf16[1,8,256,1408]{3,2,1,0:T(8,128)(2,1)} %bitcast.117, bf16[1,512,1408]{2,1,0:T(8,128)(2,1)} %split_columns.7.refs_0_.refs_1_, bf16[1,256,1408]{2,1,0:T(8,128)(2,1)} %copy-done.21, bf16[1,256,1408]{2,1,0:T(8,128)(2,1)} %collective-permute-done.3.refs_2_.refs_3_, ...), custom_call_target="tpu_custom_call" | custom-call | flops 11811160064 | bytes 153000000 | tf_op jit(solution)/shard_map/dot_scatter/pallas_call | solution.py:813
  433.0 3.4 multiply_reduce_fusion
  436.6 3.8 fusion.21
  440.4 39.9 %gather_dot.3 = (bf16[8,256,2048]{2,1,0:T(8,128)(2,1)}, bf16[1,8,256,256]{3,2,1,0:T(8,128)(2,1)}) custom-call(bf16[256,2048]{1,0:T(8,128)(2,1)} %get-tuple-element.123.refs_0_, bf16[1,256,2048]{2,1,0:T(8,128)(2,1)} %constant_dynamic-slice_fusion.1.refs_1_), custom_call_target="tpu_custom_call" | custom-call | flops 2147483648 | bytes 142800000 | tf_op jit(solution)/shard_map/gather_dot/pallas_call | solution.py:529
  480.3 10.8 %reduce-scatter.2.cloned.1.call-done = bf16[1,4,128,1408]{3,2,1,0:T(8,128)(2,1)} async-done(((bf16[4,4,128,1408]{3,2,1,0:T(8,128)(2,1)}), bf16[1,4,128,1408]{3,2,1,0:T(8,128)(2,1)}) %reduce-scatter.2.cloned.1.call-update) | async-done | bytes 1441808 | tf_op jit(solution)/shard_map/reduce_scatter | solution.py:1666
  492.5 1.5 collective-permute-start.6
  494.1 1.5 collective-permute-start.7
  495.5 1.5 collective-permute-start.8
  497.0 7.8 collective-permute-done.6
  504.8 6.5 collective-permute-done.7
  512.7 3.9 constant_dynamic-slice_fusion.w_ref
  516.6 6.3 convolution_convert_fusion
  522.9 9.1 bitcast_convert_fusion.1
  532.0 2.4 pad_maximum_fusion.h_ref
  534.4 50.1 %attend_back.1 = (bf16[3,2048,256]{2,1,0:T(8,128)(2,1)}, f32[8,256]{1,0:T(8,128)}) custom-call(s32[16]{0:T(128)} %copy-done.5, bf16[2048,256]{1,0:T(8,128)(2,1)} %copy-done.2, bf16[2048,256]{1,0:T(8,128)(2,1)} %copy-done.3, bf16[2048,256]{1,0:T(8,128)(2,1)} %copy-done.4, bf16[2048,256]{1,0:T(8,128)(2,1)} %reorder.1.att, bf16[2048,256]{1,0:T(8,128)(2,1)} %bitcast.95, ...), custom_call_target="tpu_custom_call" | custom-call | bytes 170000000 | tf_op jit(solution)/shard_map/attend_back/pallas_call | solution.py:161
  584.5 47.5 %dot_scatter.5 = f32[256,2048]{1,0:T(8,128)} custom-call(bf16[3,8,256,256]{3,2,1,0:T(8,128)(2,1)} %bitcast.112, bf16[3,2048,256]{2,1,0:T(8,128)(2,1)} %get-tuple-element.72.refs_1_), custom_call_target="tpu_custom_call" | custom-call | flops 6442450944 | bytes 153000000 | tf_op jit(solution)/shard_map/dot_scatter/pallas_call | solution.py:813
  631.9 2.6 fusion.9
  635.4 11.2 %weight_grad.3 = bf16[3,4,512,256]{3,2,1,0:T(8,128)(2,1)} custom-call(bf16[2048,2048]{1,0:T(8,128)(2,1)} %bitcast.114, bf16[3,2048,256]{2,1,0:T(8,128)(2,1)} %get-tuple-element.102.g_ref), custom_call_target="tpu_custom_call" | custom-call | flops 6442450944 | bytes 54400000 | tf_op jit(solution)/shard_map/weight_grad/pallas_call | solution.py:1122
  646.6 1.8 fusion.13.x_ref
  648.4 275.7 %finish.1 = (bf16[2,16,4,3,32,256]{5,4,3,2,1,0:T(8,128)(2,1)}, bf16[1920,2048]{1,0:T(8,128)(2,1)}, f32[28,128]{1,0:T(8,128)}, bf16[256,2048]{1,0:T(8,128)(2,1)}, bf16[256,2048]{1,0:T(8,128)(2,1)}) custom-call(bf16[3,4,16,32,256]{4,3,2,1,0:T(8,128)(2,1)} %bitcast.90, bf16[960,2048]{1,0:T(8,128)(2,1)} %pad_maximum_fusion.h_ref, f32[4,28,128]{2,1,0:T(8,128)} %reshape.261.t_ref, ...), custom_call_target="tpu_custom_call" | custom-call | bytes 680000000 | tf_op jit(solution)/shard_map/finish/pallas_call | solution.py:1403
  924.1 1.8 slice.97
  926.0 3.7 slice.98
  929.7 1.6 convert.3
  931.2 12.1 %assemble.2 = f32[512,6144]{1,0:T(8,128)} custom-call(bf16[2,16,4,3,32,256]{5,4,3,2,1,0:T(8,128)(2,1)} %get-tuple-element.109.in_ref), custom_call_target="tpu_custom_call" | custom-call | bytes 40800000 | tf_op jit(solution)/shard_map/assemble/pallas_call | solution.py:1049
  944.5 2.7 bitcast_convert_fusion.2
  947.2 6.4 bitcast_convert_fusion
  953.6 12.5 %assemble.3 = f32[512,11264]{1,0:T(8,128)} custom-call(bf16[4,2,4,128,1408]{4,3,2,1,0:T(8,128)(2,1)} %bitcast.83), custom_call_target="tpu_custom_call" | custom-call | bytes 40800000 | tf_op jit(solution)/shard_map/assemble/pallas_call | solution.py:1049
  (115 shorter events, 18.9 us)
Async XLA Ops:
  7.2 483.9 %reduce-scatter.2.cloned.1.call-start = ((), (), s32[]{:S(2)}) async-start(), calls=%async_computation.1 | async-start | bytes 7208960 | tf_op jit(solution)/shard_map/reduce_scatter | solution.py:1666
  11.9 0.6 copy-start.17
  86.7 101.5 %collective-permute-start = (bf16[1,256,1408]{2,1,0:T(8,128)(2,1)}, bf16[1,256,1408]{2,1,0:T(8,128)(2,1)S(1)}, u32[]{:S(2)}, u32[]{:S(2)}) collective-permute-start(bf16[1,256,1408]{2,1,0:T(8,128)(2,1)} %split_columns.4), channel_id=1, source_target_pairs={{0,8},{8,16},{16,24},{24,0},{1,9},{9,17},{17,25},{25,1},{2,10},{10... | collective-permute-start | bytes 2162696 | tf_op jit(solution)/shard_map/ppermute | solution.py:1643
  90.3 97.9 %collective-permute-start.1 = (bf16[1,256,1408]{2,1,0:T(8,128)(2,1)}, bf16[1,256,1408]{2,1,0:T(8,128)(2,1)}, u32[]{:S(2)}, u32[]{:S(2)}) collective-permute-start(bf16[1,256,1408]{2,1,0:T(8,128)(2,1)} %split_columns.5), channel_id=1, source_target_pairs={{0,16},{8,24},{16,0},{24,8},{1,17},{9,25},{17,1},{25,9},{2,18},{10... | collective-permute-start | bytes 2162696 | tf_op jit(solution)/shard_map/ppermute | solution.py:1643
  90.9 6.1 copy-start.16
  90.9 6.2 copy-start.8
  94.0 94.2 %collective-permute-start.2 = (bf16[1,256,1408]{2,1,0:T(8,128)(2,1)}, bf16[1,256,1408]{2,1,0:T(8,128)(2,1)}, u32[]{:S(2)}, u32[]{:S(2)}) collective-permute-start(bf16[1,256,1408]{2,1,0:T(8,128)(2,1)} %split_columns.6), channel_id=1, source_target_pairs={{0,24},{8,0},{16,8},{24,16},{1,25},{9,1},{17,9},{25,17},{2,26},{10... | collective-permute-start | bytes 2162696 | tf_op jit(solution)/shard_map/ppermute | solution.py:1643
  104.5 3.9 copy-start.19
  108.5 95.5 %copy-start.5 = (s32[16]{0:T(128)}, s32[16]{0:T(128)S(1)}, u32[]{:S(2)}) copy-start(s32[16]{0:T(128)S(1)} %select_reduce_fusion.slot_ref) | copy-start | bytes 196
  188.2 15.7 %copy-start.21 = (bf16[1,256,1408]{2,1,0:T(8,128)(2,1)}, bf16[1,256,1408]{2,1,0:T(8,128)(2,1)S(1)}, u32[]{:S(2)}) copy-start(bf16[1,256,1408]{2,1,0:T(8,128)(2,1)S(1)} %collective-permute-done.refs_1_.refs_2_) | copy-start | bytes 2162692
  188.2 74.1 %collective-permute-start.3 = (bf16[1,256,1408]{2,1,0:T(8,128)(2,1)S(1)}, bf16[1,256,1408]{2,1,0:T(8,128)(2,1)}, u32[]{:S(2)}, u32[]{:S(2)}) collective-permute-start(bf16[1,256,1408]{2,1,0:T(8,128)(2,1)S(1)} %collective-permute-done.refs_1_.refs_2_), channel_id=1, source_target_pairs={{0,2},{2,0},{4,6},{6,4},{1,3},{3,1},{5,7},{7,5},{8,10},{10,8},{12,... | collective-permute-start | bytes 2162696 | tf_op jit(solution)/shard_map/ppermute | solution.py:1653
  194.8 67.5 %collective-permute-start.4 = (bf16[1,256,1408]{2,1,0:T(8,128)(2,1)}, bf16[1,256,1408]{2,1,0:T(8,128)(2,1)}, u32[]{:S(2)}, u32[]{:S(2)}) collective-permute-start(bf16[1,256,1408]{2,1,0:T(8,128)(2,1)} %collective-permute-done.1.refs_3_.refs_4_), channel_id=1, source_target_pairs={{0,2},{2,0},{4,6},{6,4},{1,3},{3,1},{5,7},{7,5},{8,10},{10,8},{12,... | collective-permute-start | bytes 2162696 | tf_op jit(solution)/shard_map/ppermute | solution.py:1653
  194.9 67.4 %collective-permute-start.5 = (bf16[1,256,1408]{2,1,0:T(8,128)(2,1)}, bf16[1,256,1408]{2,1,0:T(8,128)(2,1)}, u32[]{:S(2)}, u32[]{:S(2)}) collective-permute-start(bf16[1,256,1408]{2,1,0:T(8,128)(2,1)} %collective-permute-done.2.refs_5_.refs_6_), channel_id=1, source_target_pairs={{0,2},{2,0},{4,6},{6,4},{1,3},{3,1},{5,7},{7,5},{8,10},{10,8},{12,... | collective-permute-start | bytes 2162696 | tf_op jit(solution)/shard_map/ppermute | solution.py:1653
  203.9 8.0 copy-start
  203.9 8.1 copy-start.1
  212.0 1.0 copy-start.2
  213.0 1.0 copy-start.3
  213.9 1.0 copy-start.4
  311.1 1.8 copy-start.6
  383.2 570.3 %all-gather.2.cloned.1.call-start = ((), (), s32[]{:S(2)}) async-start(), calls=%async_computation.2 | async-start | bytes 12976128 | tf_op jit(solution)/shard_map/all_gather | solution.py:1685
  433.0 3.5 copy-start.7
  433.0 3.6 copy-start.10
  492.5 12.3 %collective-permute-start.6 = (bf16[128,1408]{1,0:T(8,128)(2,1)S(1)}, bf16[128,1408]{1,0:T(8,128)(2,1)S(1)}, u32[]{:S(2)}, u32[]{:S(2)}) collective-permute-start(bf16[128,1408]{1,0:T(8,128)(2,1)S(1)} %get-tuple-element.129), channel_id=1, source_target_pairs={{0,8},{8,16},{16,24},{24,0},{1,9},{9,17},{17,25},{25,1},{2,10},{10... | collective-permute-start | bytes 1081352 | tf_op jit(solution)/shard_map/ppermute | solution.py:1677
  494.1 17.2 %collective-permute-start.7 = (bf16[128,1408]{1,0:T(8,128)(2,1)S(1)}, bf16[128,1408]{1,0:T(8,128)(2,1)S(1)}, u32[]{:S(2)}, u32[]{:S(2)}) collective-permute-start(bf16[128,1408]{1,0:T(8,128)(2,1)S(1)} %get-tuple-element.128), channel_id=1, source_target_pairs={{0,16},{8,24},{16,0},{24,8},{1,17},{9,25},{17,1},{25,9},{2,18},{10... | collective-permute-start | bytes 1081352 | tf_op jit(solution)/shard_map/ppermute | solution.py:1677
  495.5 15.8 %collective-permute-start.8 = (bf16[128,1408]{1,0:T(8,128)(2,1)S(1)}, bf16[128,1408]{1,0:T(8,128)(2,1)S(1)}, u32[]{:S(2)}, u32[]{:S(2)}) collective-permute-start(bf16[128,1408]{1,0:T(8,128)(2,1)S(1)} %get-tuple-element.127), channel_id=1, source_target_pairs={{0,24},{8,0},{16,8},{24,16},{1,25},{9,1},{17,9},{25,17},{2,26},{10... | collective-permute-start | bytes 1081352 | tf_op jit(solution)/shard_map/ppermute | solution.py:1677
  512.7 3.9 copy-start.9
  516.6 6.3 copy-start.13
  631.9 2.6 copy-start.20
  635.4 11.2 %copy-start.11 = (f32[256,2048]{1,0:T(8,128)S(1)}, f32[256,2048]{1,0:T(8,128)}, u32[]{:S(2)}) copy-start(f32[256,2048]{1,0:T(8,128)} %get-tuple-element.124) | copy-start | bytes 6291460
  635.4 11.2 %copy-start.12 = (f32[256,2048]{1,0:T(8,128)S(1)}, f32[256,2048]{1,0:T(8,128)}, u32[]{:S(2)}) copy-start(f32[256,2048]{1,0:T(8,128)} %dot_scatter.5) | copy-start | bytes 6291460
  925.9 3.7 copy-start.14
  931.2 12.1 %copy-start.18 = (f32[28,128]{1,0:T(8,128)S(1)}, f32[28,128]{1,0:T(8,128)}, u32[]{:S(2)}) copy-start(f32[28,128]{1,0:T(8,128)} %get-tuple-element.108) | copy-start | bytes 43012
  953.6 12.5 %copy-start.15 = (bf16[256,2048]{1,0:T(8,128)(2,1)S(1)}, bf16[256,2048]{1,0:T(8,128)(2,1)}, u32[]{:S(2)}) copy-start(bf16[256,2048]{1,0:T(8,128)(2,1)} %get-tuple-element.106) | copy-start | bytes 3145732
Sparse Core Ops, SparseCore 0:
  383.4 107.7 reduce-scatter.1
  512.8 107.8 all-gather.1
